TPU v7x, 32 devices: a whole 2x2x4 slice. The times are simulated.
32 devices in a mesh: dp: 2 (over x), row: 4 (over z), col: 4 (over y, core).
Axes of the slice: x: 2, y: 2, z: 4, core: 2. Of those that a mesh axis runs over, the one named last changes fastest.
Arguments:
- inputs: bfloat16 [768, 8192], P('row', ('dp', 'col')), may hold values from -6 to 6
- w_query: bfloat16 [4, 4, 36864], P('row', 'col'), may hold values from -0.21875 to 0.21875
- w_key: bfloat16 [4, 4, 36864], P('row', 'col'), may hold values from -0.21875 to 0.21875
- w_value: bfloat16 [4, 4, 36864], P('row', 'col'), may hold values from -0.21875 to 0.21875
- w_out: bfloat16 [4, 4, 36864], P('col', 'row'), may hold values from -0.875 to 0.875
- w_up: bfloat16 [768, 3072], P('row', 'col'), may hold values from -0.21875 to 0.21875
- w_down: bfloat16 [768, 3072], P('row', 'col'), may hold values from -0.109375 to 0.109375
- ln1_gain: float32 [768], P('row'), may hold values from 0.5 to 1.5
- ln1_bias: float32 [768], P('row'), may hold values from -1.75 to 1.75
- ln2_gain: float32 [768], P('row'), may hold values from 0.5 to 1.5
- ln2_bias: float32 [768], P('row'), may hold values from -1.75 to 1.75
- segment_ids: int32 [8192], P('dp'), may hold values from 0 to 20, as said below
- pad_mask: int32 [8192], P('dp'), may hold values from 0 to 1, as said below
- rand_blocks: int32 [2, 12, 64, 3], P('dp', 'col'), may hold values from 1 to 62, as said below
- grad_out: bfloat16 [768, 8192], P('row', ('dp', 'col')), may hold values from -6 to 6
Outputs:
- output: bfloat16 [768, 8192], P('row', ('dp', 'col'))
- grad_inputs: float32 [768, 8192], P('row', ('dp', 'col'))
- grad_w_query: float32 [4, 4, 36864], P('row', 'col')
- grad_w_key: float32 [4, 4, 36864], P('row', 'col')
- grad_w_value: float32 [4, 4, 36864], P('row', 'col')
- grad_w_out: float32 [4, 4, 36864], P('col', 'row')
- grad_w_up: float32 [768, 3072], P('row', 'col')
- grad_w_down: float32 [768, 3072], P('row', 'col')
- grad_ln1_gain: float32 [768], P('row')
- grad_ln1_bias: float32 [768], P('row')
- grad_ln2_gain: float32 [768], P('row')
- grad_ln2_bias: float32 [768], P('row')
Inputs may be any that keep to these rules, and one draw needn't show every extreme that they name: `segment_ids`: within each sequence of 4096 tokens the ids never fall, the last token's id is 4096 // 204, and every run of one id except the one that the sequence's end cuts spans 204 to 2048 tokens. `pad_mask`: in each sequence the last 1 to 204 tokens are 0 and all others 1. `rand_blocks`: for each sequence, head and query block i: three different block numbers, none of them 0, 63, i - 1, i or i + 1.
All inputs are finite; a program needn't handle non-finite values.
Results may differ from a plain program's by a relative error of at most 0.015.
Values may be sent and summed in bfloat16 or wider, within the bound.
A program may use at most 192 MiB of HBM per device.

v0:
```python
import jax
import jax.numpy as jnp
from jax import lax
from jax.sharding import PartitionSpec as P

D = 768
BLOCK = 64
LEN = 4096
NB = 64


NEG = -1000000000.0
EPS = 1e-06


def gelu_tanh(value):
    return jax.nn.gelu(value, approximate=True)


def contract_rows(left, right):
    return lax.dot_general(
        left, right, (((0,), (0,)), ((), ())), preferred_element_type=jnp.float32
    )


def project(block_rows, weight, flipped):
    if flipped:
        return lax.dot_general(
            block_rows, weight, (((1,), (1,)), ((), ())), preferred_element_type=jnp.float32
        )
    return jnp.dot(block_rows, weight, preferred_element_type=jnp.float32)


def across_col_row(values, weight, flipped):
    gathered = lax.all_gather(values, "col", axis=0, tiled=True)
    own_rows = gathered.shape[0] // lax.axis_size("row")

    def partial_term(offset, amount):
        return project(gathered, weight, flipped)

    return (
        gathered,
        lax.psum_scatter(
            partial_term(jnp.int32(0), own_rows * lax.axis_size("row")),
            "row",
            scatter_dimension=0,
            tiled=True,
        ),
    )


def across_row_col(values, weight, flipped):
    gathered = lax.all_gather(values, "row", axis=0, tiled=True)
    own_rows = gathered.shape[0] // lax.axis_size("col")

    def partial_term(offset, amount):
        return project(gathered, weight, flipped)

    return (
        gathered,
        lax.psum_scatter(
            partial_term(jnp.int32(0), own_rows * lax.axis_size("col")),
            "col",
            scatter_dimension=0,
            tiled=True,
        ),
    )


def row_totals(first_sum, second_sum):
    return lax.psum((first_sum, second_sum), "row")


def norm_forward(resid, gain, bias):
    totals = row_totals(jnp.sum(resid, axis=1), jnp.sum(resid * resid, axis=1))
    mean_row = totals[0] / D
    var_row = totals[1] / D - mean_row * mean_row
    rstd = lax.rsqrt(var_row + EPS)
    normed = (resid - mean_row[:, None]) * rstd[:, None]
    return (normed * gain + bias, normed, rstd)


def norm_backward(grad_rows, normed, rstd, gain):
    scaled = grad_rows * gain
    totals = row_totals(jnp.sum(scaled, axis=1), jnp.sum(scaled * normed, axis=1))
    return rstd[:, None] * (scaled - totals[0][:, None] / D - normed * (totals[1][:, None] / D))


def candidates(query_blocks):
    places = []
    places.append(0)
    places.append(min(NB, query_blocks) - 1)
    return places


def arrange(q_own, k_all, v_all, segs, pads, rand_local):
    row_index = lax.axis_index("row")
    head_count = rand_local.shape[1]
    head_width = q_own.shape[1] // head_count
    query_blocks = q_own.shape[0] // BLOCK
    total_blocks = k_all.shape[0] // BLOCK
    seqs_here = k_all.shape[0] // LEN
    block_span = jnp.arange(BLOCK, dtype=jnp.int32)
    own_blocks = row_index * query_blocks + jnp.arange(query_blocks, dtype=jnp.int32)
    seq_of = own_blocks // NB
    block_pos = own_blocks % NB
    is_global = (block_pos == 0) | (block_pos == NB - 1)
    rand_flat = rand_local.transpose(1, 0, 2, 3).reshape(head_count, seqs_here * NB, 3)
    chosen = jnp.take(rand_flat, own_blocks, axis=1)
    fixed_ids = jnp.stack(
        [
            jnp.zeros_like(block_pos),
            jnp.full_like(block_pos, NB - 1),
            block_pos - 1,
            block_pos,
            block_pos + 1,
        ],
        axis=1,
    )
    fixed_ids = jnp.clip(fixed_ids, 0, NB - 1)
    in_seq = jnp.concatenate(
        [jnp.broadcast_to(fixed_ids[None], (head_count, query_blocks, 5)), chosen], axis=2
    )
    key_table = in_seq + (seq_of * NB)[None, :, None]
    always = jnp.ones_like(is_global)
    entry_ok = jnp.stack(
        [always, always, block_pos >= 2, always, block_pos <= NB - 3, always, always, always],
        axis=1,
    )
    entry_tok = jnp.repeat(entry_ok, BLOCK, axis=1)
    key_tok = (key_table[..., None] * BLOCK + block_span).reshape(
        head_count, query_blocks, 8 * BLOCK
    )
    query_tok = own_blocks[:, None] * BLOCK + block_span[None, :]
    same_doc = (segs[query_tok][None, :, :, None] == segs[key_tok][:, :, None, :]) & (
        pads[key_tok][:, :, None, :] == 1
    )
    allowed_sparse = entry_tok[None, :, None, :] & (
        same_doc | (query_tok[None, :, :, None] == key_tok[:, :, None, :])
    )
    query_tiles = q_own.reshape(query_blocks, BLOCK, head_count, head_width).transpose(2, 0, 1, 3)
    key_heads = k_all.reshape(total_blocks, BLOCK, head_count, head_width).transpose(2, 0, 1, 3)
    value_heads = v_all.reshape(total_blocks, BLOCK, head_count, head_width).transpose(2, 0, 1, 3)
    head_pick = jnp.arange(head_count)[:, None, None]
    key_gath = key_heads[head_pick, key_table].reshape(
        head_count, query_blocks, 8 * BLOCK, head_width
    )
    value_gath = value_heads[head_pick, key_table].reshape(
        head_count, query_blocks, 8 * BLOCK, head_width
    )
    cand_pos = jnp.array(candidates(query_blocks), dtype=jnp.int32)
    cand_blocks = own_blocks[cand_pos]
    cand_seq = cand_blocks // NB
    cand_in_seq = cand_blocks % NB
    cand_global = (cand_in_seq == 0) | (cand_in_seq == NB - 1)
    key_seq = k_all.reshape(seqs_here, LEN, head_count, head_width)[cand_seq].transpose(2, 0, 1, 3)
    value_seq = v_all.reshape(seqs_here, LEN, head_count, head_width)[cand_seq].transpose(
        2, 0, 1, 3
    )
    seg_seq = segs.reshape(seqs_here, LEN)[cand_seq]
    pad_seq = pads.reshape(seqs_here, LEN)[cand_seq]
    query_place = cand_in_seq[:, None] * BLOCK + block_span[None, :]
    seg_query = jnp.take_along_axis(seg_seq, query_place, axis=1)
    positions = jnp.arange(LEN, dtype=jnp.int32)
    allowed_dense = (seg_query[:, :, None] == seg_seq[:, None, :]) & (pad_seq[:, None, :] == 1) | (
        query_place[:, :, None] == positions[None, None, :]
    )
    sparse_part = (query_tiles, key_gath, value_gath, allowed_sparse)
    dense_part = (query_tiles[:, cand_pos], key_seq, value_seq, allowed_dense[None])
    layout = (
        is_global,
        cand_pos,
        cand_global,
        cand_seq,
        key_table,
        head_pick,
        total_blocks,
        seqs_here,
    )
    return (sparse_part, dense_part, layout)


def masked_scores(queries, keys, allowed):
    scale = queries.shape[-1] ** (-0.5)
    raw_scores = (
        jnp.einsum("hgbd,hgkd->hgbk", queries, keys, preferred_element_type=jnp.float32) * scale
    )
    return jnp.where(allowed, raw_scores, NEG)


def group_forward(part):
    queries, keys, values, allowed = part
    scores = masked_scores(queries, keys, allowed)
    row_top = jnp.max(scores, axis=-1, keepdims=True)
    log_total = row_top + jnp.log(jnp.sum(jnp.exp(scores - row_top), axis=-1, keepdims=True))
    softmax_w = jnp.exp(scores - log_total).astype(jnp.bfloat16)
    heads_out = jnp.einsum("hgbk,hgkd->hgbd", softmax_w, values, preferred_element_type=jnp.float32)
    return (heads_out, log_total)


def group_backward(part, log_total, grad_tiles):
    queries, keys, values, allowed = part
    scale = queries.shape[-1] ** (-0.5)
    softmax_w = jnp.exp(masked_scores(queries, keys, allowed) - log_total)
    grad_probs = jnp.einsum(
        "hgbd,hgkd->hgbk", grad_tiles, values, preferred_element_type=jnp.float32
    )
    row_dot = jnp.sum(softmax_w * grad_probs, axis=-1, keepdims=True)
    grad_scores = (softmax_w * (grad_probs - row_dot)).astype(jnp.bfloat16)
    grad_query = (
        jnp.einsum("hgbk,hgkd->hgbd", grad_scores, keys, preferred_element_type=jnp.float32) * scale
    )
    grad_key = (
        jnp.einsum("hgbk,hgbd->hgkd", grad_scores, queries, preferred_element_type=jnp.float32)
        * scale
    )
    grad_value = jnp.einsum(
        "hgbk,hgbd->hgkd",
        softmax_w.astype(jnp.bfloat16),
        grad_tiles,
        preferred_element_type=jnp.float32,
    )
    return (grad_query, grad_key, grad_value)


def attention_forward(arranged):
    sparse_part, dense_part, layout = arranged
    out_sparse, lse_sparse = group_forward(sparse_part)
    out_dense, lse_dense = group_forward(dense_part)
    cand_pos = layout[1]
    cand_global = layout[2]
    merged = out_sparse.at[:, cand_pos].set(
        jnp.where(cand_global[None, :, None, None], out_dense, out_sparse[:, cand_pos])
    )
    head_count = merged.shape[0]
    query_blocks = merged.shape[1]
    head_width = merged.shape[3]
    heads_own = merged.transpose(1, 2, 0, 3).reshape(query_blocks * BLOCK, head_count * head_width)
    return (heads_own, (lse_sparse, lse_dense))


def attention_backward(arranged, lses, grad_own):
    sparse_part, dense_part, layout = arranged
    is_global, cand_pos, cand_global, cand_seq, key_table, head_pick, total_blocks, seqs_here = (
        layout
    )
    head_count = sparse_part[0].shape[0]
    query_blocks = sparse_part[0].shape[1]
    head_width = sparse_part[0].shape[3]
    grad_tiles = grad_own.reshape(query_blocks, BLOCK, head_count, head_width).transpose(2, 0, 1, 3)
    zero_tiles = jnp.zeros_like(grad_tiles)
    grad_sparse = jnp.where(is_global[None, :, None, None], zero_tiles, grad_tiles)
    grad_dense = jnp.where(
        cand_global[None, :, None, None], grad_tiles[:, cand_pos], zero_tiles[:, cand_pos]
    )
    dq_sparse, dk_sparse, dv_sparse = group_backward(sparse_part, lses[0], grad_sparse)
    dq_dense, dk_dense, dv_dense = group_backward(dense_part, lses[1], grad_dense)
    grad_query = dq_sparse.at[:, cand_pos].add(dq_dense)
    grad_query = grad_query.transpose(1, 2, 0, 3).reshape(
        query_blocks * BLOCK, head_count * head_width
    )

    def to_rows(sparse_grad, dense_grad):
        blocks_sum = jnp.zeros((head_count, total_blocks, BLOCK, head_width), jnp.float32)
        blocks_sum = blocks_sum.at[head_pick, key_table].add(
            sparse_grad.reshape(head_count, query_blocks, 8, BLOCK, head_width)
        )
        seq_sum = jnp.zeros((seqs_here, LEN, head_count, head_width), jnp.float32)
        seq_sum = seq_sum.at[cand_seq].add(dense_grad.transpose(1, 2, 0, 3))
        return blocks_sum.transpose(1, 2, 0, 3).reshape(
            total_blocks * BLOCK, head_count * head_width
        ) + seq_sum.reshape(total_blocks * BLOCK, head_count * head_width)

    return (grad_query, to_rows(dk_sparse, dk_dense), to_rows(dv_sparse, dv_dense))


def layer_forward(inputs, weights, segment_ids, pad_mask, rand_blocks):
    w_qkv, w_out, w_up, w_down, ln1_gain, ln1_bias, ln2_gain, ln2_bias = weights
    input_rows, qkv_own = across_col_row(inputs, w_qkv, False)
    qkv_low = qkv_own.astype(jnp.bfloat16)
    part_width = qkv_low.shape[1] // 3
    q_own = qkv_low[:, :part_width]
    k_own = qkv_low[:, part_width : 2 * part_width]
    v_own = qkv_low[:, 2 * part_width :]
    k_all, v_all = (
        lax.all_gather(k_own, "row", axis=0, tiled=True),
        lax.all_gather(v_own, "row", axis=0, tiled=True),
    )
    arranged = arrange(q_own, k_all, v_all, segment_ids, pad_mask, rand_blocks)
    heads_own, lses = attention_forward(arranged)
    heads_rows, attn = across_row_col(heads_own.astype(jnp.bfloat16), w_out, False)
    hidden, normed_one, rstd_one = norm_forward(
        inputs.astype(jnp.float32) + attn, ln1_gain, ln1_bias
    )
    hidden_rows, up_own = across_col_row(hidden.astype(jnp.bfloat16), w_up, False)
    act_low = gelu_tanh(up_own).astype(jnp.bfloat16)
    act_rows, down_own = across_row_col(act_low, w_down, True)
    result, normed_two, rstd_two = norm_forward(hidden + down_own, ln2_gain, ln2_bias)
    saved = (
        input_rows,
        arranged,
        lses,
        heads_rows,
        normed_one,
        rstd_one,
        hidden_rows,
        up_own,
        act_rows,
        normed_two,
        rstd_two,
    )
    return (result, saved)


def layer_backward(grad_out, weights, saved):
    w_qkv, w_out, w_up, w_down, ln1_gain, ln1_bias, ln2_gain, ln2_bias = weights
    (
        input_rows,
        arranged,
        lses,
        heads_rows,
        normed_one,
        rstd_one,
        hidden_rows,
        up_own,
        act_rows,
        normed_two,
        rstd_two,
    ) = saved
    grad_top = grad_out.astype(jnp.float32)
    gain_two_grad = jnp.sum(grad_top * normed_two, axis=0)
    bias_two_grad = jnp.sum(grad_top, axis=0)
    grad_r2 = norm_backward(grad_top, normed_two, rstd_two, ln2_gain)
    down_rows, grad_act = across_col_row(grad_r2.astype(jnp.bfloat16), w_down, False)
    grad_down = contract_rows(down_rows, act_rows)
    primal_out, gelu_back = jax.vjp(gelu_tanh, up_own)
    grad_up_low = gelu_back(grad_act)[0].astype(jnp.bfloat16)
    up_rows, grad_hidden_ffn = across_row_col(grad_up_low, w_up, True)
    grad_up = contract_rows(hidden_rows, up_rows)
    grad_hidden = grad_hidden_ffn + grad_r2
    gain_one_grad = jnp.sum(grad_hidden * normed_one, axis=0)
    bias_one_grad = jnp.sum(grad_hidden, axis=0)
    grad_r1 = norm_backward(grad_hidden, normed_one, rstd_one, ln1_gain)
    attn_rows, grad_heads = across_col_row(grad_r1.astype(jnp.bfloat16), w_out, True)
    grad_w_out = contract_rows(heads_rows, attn_rows)
    grad_q_own, grad_k_all, grad_v_all = attention_backward(
        arranged, lses, grad_heads.astype(jnp.bfloat16)
    )
    grad_k_own, grad_v_own = (
        lax.psum_scatter(
            grad_k_all.astype(jnp.bfloat16), "row", scatter_dimension=0, tiled=True
        ).astype(jnp.float32),
        lax.psum_scatter(
            grad_v_all.astype(jnp.bfloat16), "row", scatter_dimension=0, tiled=True
        ).astype(jnp.float32),
    )
    grad_qkv_low = jnp.concatenate([grad_q_own, grad_k_own, grad_v_own], axis=1).astype(
        jnp.bfloat16
    )
    qkv_rows, grad_in_proj = across_row_col(grad_qkv_low, w_qkv, True)
    grad_qkv = contract_rows(input_rows, qkv_rows)
    grad_qkv, grad_w_out, grad_up, grad_down = (
        lax.psum(grad_qkv.astype(jnp.bfloat16), "dp").astype(jnp.float32),
        lax.psum(grad_w_out.astype(jnp.bfloat16), "dp").astype(jnp.float32),
        lax.psum(grad_up.astype(jnp.bfloat16), "dp").astype(jnp.float32),
        lax.psum(grad_down.astype(jnp.bfloat16), "dp").astype(jnp.float32),
    )
    norm_sums = lax.psum(
        (gain_one_grad, bias_one_grad, gain_two_grad, bias_two_grad), ("dp", "col")
    )
    return (grad_in_proj + grad_r1, grad_qkv, grad_w_out, grad_up, grad_down, norm_sums)


def on_device(
    inputs,
    w_query,
    w_key,
    w_value,
    w_out,
    w_up,
    w_down,
    ln1_gain,
    ln1_bias,
    ln2_gain,
    ln2_bias,
    segment_ids,
    pad_mask,
    rand_blocks,
    grad_out,
):
    feat_part = D // lax.axis_size("row")
    head_part = D // lax.axis_size("col")
    query_local = w_query.reshape(feat_part, head_part)
    key_local = w_key.reshape(feat_part, head_part)
    value_local = w_value.reshape(feat_part, head_part)
    out_local = w_out.reshape(head_part, feat_part)
    w_qkv = jnp.concatenate([query_local, key_local, value_local], axis=1)
    weights = (w_qkv, out_local, w_up, w_down, ln1_gain, ln1_bias, ln2_gain, ln2_bias)
    token_rows = inputs.T
    grad_rows = grad_out.T
    result, saved = layer_forward(token_rows, weights, segment_ids, pad_mask, rand_blocks)
    rows_again, weights_again, grad_again = lax.optimization_barrier(
        (token_rows, weights, grad_rows)
    )
    unused_out, saved_again = layer_forward(
        rows_again, weights_again, segment_ids, pad_mask, rand_blocks
    )
    grads = layer_backward(grad_again, weights_again, saved_again)
    grad_inputs, grad_qkv, grad_w_out, grad_up, grad_down, norm_sums = grads
    return (
        result.astype(jnp.bfloat16).T,
        grad_inputs.T,
        grad_qkv[:, :head_part].reshape(1, 1, -1),
        grad_qkv[:, head_part : 2 * head_part].reshape(1, 1, -1),
        grad_qkv[:, 2 * head_part :].reshape(1, 1, -1),
        grad_w_out.reshape(1, 1, -1),
        grad_up,
        grad_down,
        norm_sums[0],
        norm_sums[1],
        norm_sums[2],
        norm_sums[3],
    )


def solution(mesh):
    return jax.shard_map(
        on_device,
        mesh=mesh,
        in_specs=(
            P("row", ("dp", "col")),
            P("row", "col", None),
            P("row", "col", None),
            P("row", "col", None),
            P("col", "row", None),
            P("row", "col"),
            P("row", "col"),
            P("row"),
            P("row"),
            P("row"),
            P("row"),
            P("dp"),
            P("dp"),
            P("dp", "col", None, None),
            P("row", ("dp", "col")),
        ),
        out_specs=(
            P("row", ("dp", "col")),
            P("row", ("dp", "col")),
            P("row", "col", None),
            P("row", "col", None),
            P("row", "col", None),
            P("col", "row", None),
            P("row", "col"),
            P("row", "col"),
            P("row"),
            P("row"),
            P("row"),
            P("row"),
        ),
        check_vma=False,
    )
```

profile of v0, /device:TPU:0, one launch (start us, length us, event | category | flops | bytes accessed | tf_op | source)
XLA Modules:
  0.0 2603.8 jit_solution(2643630023078504558)
XLA Ops:
  13.2 22.5 all-gather.29.cloned.1.call-done
  44.9 135.5 %gather_fusion.2 = s32[24576]{0:T(1024)S(1)} fusion(s32[4096]{0:T(1024)S(1)} %copy-done.3, s32[24576]{0:T(1024)S(1)} %broadcast_clamp_fusion), kind=kCustom, calls=%fused_computation.4 | custom fusion | bytes 294912 | tf_op jit(solution)/shard_map/gather | solution.py:136
  180.5 23.0 reduce-scatter.23.cloned.1.call-done
  207.3 135.5 %gather_fusion.1 = s32[24576]{0:T(1024)S(1)} fusion(s32[4096]{0:T(1024)S(1)} %copy-done.2, s32[24576]{0:T(1024)S(1)} %broadcast_clamp_fusion), kind=kCustom, calls=%fused_computation.3 | custom fusion | bytes 294912 | tf_op jit(solution)/shard_map/gather | solution.py:135
  419.7 35.4 %all-gather.35.cloned.1.call-done = bf16[4096,192]{0,1:T(8,128)(2,1)} async-done(((bf16[1024,192]{0,1:T(8,128)(2,1)}), bf16[4096,192]{0,1:T(8,128)(2,1)}) %all-gather.35.cloned.1.call-update) | async-done | bytes 1572880 | tf_op jit(solution)/shard_map/all_gather | solution.py:53
  458.9 16.2 all-gather.17.cloned.1.call-done
  481.6 33.8 %reduce-scatter.25.cloned.1.call-done = f32[1024,192]{0,1:T(8,128)} async-done(((f32[4096,192]{0,1:T(8,128)}), f32[1024,192]{0,1:T(8,128)}) %reduce-scatter.25.cloned.1.call-update) | async-done | bytes 786448 | tf_op jit(solution)/shard_map/reduce_scatter | solution.py:61
  529.9 149.2 %reduce-scatter.15.cloned.1.call-done = f32[1024,576]{0,1:T(8,128)} async-done(((f32[4096,576]{0,1:T(8,128)}), f32[1024,576]{0,1:T(8,128)}) %reduce-scatter.15.cloned.1.call-update) | async-done | bytes 2359312 | tf_op jit(solution)/shard_map/reduce_scatter | solution.py:43
  682.7 19.1 all-gather.37.cloned.1.call-done
  712.3 28.6 %all-gather.19.cloned.1.call-done = bf16[4096,192]{0,1:T(8,128)(2,1)} async-done(((bf16[1024,192]{0,1:T(8,128)(2,1)}), bf16[4096,192]{0,1:T(8,128)(2,1)}) %all-gather.19.cloned.1.call-update) | async-done | bytes 1572880 | tf_op jit(solution)/shard_map/all_gather | solution.py:286
  756.7 22.2 all-gather.21.cloned.1.call-done
  820.5 171.5 %reduce-scatter.27.cloned.1.call-done = f32[1024,768]{1,0:T(8,128)} async-done(((f32[4096,768]{1,0:T(8,128)}), f32[1024,768]{1,0:T(8,128)}) %reduce-scatter.27.cloned.1.call-update) | async-done | bytes 3145744 | tf_op jit(solution)/shard_map/reduce_scatter | solution.py:43
  996.0 36.1 %all-gather.23.cloned.1.call-done = bf16[4096,192]{0,1:T(8,128)(2,1)} async-done(((bf16[1024,192]{0,1:T(8,128)(2,1)}), bf16[4096,192]{0,1:T(8,128)(2,1)}) %all-gather.23.cloned.1.call-update) | async-done | bytes 1572880 | tf_op jit(solution)/shard_map/all_gather | solution.py:53
  1035.9 111.9 %all-gather.39.cloned.1.call-done = bf16[4096,768]{1,0:T(8,128)(2,1)} async-done(((bf16[1024,768]{1,0:T(8,128)(2,1)}), bf16[4096,768]{1,0:T(8,128)(2,1)}) %all-gather.39.cloned.1.call-update) | async-done | bytes 6291472 | tf_op jit(solution)/shard_map/all_gather | solution.py:53
  1154.6 31.5 %reduce-scatter.17.cloned.1.call-done = f32[1024,192]{0,1:T(8,128)} async-done(((f32[4096,192]{0,1:T(8,128)}), f32[1024,192]{0,1:T(8,128)}) %reduce-scatter.17.cloned.1.call-update) | async-done | bytes 786448 | tf_op jit(solution)/shard_map/reduce_scatter | solution.py:61
  1188.1 38.2 %reduce-scatter.29.cloned.1.call-done = f32[1024,192]{0,1:T(8,128)} async-done(((f32[4096,192]{0,1:T(8,128)}), f32[1024,192]{0,1:T(8,128)}) %reduce-scatter.29.cloned.1.call-update) | async-done | bytes 786448 | tf_op jit(solution)/shard_map/reduce_scatter | solution.py:61
  1243.3 16.7 all-reduce.2
  1310.7 206.3 %reduce-scatter.31.cloned.1.call-done = f32[1024,768]{1,0:T(8,128)} async-done(((f32[4096,768]{1,0:T(8,128)}), f32[1024,768]{1,0:T(8,128)}) %reduce-scatter.31.cloned.1.call-update) | async-done | bytes 3145744 | tf_op jit(solution)/shard_map/reduce_scatter | solution.py:43
  1522.4 209.8 %reduce-scatter.19.cloned.1.call-done = f32[1024,768]{1,0:T(8,128)} async-done(((f32[4096,768]{1,0:T(8,128)}), f32[1024,768]{1,0:T(8,128)}) %reduce-scatter.19.cloned.1.call-update) | async-done | bytes 3145744 | tf_op jit(solution)/shard_map/reduce_scatter | solution.py:43
  1736.3 113.8 %all-gather.43.cloned.1.call-done = bf16[4096,768]{1,0:T(8,128)(2,1)} async-done(((bf16[1024,768]{1,0:T(8,128)(2,1)}), bf16[4096,768]{1,0:T(8,128)(2,1)}) %all-gather.43.cloned.1.call-update) | async-done | bytes 6291472 | tf_op jit(solution)/shard_map/all_gather | solution.py:53
  1856.9 108.3 %all-gather.27.cloned.1.call-done = bf16[4096,768]{1,0:T(8,128)(2,1)} async-done(((bf16[1024,768]{1,0:T(8,128)(2,1)}), bf16[4096,768]{1,0:T(8,128)(2,1)}) %all-gather.27.cloned.1.call-update) | async-done | bytes 6291472 | tf_op jit(solution)/shard_map/all_gather | solution.py:53
  1972.1 31.7 %reduce-scatter.33.cloned.1.call-done = f32[1024,192]{0,1:T(8,128)} async-done(((f32[4096,192]{0,1:T(8,128)}), f32[1024,192]{0,1:T(8,128)}) %reduce-scatter.33.cloned.1.call-update) | async-done | bytes 786448 | tf_op jit(solution)/shard_map/reduce_scatter | solution.py:61
  2005.6 38.3 %reduce-scatter.21.cloned.1.call-done = f32[1024,192]{0,1:T(8,128)} async-done(((f32[4096,192]{0,1:T(8,128)}), f32[1024,192]{0,1:T(8,128)}) %reduce-scatter.21.cloned.1.call-update) | async-done | bytes 786448 | tf_op jit(solution)/shard_map/reduce_scatter | solution.py:61
  2046.5 18.7 all-reduce.1
  2066.2 17.0 all-gather.45.cloned.1.call-done
  2088.2 59.3 %reduce-scatter.35.cloned.1.call-done = f32[1024,192]{0,1:T(8,128)} async-done(((f32[4096,192]{0,1:T(8,128)}), f32[1024,192]{0,1:T(8,128)}) %reduce-scatter.35.cloned.1.call-update) | async-done | bytes 786448 | tf_op jit(solution)/shard_map/reduce_scatter | solution.py:43
  2196.8 62.2 %scatter_fusion.3 = f32[3,64,64,64]{3,2,1,0:T(8,128)} fusion(f32[3,64,64,64]{3,2,1,0:T(8,128)} %broadcast.946.clone.1, s32[384]{0:T(512)S(1)} %reshape.901, f32[384,64,64]{2,1,0:T(8,128)} %bitcast.245), kind=kCustom, calls=%fused_computation.19 | custom fusion | flops 1572864 | bytes 18877440 | tf_op jit(solution)/shard_map/scatter-add | solution.py:265
  2301.5 61.7 %scatter_fusion.5 = f32[3,64,64,64]{3,2,1,0:T(8,128)} fusion(f32[3,64,64,64]{3,2,1,0:T(8,128)} %broadcast.946.clone, s32[384]{0:T(512)S(1)} %reshape.901, f32[384,64,64]{2,1,0:T(8,128)} %bitcast.244), kind=kCustom, calls=%fused_computation.21 | custom fusion | flops 1572864 | bytes 18877440 | tf_op jit(solution)/shard_map/scatter-add | solution.py:265
  2399.1 21.9 reduce-scatter.39.cloned.1.call-done
  2435.3 76.3 %all-gather.47.cloned.1.call-done = bf16[4096,576]{0,1:T(8,128)(2,1)} async-done(((bf16[1024,576]{0,1:T(8,128)(2,1)}), bf16[4096,576]{0,1:T(8,128)(2,1)}) %all-gather.47.cloned.1.call-update) | async-done | bytes 4718608 | tf_op jit(solution)/shard_map/all_gather | solution.py:53
  2538.4 15.5 all-reduce.8.cloned.1.call-done
  2561.2 33.1 %reduce-scatter.41.cloned.1.call-done = f32[1024,192]{0,1:T(8,128)} async-done(((f32[4096,192]{0,1:T(8,128)}), f32[1024,192]{0,1:T(8,128)}) %reduce-scatter.41.cloned.1.call-update) | async-done | bytes 786448 | tf_op jit(solution)/shard_map/reduce_scatter | solution.py:61
  (461 shorter events, 486.6 us)
Async XLA Ops:
  7.2 694.6 %copy-start = (bf16[192,768]{1,0:T(8,128)(2,1)S(1)}, bf16[192,768]{1,0:T(8,128)(2,1)}, u32[]{:S(2)}) copy-start(bf16[192,768]{1,0:T(8,128)(2,1)} %param.26) | copy-start | bytes 884740
  7.2 28.5 %all-gather.29.cloned.1.call-start = ((), (), s32[]{:S(2)}) async-start(), calls=%async_computation.24 | async-start | bytes 1966080 | tf_op jit(solution)/shard_map/all_gather | solution.py:35
  13.2 190.4 %reduce-scatter.23.cloned.1.call-start = ((), (), s32[]{:S(2)}) async-start(), calls=%async_computation.25 | async-start | bytes 11796480 | tf_op jit(solution)/shard_map/reduce_scatter | solution.py:43
  42.2 317.8 %all-gather.31.cloned.1.call-start = ((), (), s32[]{:S(2)}) async-start(), calls=%async_computation.26 | async-start | bytes 1966080 | tf_op jit(solution)/shard_map/all_gather | solution.py:286
  206.3 180.5 %all-gather.33.cloned.1.call-start = ((), (), s32[]{:S(2)}) async-start(), calls=%async_computation.27 | async-start | bytes 1966080 | tf_op jit(solution)/shard_map/all_gather | solution.py:287
  348.7 106.4 %all-gather.35.cloned.1.call-start = ((), (), s32[]{:S(2)}) async-start(), calls=%async_computation.28 | async-start | bytes 1966080 | tf_op jit(solution)/shard_map/all_gather | solution.py:53
  419.1 56.0 %all-gather.17.cloned.1.call-start = ((), (), s32[]{:S(2)}) async-start(), calls=%async_computation.14 | async-start | bytes 1966080 | tf_op jit(solution)/shard_map/all_gather | solution.py:35
  419.7 95.7 %reduce-scatter.25.cloned.1.call-start = ((), (), s32[]{:S(2)}) async-start(), calls=%async_computation.29 | async-start | bytes 3932160 | tf_op jit(solution)/shard_map/reduce_scatter | solution.py:61
  458.8 220.2 %reduce-scatter.15.cloned.1.call-start = ((), (), s32[]{:S(2)}) async-start(), calls=%async_computation.15 | async-start | bytes 11796480 | tf_op jit(solution)/shard_map/reduce_scatter | solution.py:43
  481.6 220.2 %all-gather.37.cloned.1.call-start = ((), (), s32[]{:S(2)}) async-start(), calls=%async_computation.30 | async-start | bytes 1966080 | tf_op jit(solution)/shard_map/all_gather | solution.py:35
  529.8 211.1 %all-gather.19.cloned.1.call-start = ((), (), s32[]{:S(2)}) async-start(), calls=%async_computation.16 | async-start | bytes 1966080 | tf_op jit(solution)/shard_map/all_gather | solution.py:286
  681.9 97.0 %all-gather.21.cloned.1.call-start = ((), (), s32[]{:S(2)}) async-start(), calls=%async_computation.17 | async-start | bytes 1966080 | tf_op jit(solution)/shard_map/all_gather | solution.py:287
  682.6 309.3 %reduce-scatter.27.cloned.1.call-start = ((), (), s32[]{:S(2)}) async-start(), calls=%async_computation.31 | async-start | bytes 15728640 | tf_op jit(solution)/shard_map/reduce_scatter | solution.py:43
  709.7 322.5 %all-gather.23.cloned.1.call-start = ((), (), s32[]{:S(2)}) async-start(), calls=%async_computation.18 | async-start | bytes 1966080 | tf_op jit(solution)/shard_map/all_gather | solution.py:53
  820.4 327.4 %all-gather.39.cloned.1.call-start = ((), (), s32[]{:S(2)}) async-start(), calls=%async_computation.32 | async-start | bytes 7864320 | tf_op jit(solution)/shard_map/all_gather | solution.py:53
  996.0 190.2 %reduce-scatter.17.cloned.1.call-start = ((), (), s32[]{:S(2)}) async-start(), calls=%async_computation.19 | async-start | bytes 3932160 | tf_op jit(solution)/shard_map/reduce_scatter | solution.py:61
  1035.9 190.4 %reduce-scatter.29.cloned.1.call-start = ((), (), s32[]{:S(2)}) async-start(), calls=%async_computation.33 | async-start | bytes 3932160 | tf_op jit(solution)/shard_map/reduce_scatter | solution.py:61
  1154.6 126.5 %all-gather.41.cloned.1.call-start = ((), (), s32[]{:S(2)}) async-start(), calls=%async_computation.34 | async-start | bytes 1966080 | tf_op jit(solution)/shard_map/all_gather | solution.py:35
  1263.6 39.1 %all-gather.25.cloned.1.call-start = ((), (), s32[]{:S(2)}) async-start(), calls=%async_computation.20 | async-start | bytes 1966080 | tf_op jit(solution)/shard_map/all_gather | solution.py:35
  1266.7 250.3 %reduce-scatter.31.cloned.1.call-start = ((), (), s32[]{:S(2)}) async-start(), calls=%async_computation.35 | async-start | bytes 15728640 | tf_op jit(solution)/shard_map/reduce_scatter | solution.py:43
  1288.9 443.3 %reduce-scatter.19.cloned.1.call-start = ((), (), s32[]{:S(2)}) async-start(), calls=%async_computation.21 | async-start | bytes 15728640 | tf_op jit(solution)/shard_map/reduce_scatter | solution.py:43
  1310.6 539.5 %all-gather.43.cloned.1.call-start = ((), (), s32[]{:S(2)}) async-start(), calls=%async_computation.36 | async-start | bytes 7864320 | tf_op jit(solution)/shard_map/all_gather | solution.py:53
  1521.9 443.3 %all-gather.27.cloned.1.call-start = ((), (), s32[]{:S(2)}) async-start(), calls=%async_computation.22 | async-start | bytes 7864320 | tf_op jit(solution)/shard_map/all_gather | solution.py:53
  1736.3 267.5 %reduce-scatter.33.cloned.1.call-start = ((), (), s32[]{:S(2)}) async-start(), calls=%async_computation.37 | async-start | bytes 3932160 | tf_op jit(solution)/shard_map/reduce_scatter | solution.py:61
  1856.9 187.0 %reduce-scatter.21.cloned.1.call-start = ((), (), s32[]{:S(2)}) async-start(), calls=%async_computation.23 | async-start | bytes 3932160 | tf_op jit(solution)/shard_map/reduce_scatter | solution.py:61
  1972.0 111.2 %all-gather.45.cloned.1.call-start = ((), (), s32[]{:S(2)}) async-start(), calls=%async_computation.38 | async-start | bytes 1966080 | tf_op jit(solution)/shard_map/all_gather | solution.py:35
  2066.2 81.3 %reduce-scatter.35.cloned.1.call-start = ((), (), s32[]{:S(2)}) async-start(), calls=%async_computation.39 | async-start | bytes 3932160 | tf_op jit(solution)/shard_map/reduce_scatter | solution.py:43
  2086.9 312.1 %reduce-scatter.37.cloned.1.call-start = ((), (), s32[]{:S(2)}) async-start(), calls=%async_computation.40 | async-start | bytes 1966080 | tf_op jit(solution)/shard_map/reduce_scatter | solution.py:350
  2281.0 139.9 %reduce-scatter.39.cloned.1.call-start = ((), (), s32[]{:S(2)}) async-start(), calls=%async_computation.41 | async-start | bytes 1966080 | tf_op jit(solution)/shard_map/reduce_scatter | solution.py:353
  2385.3 126.3 %all-gather.47.cloned.1.call-start = ((), (), s32[]{:S(2)}) async-start(), calls=%async_computation.42 | async-start | bytes 5898240 | tf_op jit(solution)/shard_map/all_gather | solution.py:53
  2423.2 130.7 %all-reduce.8.cloned.1.call-start = ((), (), s32[]{:S(2)}) async-start(), calls=%async_computation.44 | async-start | bytes 1966080 | tf_op jit(solution)/shard_map/psum | solution.py:363
  2516.5 77.7 %reduce-scatter.41.cloned.1.call-start = ((), (), s32[]{:S(2)}) async-start(), calls=%async_computation.43 | async-start | bytes 3932160 | tf_op jit(solution)/shard_map/reduce_scatter | solution.py:61
  (94 other events, 2411.3 us)
Sparse Core Ops, SparseCore 0:
  13.3 22.3 all-gather.28
  42.3 161.1 reduce-scatter.22
  206.5 37.9 all-gather.30
  348.8 37.9 all-gather.32
  419.2 35.8 all-gather.34
  456.6 18.4 all-gather.16
  477.6 37.7 reduce-scatter.24
  517.7 161.2 reduce-scatter.14
  681.2 20.5 all-gather.36
  703.8 37.0 all-gather.18
  743.0 35.8 all-gather.20
  781.1 210.7 reduce-scatter.26
  994.1 38.0 all-gather.22
  1033.6 114.1 all-gather.38
  1150.2 35.9 reduce-scatter.16
  1188.5 37.7 reduce-scatter.28
  1263.8 17.2 all-gather.40
  1283.1 19.6 all-gather.24
  1305.1 211.8 reduce-scatter.30
  1519.2 212.9 reduce-scatter.18
  1733.7 116.3 all-gather.42
  1851.7 113.5 all-gather.26
  1967.8 35.9 reduce-scatter.32
  2006.1 37.7 reduce-scatter.20
  2066.3 16.8 all-gather.44
  2087.0 60.3 reduce-scatter.34
  2281.1 35.3 reduce-scatter.36
  2385.4 35.5 reduce-scatter.38
  2423.3 88.2 all-gather.46
  2516.6 37.2 all-reduce.7
  2556.5 37.7 reduce-scatter.40
where the time goes:
time: 2610 us; the launch traced here: 2600 us
  waiting for transfers between devices  1700 us (65%)
  local copies, waits for them, and re-layouts  430 us (16%)
  other arithmetic  219 us (8%)
  matrix products  159 us (6%)
  blocking collectives  74.8 us (3%)
    reduce_scatter x6, waiting for transfers between devices, across_col_row(): lax.psum_scatter(partial_term(jnp.int32(0), own_rows * lax.axis_size('row...  819 us
    all_gather x6, waiting for transfers between devices, across_row_col(): gathered = lax.all_gather(values, 'row', axis=0, tiled=True)  482 us
    reduce_scatter x6, waiting for transfers between devices, across_row_col(): lax.psum_scatter(partial_term(jnp.int32(0), own_rows * lax.axis_size('col...  207 us
    gather x2, local copies, waits for them, and re-layouts, arrange(): segs[key_tok][:, :, None, :]  136 us
    gather x1, local copies, waits for them, and re-layouts, arrange(): pads[key_tok][:, :, None, :] == 1  136 us
    scatter-add x2, other arithmetic, to_rows(): blocks_sum.at[head_pick, key_table]  124 us
    all_gather x6, waiting for transfers between devices, across_col_row(): gathered = lax.all_gather(values, 'col', axis=0, tiled=True)  103 us
    psum x4, blocking collectives, row_totals(): return lax.psum((first_sum, second_sum), 'row')  60.1 us
  transfers between devices with their start and end apart: 31, of which 29 were waited for; matrix products, arithmetic and copies ran while one was open for 23% of the time, Pallas kernels for 0%

commit v1 on v0

v1 whole, which is shorter than its diff:
```python
import functools

import jax
import jax.numpy as jnp
from jax import lax
from jax.experimental import pallas as pl
from jax.experimental.pallas import tpu as pltpu
from jax.sharding import PartitionSpec as P

BLOCK = 64
HW = 64
LANES = 128
NEG = -1000000000.0
EPS = 1e-06
BF = jnp.bfloat16
F32 = jnp.float32


def mm(left, right):
    return lax.dot_general(left, right, (((1,), (0,)), ((), ())), preferred_element_type=F32)


def mm_nt(left, right):
    return lax.dot_general(left, right, (((1,), (1,)), ((), ())), preferred_element_type=F32)


def mm_tn(left, right):
    return lax.dot_general(left, right, (((0,), (0,)), ((), ())), preferred_element_type=F32)


def block_of(j, row, per, rows):
    return (j // per) * (per * rows) + row * per + j % per


def rows_at(ref, block, head):
    start = pl.multiple_of(block * BLOCK, BLOCK)
    return ref[pl.ds(start, BLOCK), head * LANES : (head + 1) * LANES]


def sparse_lists(rand_ref, head, pos, nb):
    picks = [rand_ref[(head * nb + pos) * 3 + i] for i in range(3)]
    before = jnp.maximum(pos - 1, 0)
    after = jnp.minimum(pos + 1, nb - 1)
    blocks = [0, nb - 1, before, pos, after] + picks
    masks = [
        0,
        nb - 1,
        jnp.where(pos >= 2, before, 2 * nb),
        nb + pos,
        jnp.where(pos <= nb - 3, after, 2 * nb),
    ] + picks
    return blocks, masks


def dense_lists(group, pos, nb):
    blocks = [group * 8 + i for i in range(8)]
    masks = [jnp.where(b == pos, nb + b, b) for b in blocks]
    return blocks, masks


def gather(ref, blocks, head):
    return jnp.concatenate([rows_at(ref, b, head) for b in blocks], axis=0)


def scores_of(query, query_mask, keys, key_mask):
    return jnp.where(mm_nt(query_mask, key_mask) > 0.5, mm_nt(query, keys), NEG)


def forward_kernel(heads, nb, per, rows, row_ref, rand_ref, q_ref, qm_ref, kv_ref, km_ref, o_ref, lse_ref):
    row = row_ref[0]

    def place(j, head):
        start = pl.multiple_of(j * BLOCK, BLOCK)
        return pl.ds(start, BLOCK), slice(head * LANES, (head + 1) * LANES)

    def step(j, carry):
        pos = block_of(j, row, per, rows)
        is_global = (pos == 0) | (pos == nb - 1)
        query_mask = qm_ref[pl.ds(pl.multiple_of(j * BLOCK, BLOCK), BLOCK), :]

        @pl.when(jnp.logical_not(is_global))
        def _():
            for head in range(heads):
                at = place(j, head)
                blocks, masks = sparse_lists(rand_ref, head, pos, nb)
                keys = gather(kv_ref, blocks, head)
                score = scores_of(q_ref[at], query_mask, keys, gather(km_ref, masks, 0))
                top = jnp.max(score, axis=1, keepdims=True)
                weight = jnp.exp(score - top)
                total = jnp.sum(weight, axis=1, keepdims=True)
                probs = (weight * (1.0 / total)).astype(BF)
                o_ref[at] = mm(probs, keys).astype(BF)
                lse_ref[at] = jnp.broadcast_to(top + jnp.log(total), (BLOCK, LANES))

        @pl.when(is_global)
        def _():
            def score_at(group, head):
                blocks, masks = dense_lists(group, pos, nb)
                keys = gather(kv_ref, blocks, head)
                score = scores_of(
                    q_ref[place(j, head)], query_mask, keys, gather(km_ref, masks, 0)
                )
                return score, keys

            def stats(group, kept):
                new = []
                for head in range(heads):
                    top, total = kept[head]
                    score, _ = score_at(group, head)
                    above = jnp.maximum(top, jnp.max(score, axis=1, keepdims=True))
                    total = total * jnp.exp(top - above) + jnp.sum(
                        jnp.exp(score - above), axis=1, keepdims=True
                    )
                    new.append((above, total))
                return tuple(new)

            first = tuple(
                (jnp.full((BLOCK, 1), 2 * NEG, F32), jnp.zeros((BLOCK, 1), F32))
                for _ in range(heads)
            )
            found = lax.fori_loop(0, nb // 8, stats, first)
            lses = [top + jnp.log(total) for top, total in found]

            def outs(group, kept):
                new = []
                for head in range(heads):
                    score, keys = score_at(group, head)
                    new.append(kept[head] + mm(jnp.exp(score - lses[head]).astype(BF), keys))
                return tuple(new)

            done = lax.fori_loop(
                0, nb // 8, outs, tuple(jnp.zeros((BLOCK, LANES), F32) for _ in range(heads))
            )
            for head in range(heads):
                at = place(j, head)
                o_ref[at] = done[head].astype(BF)
                lse_ref[at] = jnp.broadcast_to(lses[head], (BLOCK, LANES))

        return carry

    lax.fori_loop(0, q_ref.shape[0] // BLOCK, step, 0)


def backward_kernel(
    heads, nb, per, rows, row_ref, rand_ref, q_ref, qm_ref, kv_ref, km_ref, do_ref, lse_ref,
    dq_ref, dkv_ref, acc_ref,
):
    row = row_ref[0]
    acc_ref[...] = jnp.zeros_like(acc_ref)

    def place(j, head):
        start = pl.multiple_of(j * BLOCK, BLOCK)
        return pl.ds(start, BLOCK), slice(head * LANES, (head + 1) * LANES)

    def parts(j, head, query_mask, blocks, masks):
        at = place(j, head)
        keys = gather(kv_ref, blocks, head)
        score = scores_of(q_ref[at], query_mask, keys, gather(km_ref, masks, 0))
        lse = lse_ref[at][:, :1]
        probs = jnp.exp(score - lse)
        return keys, probs, mm_nt(do_ref[at], keys)

    def finish(j, head, blocks, keys, probs, grad_probs, dot_row):
        at = place(j, head)
        low = (probs * (grad_probs - dot_row)).astype(BF)
        both = jnp.concatenate([low, probs.astype(BF)], axis=0)
        sides = jnp.concatenate([q_ref[at], do_ref[at]], axis=0)
        grad = mm_tn(both, sides)
        for i, block in enumerate(blocks):
            start = pl.multiple_of(block * BLOCK, BLOCK)
            acc_ref[pl.ds(start, BLOCK), at[1]] += grad[i * BLOCK : (i + 1) * BLOCK, :]
        return mm(low, keys)

    def step(j, carry):
        pos = block_of(j, row, per, rows)
        is_global = (pos == 0) | (pos == nb - 1)
        query_mask = qm_ref[pl.ds(pl.multiple_of(j * BLOCK, BLOCK), BLOCK), :]

        @pl.when(jnp.logical_not(is_global))
        def _():
            for head in range(heads):
                blocks, masks = sparse_lists(rand_ref, head, pos, nb)
                keys, probs, grad_probs = parts(j, head, query_mask, blocks, masks)
                dot_row = jnp.sum(probs * grad_probs, axis=1, keepdims=True)
                grad_q = finish(j, head, blocks, keys, probs, grad_probs, dot_row)
                dq_ref[place(j, head)] = (grad_q * 0.125).astype(BF)

        @pl.when(is_global)
        def _():
            def dots(group, kept):
                blocks, masks = dense_lists(group, pos, nb)
                new = []
                for head in range(heads):
                    _, probs, grad_probs = parts(j, head, query_mask, blocks, masks)
                    new.append(kept[head] + jnp.sum(probs * grad_probs, axis=1, keepdims=True))
                return tuple(new)

            dot_rows = lax.fori_loop(
                0, nb // 8, dots, tuple(jnp.zeros((BLOCK, 1), F32) for _ in range(heads))
            )

            def grads(group, kept):
                blocks, masks = dense_lists(group, pos, nb)
                new = []
                for head in range(heads):
                    keys, probs, grad_probs = parts(j, head, query_mask, blocks, masks)
                    new.append(
                        kept[head]
                        + finish(j, head, blocks, keys, probs, grad_probs, dot_rows[head])
                    )
                return tuple(new)

            done = lax.fori_loop(
                0, nb // 8, grads, tuple(jnp.zeros((BLOCK, LANES), F32) for _ in range(heads))
            )
            for head in range(heads):
                dq_ref[place(j, head)] = (done[head] * 0.125).astype(BF)

        return carry

    lax.fori_loop(0, q_ref.shape[0] // BLOCK, step, 0)
    span = per * BLOCK

    def out(i, carry):
        source = (i % rows) * (rows * span) + (i // rows) * span
        dkv_ref[pl.ds(pl.multiple_of(i * span, span), span), :] = acc_ref[
            pl.ds(pl.multiple_of(source, span), span), :
        ].astype(BF)
        return carry

    lax.fori_loop(0, kv_ref.shape[0] // span, out, 0)


def specs(count):
    return [pl.BlockSpec(memory_space=pltpu.SMEM)] * 2 + [
        pl.BlockSpec(memory_space=pltpu.VMEM)
    ] * count


def attention_forward(dims, row, rand, q, q_mask, kv, k_mask):
    own, wide = q.shape
    vmem = pl.BlockSpec(memory_space=pltpu.VMEM)
    return pl.pallas_call(
        functools.partial(forward_kernel, *dims),
        name="attn_fwd",
        out_shape=(
            jax.ShapeDtypeStruct((own, wide), BF),
            jax.ShapeDtypeStruct((own, wide), F32),
        ),
        in_specs=specs(4),
        out_specs=(vmem, vmem),
        cost_estimate=pl.CostEstimate(
            flops=own * 512 * wide * 6, bytes_accessed=12 << 20, transcendentals=own * 512 * 3
        ),
        compiler_params=pltpu.CompilerParams(vmem_limit_bytes=48 << 20),
    )(row, rand, q, q_mask, kv, k_mask)


def attention_backward(dims, row, rand, q, q_mask, kv, k_mask, d_o, lse):
    own, wide = q.shape
    vmem = pl.BlockSpec(memory_space=pltpu.VMEM)
    return pl.pallas_call(
        functools.partial(backward_kernel, *dims),
        name="attn_bwd",
        out_shape=(
            jax.ShapeDtypeStruct((own, wide), BF),
            jax.ShapeDtypeStruct(kv.shape, BF),
        ),
        in_specs=specs(6),
        out_specs=(vmem, vmem),
        scratch_shapes=[pltpu.VMEM(kv.shape, F32)],
        cost_estimate=pl.CostEstimate(
            flops=own * 512 * wide * 12, bytes_accessed=20 << 20, transcendentals=own * 512 * 3
        ),
        compiler_params=pltpu.CompilerParams(vmem_limit_bytes=48 << 20),
    )(row, rand, q, q_mask, kv, k_mask, d_o, lse)


def norm(resid, gain, bias):
    mean = jnp.mean(resid, axis=1, keepdims=True)
    var = jnp.mean(resid * resid, axis=1, keepdims=True) - mean * mean
    rstd = lax.rsqrt(var + EPS)
    normed = (resid - mean) * rstd
    return normed * gain + bias, normed, rstd


def norm_grad(grad, normed, rstd, gain):
    scaled = grad * gain
    first = jnp.mean(scaled, axis=1, keepdims=True)
    second = jnp.mean(scaled * normed, axis=1, keepdims=True)
    return rstd * (scaled - first - normed * second)


def gelu(value):
    return jax.nn.gelu(value, approximate=True)


def on_device(
    inputs, w_query, w_key, w_value, w_out, w_up, w_down,
    ln1_gain, ln1_bias, ln2_gain, ln2_bias, segment_ids, pad_mask, rand_blocks, grad_out,
):
    rows, cols = lax.axis_size("row"), lax.axis_size("col")
    row, col = lax.axis_index("row"), lax.axis_index("col")
    feat, local = inputs.shape
    model = feat * rows
    hid = model // cols
    heads = hid // HW
    length = local * cols
    nb = length // BLOCK
    span = local // rows
    per = span // BLOCK
    dims = (heads, nb, per, rows)
    own = cols * span

    blk_q = w_query.reshape(feat, hid)
    blk_k = w_key.reshape(feat, hid)
    blk_v = w_value.reshape(feat, hid)
    blk_o = w_out.reshape(hid, feat)
    w_qkv = jnp.concatenate([blk_q, blk_k, blk_v], axis=1)
    w_own = lax.all_gather(w_qkv, "row", axis=0, tiled=True)
    x_parts = lax.all_gather(inputs, ("row", "col"), axis=0).reshape(rows, cols, feat, local)
    gains = lax.all_gather(
        jnp.stack([ln1_gain, ln1_bias, ln2_gain, ln2_bias]), "row", axis=0
    ).transpose(1, 0, 2).reshape(4, 1, model)
    grad_rows = lax.all_to_all(grad_out, "row", 1, 0, tiled=True).T.astype(F32)

    w_heads = w_own.reshape(model, 3, heads, HW)
    w_kv = jnp.concatenate([w_heads[:, 1], w_heads[:, 2]], axis=2).reshape(model, heads * LANES)
    w_q = jnp.pad(w_heads[:, 0], ((0, 0), (0, 0), (0, HW))).reshape(model, heads * LANES)
    x_all = x_parts.transpose(0, 2, 1, 3).reshape(model, length)
    x_own = lax.dynamic_index_in_dim(
        x_parts.reshape(rows, cols, feat, rows, span), row, axis=3, keepdims=False
    )
    x_res = lax.dynamic_index_in_dim(x_own, col, axis=1, keepdims=False)
    x_res = x_res.reshape(model, span).T.astype(F32)
    x_own = x_own.transpose(0, 2, 1, 3).reshape(model, own)
    kv = mm_tn(x_all, w_kv).astype(BF)
    q = (mm_tn(x_own, w_q).astype(BF) * 0.125).astype(BF)

    kinds = jnp.arange(BLOCK, dtype=jnp.int32)
    seg_hot = segment_ids[:, None] == kinds[None, :]
    key_hot = (seg_hot & (pad_mask[:, None] == 1)).astype(BF)
    place_hot = ((jnp.arange(length, dtype=jnp.int32) % BLOCK)[:, None] == kinds[None, :]).astype(BF)
    zeros = jnp.zeros_like(key_hot)
    k_mask = jnp.concatenate(
        [
            jnp.concatenate([key_hot, zeros], axis=1),
            jnp.concatenate([key_hot, place_hot], axis=1),
            jnp.zeros((BLOCK, LANES), BF),
        ],
        axis=0,
    )
    q_mask = jnp.concatenate([seg_hot.astype(BF), place_hot], axis=1)
    q_mask = lax.dynamic_index_in_dim(
        q_mask.reshape(cols, rows, span, LANES), row, axis=1, keepdims=False
    ).reshape(own, LANES)
    rand = rand_blocks.reshape(-1)
    row_arr = jnp.reshape(row, (1,)).astype(jnp.int32)

    o_wide, lse = attention_forward(dims, row_arr, rand, q, q_mask, kv, k_mask)
    o_own = o_wide.reshape(own, heads, 2, HW)[:, :, 1].reshape(own, hid)
    o = lax.all_to_all(o_own, "col", 0, 1, tiled=True)

    small = lax.all_gather(jnp.concatenate([w_qkv, blk_o.T], axis=1), ("row", "col"), axis=0)
    small = small.reshape(rows, cols, feat, 3 * hid + hid)
    w_o = small[..., 3 * hid :].transpose(0, 2, 1, 3).reshape(model, model)
    w_back = small[..., : 3 * hid].transpose(0, 2, 1, 3).reshape(model, 3 * model)
    up = lax.all_gather(w_up, ("row", "col"), axis=0).reshape(rows, cols, feat, -1)
    up = up.transpose(0, 2, 1, 3).reshape(model, -1)
    down = lax.all_gather(w_down, ("row", "col"), axis=0).reshape(rows, cols, feat, -1)
    down = down.transpose(0, 2, 1, 3).reshape(model, -1)

    gain1, bias1, gain2, bias2 = gains[0], gains[1], gains[2], gains[3]
    hidden, normed1, rstd1 = norm(x_res + mm_nt(o, w_o), gain1, bias1)
    hidden_low = hidden.astype(BF)
    up_val = mm(hidden_low, up)
    act, gelu_back = jax.vjp(gelu, up_val)
    act = act.astype(BF)
    result, normed2, rstd2 = norm(hidden + mm_nt(act, down), gain2, bias2)
    output = lax.all_to_all(result.T.astype(BF), "row", 0, 1, tiled=True)

    g_gain2 = jnp.sum(grad_rows * normed2, axis=0)
    g_bias2 = jnp.sum(grad_rows, axis=0)
    grad2 = norm_grad(grad_rows, normed2, rstd2, gain2)
    df = grad2.astype(BF)
    g_down = mm_tn(df, act).astype(BF)
    du = gelu_back(mm(df, down))[0].astype(BF)
    g_up = mm_tn(hidden_low, du).astype(BF)
    dh = mm_nt(du, up) + grad2
    g_gain1 = jnp.sum(dh * normed1, axis=0)
    g_bias1 = jnp.sum(dh, axis=0)
    grad1 = norm_grad(dh, normed1, rstd1, gain1)
    dattn = grad1.astype(BF)
    g_out = mm_tn(dattn, o).astype(BF)
    d_o = mm(dattn, w_o).astype(BF)
    d_o = lax.all_to_all(d_o, "col", 1, 0, tiled=True)
    d_o = jnp.pad(d_o.reshape(own, heads, HW), ((0, 0), (0, 0), (HW, 0))).reshape(own, -1)

    dq, dkv = attention_backward(dims, row_arr, rand, q, q_mask, kv, k_mask, d_o, lse)
    dkv = lax.psum_scatter(dkv, "row", scatter_dimension=0, tiled=True)

    def grid(grad):
        return grad.reshape(rows, feat, cols, -1).transpose(0, 2, 1, 3).reshape(rows * cols, feat, -1)

    g_ffn = jnp.concatenate([grid(g_up), grid(g_down), grid(g_out)], axis=2)
    g_ffn = lax.psum_scatter(g_ffn, ("row", "col"), scatter_dimension=0, tiled=True)
    g_ffn = lax.psum(g_ffn.reshape(feat, -1), "dp").astype(F32)

    dq = dq.reshape(own, heads, 2, HW)[:, :, 0].reshape(own, hid)
    dkv = dkv.reshape(own, heads, 2, HW)
    dqkv = jnp.concatenate(
        [dq, dkv[:, :, 0].reshape(own, hid), dkv[:, :, 1].reshape(own, hid)], axis=1
    )
    g_qkv = mm(x_own, dqkv).astype(BF)
    g_qkv = lax.psum_scatter(g_qkv, "row", scatter_dimension=0, tiled=True)
    g_qkv = lax.psum(g_qkv, "dp").astype(F32)
    dqkv = lax.all_to_all(dqkv, "col", 0, 1, tiled=True)
    grad_in = mm_nt(dqkv, w_back) + grad1
    grad_in = lax.all_to_all(grad_in.T, "row", 0, 1, tiled=True)

    sums = lax.psum(jnp.stack([g_gain1, g_bias1, g_gain2, g_bias2]), ("dp", "row", "col"))
    sums = lax.dynamic_slice_in_dim(sums, row * feat, feat, axis=1)
    ff = w_up.shape[1]
    return (
        output,
        grad_in,
        g_qkv[:, :hid].reshape(1, 1, -1),
        g_qkv[:, hid : 2 * hid].reshape(1, 1, -1),
        g_qkv[:, 2 * hid :].reshape(1, 1, -1),
        g_ffn[:, 2 * ff :].T.reshape(1, 1, -1),
        g_ffn[:, :ff],
        g_ffn[:, ff : 2 * ff],
        sums[0],
        sums[1],
        sums[2],
        sums[3],
    )


def solution(mesh):
    tokens = P("row", ("dp", "col"))
    grid = P("row", "col", None)
    return jax.shard_map(
        on_device,
        mesh=mesh,
        in_specs=(
            tokens,
            grid,
            grid,
            grid,
            P("col", "row", None),
            P("row", "col"),
            P("row", "col"),
            P("row"),
            P("row"),
            P("row"),
            P("row"),
            P("dp"),
            P("dp"),
            P("dp", "col", None, None),
            tokens,
        ),
        out_specs=(
            tokens,
            tokens,
            grid,
            grid,
            grid,
            P("col", "row", None),
            P("row", "col"),
            P("row", "col"),
            P("row"),
            P("row"),
            P("row"),
            P("row"),
        ),
        check_vma=False,
    )
```

time: 2610 us -> 690 us (0.26)
  waiting for transfers between devices: 1700 us -> 240 us
  local copies, waits for them, and re-layouts: 430 us -> 145 us
  other arithmetic: 219 us -> 39.6 us
  matrix products: 159 us -> 39.5 us
  Pallas kernels: 0 us -> 71.5 us
  blocking collectives: 74.8 us -> 108 us
    reduce_scatter x14 -> x3, waiting for transfers between devices: 1050 us -> 152 us  [the longest x1 93.3 us: on_device(): lax.psum_scatter(g_ffn, ('row', 'col'), scatter_dimension=0, tiled=True)]
    all_gather x16 -> x4, waiting for transfers between devices: 638 us -> 70.2 us  [the longest x1 53.1 us: on_device(): lax.all_gather(inputs, ('row', 'col'), axis=0)]
    gather x21 -> x0, local copies, waits for them, and re-layouts: 312 us -> none  [the longest x2 136 us: arrange(): segs[key_tok][:, :, None, :]]
    scatter-add x5 -> x0, other arithmetic: 137 us -> none  [the longest x2 124 us: to_rows(): blocks_sum.at[head_pick, key_table]]
    dot_general x31 -> x13, matrix products: 149 us -> 39.5 us  [the longest x5 15 us: mm_tn(): lax.dot_general(left, right, (((0,), (0,)), ((), ())), preferred_element_...]
    pallas_call x0 -> x2, Pallas kernels: none -> 71.5 us  [the longest x1 40.5 us: attention_backward(): pl.pallas_call(functools.partial(backward_kernel, *dims), name='attn_bwd'...]
    all_gather x0 -> x2, blocking collectives: none -> 56.7 us  [the longest x1 39.7 us: on_device(): w_own = lax.all_gather(w_qkv, 'row', axis=0, tiled=True)]
    psum x5 -> x1, blocking collectives: 74.8 us -> 40.7 us  [on_device(): lax.psum(jnp.stack([g_gain1, g_bias1, g_gain2, g_bias2]), ('dp', 'row', '...]
  transfers between devices with their start and end apart: 31 -> 13, of which waited for: 29 -> 5; matrix products, arithmetic and copies ran while one was open for 23% -> 27% of each run, Pallas kernels for 0% -> 5%
where the time goes in v1:
time: 690 us; the launch traced here: 681 us
  waiting for transfers between devices  240 us (35%)
  local copies, waits for them, and re-layouts  145 us (21%)
  blocking collectives  108 us (16%)
  Pallas kernels  71.5 us (10%)
  other arithmetic  39.6 us (6%)
  matrix products  39.5 us (6%)
  starting transfers between devices  22.7 us (3%)
  between operations  15.4 us (2%)
    reduce_scatter x1, waiting for transfers between devices, on_device(): lax.psum_scatter(g_ffn, ('row', 'col'), scatter_dimension=0, tiled=True)  93.3 us
    reduce_scatter x1, waiting for transfers between devices, on_device(): dkv = lax.psum_scatter(dkv, 'row', scatter_dimension=0, tiled=True)  58.3 us
    all_gather x1, waiting for transfers between devices, on_device(): lax.all_gather(inputs, ('row', 'col'), axis=0)  53.1 us
    psum x1, blocking collectives, on_device(): lax.psum(jnp.stack([g_gain1, g_bias1, g_gain2, g_bias2]), ('dp', 'row', '...  40.7 us
    pallas_call x1, Pallas kernels, attention_backward(): pl.pallas_call(functools.partial(backward_kernel, *dims), name='attn_bwd'...  40.5 us
    all_gather x1, blocking collectives, on_device(): w_own = lax.all_gather(w_qkv, 'row', axis=0, tiled=True)  39.7 us
    pallas_call x1, Pallas kernels, attention_forward(): pl.pallas_call(functools.partial(forward_kernel, *dims), name='attn_fwd',...  31.1 us
    reshape x3, local copies, waits for them, and re-layouts, grid(): grad.reshape(rows, feat, cols, -1).transpose(0, 2, 1, 3)  23.4 us
  transfers between devices with their start and end apart: 13, of which 5 were waited for; matrix products, arithmetic and copies ran while one was open for 27% of the time, Pallas kernels for 5%

profile of v1, /device:TPU:0, one launch (start us, length us, event | category | flops | bytes accessed | tf_op | source)
XLA Modules:
  0.0 681.3 jit_solution(3230870901898116265)
XLA Ops:
  17.0 6.3 all-to-all-start.2
  23.5 39.7 %all_gather.35 = bf16[768,576]{1,0:T(8,128)(2,1)S(1)} all-gather(bf16[192,576]{1,0:T(8,128)(2,1)S(1)} %pad_maximum_fusion.4), channel_id=1, replica_groups=mesh['dp'=2,'row'=4,'col'=4] {'row'}, dimensions={0}, use_global_device_ids=true | all-gather | bytes 1105920 | tf_op jit(solution)/shard_map/all_gather | solution.py:320
  63.8 17.0 %all-gather.5 = f32[4,4,192]{2,1,0:T(4,128)S(1)} all-gather(f32[1,4,192]{2,1,0:T(4,128)S(1)} %maximum_bitcast_fusion), channel_id=4, replica_groups=mesh['dp'=2,'row'=4,'col'=4] {'row'}, dimensions={0}, use_global_device_ids=true | all-gather | bytes 15360 | tf_op jit(solution)/shard_map/all_gather | solution.py:322
  85.0 13.2 %fusion.10.km_ref = bf16[8256,128]{1,0:T(8,128)(2,1)S(1)} fusion(bf16[4096,64]{1,0:T(8,128)(2,1)S(1)} %fusion.12, bf16[4096,64]{1,0:T(8,128)(2,1)S(1)} %fusion.13, bf16[8256]{0:T(1024)(128)(2,1)S(1)} %pad.35.clone), kind=kLoop, calls=%fused_computation.19 | loop fusion | flops 10567680 | bytes 3178624 | tf_op jit(solution)/shard_map/concatenate | solution.py:345
  106.9 6.6 copy.182
  116.7 17.1 %all-gather.17.cloned.1.call-done = bf16[3072,768]{1,0:T(8,128)(2,1)} async-done(((bf16[192,768]{1,0:T(8,128)(2,1)}), bf16[3072,768]{1,0:T(8,128)(2,1)}) %all-gather.17.cloned.1.call-update) | async-done | bytes 4718608 | tf_op jit(solution)/shard_map/all_gather | solution.py:370
  133.8 6.0 copy.183
  142.9 53.1 %all-gather.11.cloned.1.call-done = bf16[3072,1024]{1,0:T(8,128)(2,1)} async-done(((bf16[192,1024]{1,0:T(8,128)(2,1)}), bf16[3072,1024]{1,0:T(8,128)(2,1)}) %all-gather.11.cloned.1.call-update) | async-done | bytes 6291472 | tf_op jit(solution)/shard_map/all_gather | solution.py:321
  196.0 11.4 %reshape_reshape.3 = bf16[4,4,192,4,256]{4,3,2,1,0:T(4,128)(2,1)} reshape(bf16[3072,1024]{1,0:T(8,128)(2,1)} %all-gather.11.cloned.1.call-done) | data formatting | bytes 12582912 | tf_op jit(solution)/shard_map/reshape;reshape | solution.py:332
  207.5 6.5 constant_dynamic-slice_fusion.1
  215.9 10.8 %copy.174 = bf16[4,4,192,1024]{3,1,2,0:T(4,128)(2,1)} copy(bf16[4,4,192,1024]{3,2,1,0:T(8,128)(2,1)} %bitcast.181) | data formatting | bytes 12582912 | tf_op jit(solution)/shard_map/reshape | solution.py:321
  226.7 7.3 %copy.214 = bf16[96,8,4,1024]{3,1,2,0:T(8,128)(2,1)S(1)} copy(bf16[96,8,4,1024]{3,2,1,0:T(4,128)(2,1)} %bitcast.182) | data formatting | bytes 12582912
  235.2 4.9 fusion.kv_ref
  240.1 31.1 %attn_fwd.1 = (bf16[1024,384]{1,0:T(8,128)(2,1)S(1)}, f32[1024,384]{1,0:T(8,128)S(1)}) custom-call(s32[1]{0:T(128)} %bitcast.row_ref, s32[576]{0:T(1024)S(1)} %reshape.270.rand_ref, bf16[1024,384]{1,0:T(8,128)(2,1)S(1)} %fusion.14.q_ref, bf16[1024,128]{1,0:T(8,128)(2,1)S(1)} %bitcast.179, bf16[4096,384]{1,0:T(8,128)(2,1)} %fusion.kv_ref, ...), custom_call_target="tpu_custom_call" | custom-call | flops 1207959552 | bytes 12582912 | tf_op jit(solution)/shard_map/attn_fwd/pallas_call | solution.py:243
  288.1 3.9 fusion.44
  304.5 10.5 %all_to_all.102 = bf16[256,4,192]{0,2,1:T(8,128)(2,1)S(1)} all-to-all(bf16[256,4,192]{0,2,1:T(8,128)(2,1)S(1)} %bitcast.222), channel_id=1, replica_groups=mesh['dp'=2,'row'=4,'col'=4] {'col'}, dimensions={1} | all-to-all | bytes 786432 | tf_op jit(solution)/shard_map/all_to_all | solution.py:396
  317.5 40.5 %attn_bwd.1 = (bf16[1024,384]{1,0:T(8,128)(2,1)S(1)}, bf16[4096,384]{1,0:T(8,128)(2,1)}) custom-call(s32[1]{0:T(128)} %bitcast.row_ref, s32[576]{0:T(1024)S(1)} %reshape.270.rand_ref, bf16[1024,384]{1,0:T(8,128)(2,1)S(1)} %copy-done.2, bf16[1024,128]{1,0:T(8,128)(2,1)S(1)} %bitcast.180, bf16[4096,384]{1,0:T(8,128)(2,1)} %fusion.kv_ref, ...), custom_call_target="tpu_custom_call" | custom-call | flops 2415919104 | bytes 20971520 | tf_op jit(solution)/shard_map/attn_bwd/pallas_call | solution.py:262
  359.1 58.3 %reduce-scatter.4.cloned.1.call-done = bf16[1024,384]{1,0:T(8,128)(2,1)} async-done(((bf16[4096,384]{1,0:T(8,128)(2,1)}), bf16[1024,384]{1,0:T(8,128)(2,1)}) %reduce-scatter.4.cloned.1.call-update) | async-done | bytes 786448 | tf_op jit(solution)/shard_map/reduce_scatter | solution.py:400
  424.9 3.9 reshape.301
  434.9 9.8 %reshape.299 = bf16[4,192,4,768]{3,2,1,0:T(4,128)(2,1)} reshape(bf16[768,3072]{1,0:T(8,128)(2,1)} %convolution_convert_fusion.1) | data formatting | bytes 9437184 | tf_op jit(solution)/shard_map/reshape | solution.py:403
  444.7 5.5 copy.200
  450.2 3.8 convolution_convert_fusion.2
  453.9 9.7 %reshape.297 = bf16[4,192,4,768]{3,2,1,0:T(4,128)(2,1)} reshape(bf16[768,3072]{1,0:T(8,128)(2,1)} %convolution_convert_fusion.2) | data formatting | bytes 9437184 | tf_op jit(solution)/shard_map/reshape | solution.py:403
  467.9 4.9 pad_maximum_fusion
  476.8 4.4 all-to-all-start.4
  484.9 5.0 copy.186
  489.9 8.2 %reshape.289 = bf16[768,2304]{1,0:T(8,128)(2,1)} reshape(bf16[4,192,4,576]{3,2,1,0:T(4,128)(2,1)} %copy.186) | data formatting | bytes 7077888 | tf_op jit(solution)/shard_map/reshape | solution.py:367
  504.0 4.9 convolution_add_fusion
  510.1 15.8 %all-to-all-done.1 = bf16[4,192,256]{2,1,0:T(8,128)(2,1)S(1)} async-done(((bf16[4,192,256]{2,1,0:T(8,128)(2,1)}), bf16[4,192,256]{2,1,0:T(8,128)(2,1)S(1)}, u32[]{:S(2)}, u32[]{:S(2)}) %all-to-all-start.1) | async-done | bytes 393248 | tf_op jit(solution)/shard_map/all_to_all | solution.py:380
  526.0 4.4 all-to-all-start.5
  530.4 93.3 %reduce-scatter.8.cloned.1.call-done = bf16[1,192,1728]{2,1,0:T(8,128)(2,1)} async-done(((bf16[16,192,1728]{2,1,0:T(8,128)(2,1)}), bf16[1,192,1728]{2,1,0:T(8,128)(2,1)}) %reduce-scatter.8.cloned.1.call-update) | async-done | bytes 663568 | tf_op jit(solution)/shard_map/reduce_scatter | solution.py:406
  624.1 40.7 %psum.23 = f32[4,768]{1,0:T(4,128)S(1)} all-reduce(f32[4,768]{1,0:T(4,128)S(1)} %pad_maximum_fusion.5), channel_id=1, replica_groups=mesh['dp'=2,'row'=4,'col'=4] {'dp','row','col'}, use_global_device_ids=true, to_apply=%region_17.18 | all-reduce | flops 3072 | bytes 24576 | tf_op jit(solution)/shard_map/psum | solution.py:421
  (253 shorter events, 107.3 us)
Async XLA Ops:
  7.2 99.7 %all-gather.15.cloned.1.call-start = ((), (), s32[]{:S(2)}) async-start(), calls=%async_computation.14 | async-start | bytes 5013504 | tf_op jit(solution)/shard_map/all_gather | solution.py:368
  7.9 125.9 %all-gather.17.cloned.1.call-start = ((), (), s32[]{:S(2)}) async-start(), calls=%async_computation.15 | async-start | bytes 5013504 | tf_op jit(solution)/shard_map/all_gather | solution.py:370
  8.7 187.4 %all-gather.11.cloned.1.call-start = ((), (), s32[]{:S(2)}) async-start(), calls=%async_computation.12 | async-start | bytes 6684672 | tf_op jit(solution)/shard_map/all_gather | solution.py:321
  9.4 267.9 %all-gather.13.cloned.1.call-start = ((), (), s32[]{:S(2)}) async-start(), calls=%async_computation.13 | async-start | bytes 5013504 | tf_op jit(solution)/shard_map/all_gather | solution.py:364
  15.3 48.5 %copy-start.46 = (f32[192]{0:T(256)S(1)}, f32[192]{0:T(256)}, u32[]{:S(2)}) copy-start(f32[192]{0:T(256)} %param.25) | copy-start | bytes 2308
  15.3 48.5 %copy-start.47 = (f32[192]{0:T(256)S(1)}, f32[192]{0:T(256)}, u32[]{:S(2)}) copy-start(f32[192]{0:T(256)} %param.24) | copy-start | bytes 2308
  15.3 48.5 %copy-start.48 = (f32[192]{0:T(256)S(1)}, f32[192]{0:T(256)}, u32[]{:S(2)}) copy-start(f32[192]{0:T(256)} %param.23) | copy-start | bytes 2308
  15.3 48.5 %copy-start.49 = (f32[192]{0:T(256)S(1)}, f32[192]{0:T(256)}, u32[]{:S(2)}) copy-start(f32[192]{0:T(256)} %param.22) | copy-start | bytes 2308
  15.3 65.6 %copy-start.38 = (s32[4096]{0:T(1024)S(1)}, s32[4096]{0:T(1024)}, u32[]{:S(2)}) copy-start(s32[4096]{0:T(1024)} %param.27) | copy-start | bytes 49156
  17.0 86.6 %all-to-all-start.2 = ((bf16[192,4,256]{2,0,1:T(8,128)(2,1)}), bf16[192,4,256]{2,0,1:T(8,128)(2,1)S(1)}, u32[]{:S(2)}, u32[]{:S(2)}) async-start(bf16[192,4,256]{2,0,1:T(8,128)(2,1)} %bitcast.178), calls=%async_computation.2 | async-start | bytes 786432 | tf_op jit(solution)/shard_map/all_to_all | solution.py:325
  23.5 60.1 %copy-start.33 = (s32[4096]{0:T(1024)S(1)}, s32[4096]{0:T(1024)}, u32[]{:S(2)}) copy-start(s32[4096]{0:T(1024)} %param.26) | copy-start | bytes 49156
  81.7 16.8 %copy-start.39 = (s32[1,3,64,3]{2,0,3,1:T(1,128)S(1)}, s32[1,3,64,3]{2,0,3,1:T(1,128)}, u32[]{:S(2)}) copy-start(s32[1,3,64,3]{2,0,3,1:T(1,128)} %param.28) | copy-start | bytes 6916
  98.2 142.0 %copy-start = (bf16[8256,128]{1,0:T(8,128)(2,1)}, bf16[8256,128]{1,0:T(8,128)(2,1)S(1)}, u32[]{:S(2)}) copy-start(bf16[8256,128]{1,0:T(8,128)(2,1)S(1)} %fusion.10.km_ref) | copy-start | bytes 6340612
  103.6 9.9 %copy-start.10 = (bf16[192,4,256]{2,0,1:T(8,128)(2,1)}, bf16[192,4,256]{2,0,1:T(8,128)(2,1)S(1)}, u32[]{:S(2)}) copy-start(bf16[192,4,256]{2,0,1:T(8,128)(2,1)S(1)} %all-to-all-done.2) | copy-start | bytes 1179652
  215.9 18.2 %copy-start.17 = (bf16[96,8,4,256]{3,1,2,0:T(8,128)(2,1)}, bf16[96,8,4,256]{3,1,2,0:T(8,128)(2,1)S(1)}, u32[]{:S(2)}) copy-start(bf16[96,8,4,256]{3,1,2,0:T(8,128)(2,1)S(1)} %copy.213) | copy-start | bytes 4718596
  273.8 10.9 %all-to-all-start = ((bf16[4,256,192]{1,2,0:T(8,128)(2,1)}), bf16[4,256,192]{1,2,0:T(8,128)(2,1)S(1)}, u32[]{:S(2)}, u32[]{:S(2)}) async-start(bf16[4,256,192]{1,2,0:T(8,128)(2,1)} %copy.177), calls=%async_computation | async-start | bytes 786432 | tf_op jit(solution)/shard_map/all_to_all | solution.py:362
  277.2 140.1 %reduce-scatter.4.cloned.1.call-start = ((), (), s32[]{:S(2)}) async-start(), calls=%async_computation.9 | async-start | bytes 3932160 | tf_op jit(solution)/shard_map/reduce_scatter | solution.py:400
  288.1 162.0 %copy-start.34 = (f32[256]{0:T(256)}, f32[256]{0:T(256)S(1)}, u32[]{:S(2)}) copy-start(f32[256]{0:T(256)S(1)} %get-tuple-element.57) | copy-start | bytes 3076
  302.8 12.5 %copy-start.42 = (f32[256]{0:T(256)}, f32[256]{0:T(256)S(1)}, u32[]{:S(2)}) copy-start(f32[256]{0:T(256)S(1)} %broadcast_multiply_fusion) | copy-start | bytes 3076
  302.8 12.6 %copy-start.43 = (f32[256]{0:T(256)}, f32[256]{0:T(256)S(1)}, u32[]{:S(2)}) copy-start(f32[256]{0:T(256)S(1)} %broadcast_multiply_fusion.1) | copy-start | bytes 3076
  304.3 11.8 %copy-start.2 = (bf16[1024,384]{1,0:T(8,128)(2,1)S(1)}, bf16[1024,384]{1,0:T(8,128)(2,1)}, u32[]{:S(2)}) copy-start(bf16[1024,384]{1,0:T(8,128)(2,1)} %copy-done.1) | copy-start | bytes 2359300
  358.0 172.4 %reduce-scatter.6.cloned.1.call-start = ((), (), s32[]{:S(2)}) async-start(), calls=%async_computation.10 | async-start | bytes 1228800 | tf_op jit(solution)/shard_map/reduce_scatter | solution.py:415
  359.1 60.7 %copy-start.18 = (bf16[96,8,4,256]{3,1,2,0:T(8,128)(2,1)S(1)}, bf16[96,8,4,256]{3,1,2,0:T(8,128)(2,1)}, u32[]{:S(2)}) copy-start(bf16[96,8,4,256]{3,1,2,0:T(8,128)(2,1)} %copy-done.17) | copy-start | bytes 4718596
  423.2 200.4 %reduce-scatter.8.cloned.1.call-start = ((), (), s32[]{:S(2)}) async-start(), calls=%async_computation.11 | async-start | bytes 11698176 | tf_op jit(solution)/shard_map/reduce_scatter | solution.py:406
  476.8 23.5 %all-to-all-start.4 = ((bf16[4,256,576]{1,2,0:T(8,128)(2,1)}), bf16[4,256,576]{1,2,0:T(8,128)(2,1)}, u32[]{:S(2)}, u32[]{:S(2)}) async-start(bf16[4,256,576]{1,2,0:T(8,128)(2,1)} %copy.194), calls=%async_computation.5 | async-start | bytes 2359296 | tf_op jit(solution)/shard_map/all_to_all | solution.py:417
  500.3 25.7 %all-to-all-start.1 = ((bf16[4,192,256]{2,1,0:T(8,128)(2,1)}), bf16[4,192,256]{2,1,0:T(8,128)(2,1)S(1)}, u32[]{:S(2)}, u32[]{:S(2)}) async-start(bf16[4,192,256]{2,1,0:T(8,128)(2,1)} %bitcast.31), calls=%async_computation.1 | async-start | bytes 786432 | tf_op jit(solution)/shard_map/all_to_all | solution.py:380
  509.0 114.7 %copy-start.11 = (bf16[192,4,256]{2,0,1:T(8,128)(2,1)S(1)}, bf16[192,4,256]{2,0,1:T(8,128)(2,1)}, u32[]{:S(2)}) copy-start(bf16[192,4,256]{2,0,1:T(8,128)(2,1)} %copy-done.10) | copy-start | bytes 1179652
  509.0 115.0 %copy-start.37 = (f32[768]{0:T(1024)S(1)}, f32[768]{0:T(1024)}, u32[]{:S(2)}) copy-start(f32[768]{0:T(1024)} %get-tuple-element.22) | copy-start | bytes 9220
  509.0 115.0 %copy-start.45 = (f32[768]{0:T(1024)S(1)}, f32[768]{0:T(1024)}, u32[]{:S(2)}) copy-start(f32[768]{0:T(1024)} %get-tuple-element.20) | copy-start | bytes 9220
  509.0 115.0 %copy-start.44 = (f32[768]{0:T(1024)S(1)}, f32[768]{0:T(1024)}, u32[]{:S(2)}) copy-start(f32[768]{0:T(1024)} %get-tuple-element.26) | copy-start | bytes 9220
  526.0 140.3 %all-to-all-start.5 = ((f32[4,192,256]{2,1,0:T(8,128)}), f32[4,192,256]{2,1,0:T(8,128)S(1)}, u32[]{:S(2)}, u32[]{:S(2)}) async-start(f32[4,192,256]{2,1,0:T(8,128)} %bitcast.46), calls=%async_computation.6 | async-start | bytes 1572864 | tf_op jit(solution)/shard_map/all_to_all | solution.py:419
  530.4 136.8 %all-reduce.6.cloned.1.call-start = ((), (), s32[]{:S(2)}) async-start(), calls=%async_computation.16 | async-start | bytes 1867776 | tf_op jit(solution)/shard_map/psum | solution.py:416
  (39 other events, 152.2 us)
Sparse Core Ops, SparseCore 0:
  10.3 69.1 all-gather.14
  81.8 51.9 all-gather.16
  136.1 59.9 all-gather.10
  198.2 51.8 all-gather.12
  358.1 59.2 reduce-scatter.3
  423.4 26.1 reduce-scatter.5
  473.0 150.6 reduce-scatter.7
  626.0 37.7 all-reduce.5

commit v2 on v1

--- a/solution.py
+++ b/solution.py
@@ -274,6 +274,183 @@
         ),
         compiler_params=pltpu.CompilerParams(vmem_limit_bytes=48 << 20),
     )(row, rand, q, q_mask, kv, k_mask, d_o, lse)
+
+
+def project_kernel(rows, span, row_ref, x_ref, wq_ref, wkv_ref, q_ref, kv_ref, own_ref):
+    feat = x_ref.shape[2]
+    start = pl.multiple_of(row_ref[0] * span, span)
+    kv = q = None
+    for part in range(rows):
+        at = slice(part * feat, (part + 1) * feat)
+        mine = x_ref[part, 0, :, pl.ds(start, span)]
+        own_ref[at, :] = mine
+        kv_part = mm_tn(x_ref[part, 0], wkv_ref[at, :])
+        q_part = mm_tn(mine, wq_ref[at, :])
+        kv = kv_part if kv is None else kv + kv_part
+        q = q_part if q is None else q + q_part
+    kv_ref[...] = kv.astype(BF)
+    q_ref[...] = (q.astype(BF) * 0.125).astype(BF)
+
+
+def project(row, x_parts, w_q, w_kv, span):
+    rows, cols, feat, local = x_parts.shape
+    model, wide = w_q.shape
+    return pl.pallas_call(
+        functools.partial(project_kernel, rows, span),
+        name="project",
+        grid=(cols,),
+        out_shape=(
+            jax.ShapeDtypeStruct((cols * span, wide), BF),
+            jax.ShapeDtypeStruct((cols * local, wide), BF),
+            jax.ShapeDtypeStruct((model, cols * span), BF),
+        ),
+        in_specs=[
+            pl.BlockSpec(memory_space=pltpu.SMEM),
+            pl.BlockSpec((rows, 1, feat, local), lambda c: (0, c, 0, 0)),
+            pl.BlockSpec((model, wide), lambda c: (0, 0)),
+            pl.BlockSpec((model, wide), lambda c: (0, 0)),
+        ],
+        out_specs=(
+            pl.BlockSpec((span, wide), lambda c: (c, 0)),
+            pl.BlockSpec((local, wide), lambda c: (c, 0)),
+            pl.BlockSpec((model, span), lambda c: (0, c)),
+        ),
+        cost_estimate=pl.CostEstimate(
+            flops=cols * local * model * wide * 3, bytes_accessed=16 << 20, transcendentals=0
+        ),
+        compiler_params=pltpu.CompilerParams(vmem_limit_bytes=48 << 20),
+    )(row, x_parts, w_q, w_kv)
+
+
+PIECES = 2
+
+
+def col_places():
+    me = lax.axis_index("col")
+    partner = me + 1 - 2 * lax.rem(me, 2)
+    cross = lax.rem(me + 2, 4)
+    diag = lax.rem(partner + 2, 4)
+    barrier = pltpu.get_barrier_semaphore()
+    for peer in (partner, cross):
+        pl.semaphore_signal(
+            barrier, inc=1, device_id={"col": peer}, device_id_type=pl.DeviceIdType.MESH
+        )
+    pl.semaphore_wait(barrier, 2)
+    return me, partner, cross, diag
+
+
+def send_to(source, target, sems, kind, piece, peer):
+    copy = pltpu.make_async_remote_copy(
+        src_ref=source,
+        dst_ref=target,
+        send_sem=sems[0].at[kind, piece],
+        recv_sem=sems[1].at[kind, piece],
+        device_id={"col": peer},
+        device_id_type=pl.DeviceIdType.MESH,
+    )
+    copy.start()
+    return copy
+
+
+def gather_kernel(x_ref, out_ref, send_sem, recv_sem):
+    me, partner, cross, _ = col_places()
+    sems = (send_sem, recv_sem)
+    size = x_ref.shape[0] // PIECES
+    cuts = [pl.ds(i * size, size) for i in range(PIECES)]
+    over = [
+        send_to(x_ref.at[cut], out_ref.at[me, cut], sems, 0, i, cross)
+        for i, cut in enumerate(cuts)
+    ]
+    near = [
+        send_to(x_ref.at[cut], out_ref.at[me, cut], sems, 1, i, partner)
+        for i, cut in enumerate(cuts)
+    ]
+    out_ref[me] = x_ref[...]
+    relay = []
+    for i, cut in enumerate(cuts):
+        over[i].wait_recv()
+        relay.append(
+            send_to(out_ref.at[cross, cut], out_ref.at[cross, cut], sems, 2, i, partner)
+        )
+    for i in range(PIECES):
+        over[i].wait_send()
+        near[i].wait()
+        relay[i].wait()
+
+
+def scatter_kernel(x_ref, out_ref, near_buf, sum_buf, over_buf, send_sem, recv_sem):
+    me, partner, cross, diag = col_places()
+    sems = (send_sem, recv_sem)
+    size = x_ref.shape[1] // PIECES
+    cuts = [pl.ds(i * size, size) for i in range(PIECES)]
+    first = [
+        send_to(x_ref.at[diag, cut], near_buf.at[1, cut], sems, 0, i, partner)
+        for i, cut in enumerate(cuts)
+    ]
+    second = [
+        send_to(x_ref.at[partner, cut], near_buf.at[0, cut], sems, 1, i, partner)
+        for i, cut in enumerate(cuts)
+    ]
+    over = []
+    for i, cut in enumerate(cuts):
+        first[i].wait_recv()
+        sum_buf[cut, :] = (
+            x_ref[cross, cut, :].astype(F32) + near_buf[1, cut, :].astype(F32)
+        ).astype(BF)
+        over.append(send_to(sum_buf.at[cut], over_buf.at[cut], sems, 2, i, cross))
+    for i, cut in enumerate(cuts):
+        second[i].wait_recv()
+        out_ref[cut, :] = x_ref[me, cut, :].astype(F32) + near_buf[0, cut, :].astype(F32)
+    for i, cut in enumerate(cuts):
+        over[i].wait_recv()
+        out_ref[cut, :] += over_buf[cut, :].astype(F32)
+    for i in range(PIECES):
+        first[i].wait_send()
+        second[i].wait_send()
+        over[i].wait_send()
+
+
+def comm_params(ident):
+    return pltpu.CompilerParams(
+        collective_id=ident, has_side_effects=True, vmem_limit_bytes=32 << 20
+    )
+
+
+def comm_sems(kinds):
+    return [pltpu.SemaphoreType.DMA((kinds, PIECES)), pltpu.SemaphoreType.DMA((kinds, PIECES))]
+
+
+def gather_col(value, ident):
+    count, wide = value.shape
+    vmem = pl.BlockSpec(memory_space=pltpu.VMEM)
+    return pl.pallas_call(
+        gather_kernel,
+        name="gather_col",
+        out_shape=jax.ShapeDtypeStruct((4, count, wide), BF),
+        in_specs=[vmem],
+        out_specs=vmem,
+        scratch_shapes=comm_sems(3),
+        compiler_params=comm_params(ident),
+    )(value)
+
+
+def scatter_col(value):
+    count, wide = value.shape[0] // 4, value.shape[1]
+    vmem = pl.BlockSpec(memory_space=pltpu.VMEM)
+    return pl.pallas_call(
+        scatter_kernel,
+        name="scatter_col",
+        out_shape=jax.ShapeDtypeStruct((count, wide), F32),
+        in_specs=[vmem],
+        out_specs=vmem,
+        scratch_shapes=[
+            pltpu.VMEM((2, count, wide), BF),
+            pltpu.VMEM((count, wide), BF),
+            pltpu.VMEM((count, wide), BF),
+        ]
+        + comm_sems(3),
+        compiler_params=comm_params(2),
+    )(value.reshape(4, count, wide))
 
 
 def norm(resid, gain, bias):
@@ -316,26 +493,32 @@
     blk_k = w_key.reshape(feat, hid)
     blk_v = w_value.reshape(feat, hid)
     blk_o = w_out.reshape(hid, feat)
-    w_qkv = jnp.concatenate([blk_q, blk_k, blk_v], axis=1)
+    params = jnp.stack([ln1_gain, ln1_bias, ln2_gain, ln2_bias], axis=1)
+    high = params.astype(BF)
+    rest = params - high.astype(F32)
+    middle = rest.astype(BF)
+    low = (rest - middle.astype(F32)).astype(BF)
+    w_qkv = jnp.concatenate([blk_q, blk_k, blk_v, high, middle, low], axis=1)
     w_own = lax.all_gather(w_qkv, "row", axis=0, tiled=True)
-    x_parts = lax.all_gather(inputs, ("row", "col"), axis=0).reshape(rows, cols, feat, local)
-    gains = lax.all_gather(
-        jnp.stack([ln1_gain, ln1_bias, ln2_gain, ln2_bias]), "row", axis=0
-    ).transpose(1, 0, 2).reshape(4, 1, model)
+    x_parts = lax.all_gather(inputs, ("row", "col"), axis=0)
+    w_rest = jnp.concatenate([w_up, w_down, blk_o.T], axis=1)
+    x_parts, w_rest, grad_out = lax.optimization_barrier((x_parts, w_rest, grad_out))
+    x_parts = x_parts.reshape(rows, cols, feat, local)
+    w_rest = lax.all_gather(w_rest, "row", axis=0, tiled=True)
+    ff = w_up.shape[1]
+    up, down, w_o = w_rest[:, :ff], w_rest[:, ff : 2 * ff], w_rest[:, 2 * ff :]
+    gains = w_own[:, 3 * hid :].astype(F32)
+    gains = (gains[:, :4] + gains[:, 4:8]) + gains[:, 8:12]
+    gains = gains.T.reshape(4, 1, model)
+    w_own = w_own[:, : 3 * hid]
     grad_rows = lax.all_to_all(grad_out, "row", 1, 0, tiled=True).T.astype(F32)
 
     w_heads = w_own.reshape(model, 3, heads, HW)
     w_kv = jnp.concatenate([w_heads[:, 1], w_heads[:, 2]], axis=2).reshape(model, heads * LANES)
     w_q = jnp.pad(w_heads[:, 0], ((0, 0), (0, 0), (0, HW))).reshape(model, heads * LANES)
-    x_all = x_parts.transpose(0, 2, 1, 3).reshape(model, length)
-    x_own = lax.dynamic_index_in_dim(
-        x_parts.reshape(rows, cols, feat, rows, span), row, axis=3, keepdims=False
-    )
-    x_res = lax.dynamic_index_in_dim(x_own, col, axis=1, keepdims=False)
-    x_res = x_res.reshape(model, span).T.astype(F32)
-    x_own = x_own.transpose(0, 2, 1, 3).reshape(model, own)
-    kv = mm_tn(x_all, w_kv).astype(BF)
-    q = (mm_tn(x_own, w_q).astype(BF) * 0.125).astype(BF)
+    row_arr = jnp.reshape(row, (1,)).astype(jnp.int32)
+    q, kv, x_own = project(row_arr, x_parts, w_q, w_kv, span)
+    x_res = lax.dynamic_slice_in_dim(x_own, col * span, span, axis=1).T.astype(F32)
 
     kinds = jnp.arange(BLOCK, dtype=jnp.int32)
     seg_hot = segment_ids[:, None] == kinds[None, :]
@@ -355,57 +538,52 @@
         q_mask.reshape(cols, rows, span, LANES), row, axis=1, keepdims=False
     ).reshape(own, LANES)
     rand = rand_blocks.reshape(-1)
-    row_arr = jnp.reshape(row, (1,)).astype(jnp.int32)
 
     o_wide, lse = attention_forward(dims, row_arr, rand, q, q_mask, kv, k_mask)
-    o_own = o_wide.reshape(own, heads, 2, HW)[:, :, 1].reshape(own, hid)
-    o = lax.all_to_all(o_own, "col", 0, 1, tiled=True)
-
-    small = lax.all_gather(jnp.concatenate([w_qkv, blk_o.T], axis=1), ("row", "col"), axis=0)
-    small = small.reshape(rows, cols, feat, 3 * hid + hid)
-    w_o = small[..., 3 * hid :].transpose(0, 2, 1, 3).reshape(model, model)
-    w_back = small[..., : 3 * hid].transpose(0, 2, 1, 3).reshape(model, 3 * model)
-    up = lax.all_gather(w_up, ("row", "col"), axis=0).reshape(rows, cols, feat, -1)
-    up = up.transpose(0, 2, 1, 3).reshape(model, -1)
-    down = lax.all_gather(w_down, ("row", "col"), axis=0).reshape(rows, cols, feat, -1)
-    down = down.transpose(0, 2, 1, 3).reshape(model, -1)
+    o = o_wide.reshape(own, heads, 2, HW)[:, :, 1].reshape(own, hid)
+    attn = scatter_col(mm_nt(o, w_o).astype(BF))
 
     gain1, bias1, gain2, bias2 = gains[0], gains[1], gains[2], gains[3]
-    hidden, normed1, rstd1 = norm(x_res + mm_nt(o, w_o), gain1, bias1)
-    hidden_low = hidden.astype(BF)
-    up_val = mm(hidden_low, up)
+    hidden, normed1, rstd1 = norm(x_res + attn, gain1, bias1)
+    hidden_all = gather_col(hidden.astype(BF), 1).reshape(own, model)
+    up_val = mm(hidden_all, up)
     act, gelu_back = jax.vjp(gelu, up_val)
     act = act.astype(BF)
-    result, normed2, rstd2 = norm(hidden + mm_nt(act, down), gain2, bias2)
+    ffn = scatter_col(mm_nt(act, down).astype(BF))
+    result, normed2, rstd2 = norm(hidden + ffn, gain2, bias2)
     output = lax.all_to_all(result.T.astype(BF), "row", 0, 1, tiled=True)
 
-    g_gain2 = jnp.sum(grad_rows * normed2, axis=0)
-    g_bias2 = jnp.sum(grad_rows, axis=0)
     grad2 = norm_grad(grad_rows, normed2, rstd2, gain2)
-    df = grad2.astype(BF)
+    df = gather_col(grad2.astype(BF), 1).reshape(own, model)
     g_down = mm_tn(df, act).astype(BF)
     du = gelu_back(mm(df, down))[0].astype(BF)
-    g_up = mm_tn(hidden_low, du).astype(BF)
-    dh = mm_nt(du, up) + grad2
-    g_gain1 = jnp.sum(dh * normed1, axis=0)
-    g_bias1 = jnp.sum(dh, axis=0)
+    g_up = mm_tn(hidden_all, du).astype(BF)
+    dh = scatter_col(mm_nt(du, up).astype(BF)) + grad2
     grad1 = norm_grad(dh, normed1, rstd1, gain1)
-    dattn = grad1.astype(BF)
+    sums = jnp.stack(
+        [
+            jnp.sum(dh * normed1, axis=0),
+            jnp.sum(dh, axis=0),
+            jnp.sum(grad_rows * normed2, axis=0),
+            jnp.sum(grad_rows, axis=0),
+        ]
+    )
+    extra = jnp.pad(sums, ((0, 28), (0, 0))).astype(BF)
+    dattn = gather_col(jnp.concatenate([grad1.astype(BF), extra], axis=0), 3)
+    sums = jnp.sum(dattn[:, span : span + 4].astype(F32), axis=0)
+    dattn = dattn[:, :span].reshape(own, model)
     g_out = mm_tn(dattn, o).astype(BF)
     d_o = mm(dattn, w_o).astype(BF)
-    d_o = lax.all_to_all(d_o, "col", 1, 0, tiled=True)
     d_o = jnp.pad(d_o.reshape(own, heads, HW), ((0, 0), (0, 0), (HW, 0))).reshape(own, -1)
+
+    g_ffn = jnp.concatenate([g_up, g_down, g_out, sums.T.astype(BF)], axis=1)
+    g_ffn = lax.psum_scatter(g_ffn, "row", scatter_dimension=0, tiled=True)
+    g_sums = g_ffn[:, 2 * ff + hid :]
+    g_ffn = lax.psum(g_ffn[:, : 2 * ff + hid], "dp").astype(F32)
+    g_sums = lax.psum(g_sums, ("dp",)).astype(F32).T
 
     dq, dkv = attention_backward(dims, row_arr, rand, q, q_mask, kv, k_mask, d_o, lse)
     dkv = lax.psum_scatter(dkv, "row", scatter_dimension=0, tiled=True)
-
-    def grid(grad):
-        return grad.reshape(rows, feat, cols, -1).transpose(0, 2, 1, 3).reshape(rows * cols, feat, -1)
-
-    g_ffn = jnp.concatenate([grid(g_up), grid(g_down), grid(g_out)], axis=2)
-    g_ffn = lax.psum_scatter(g_ffn, ("row", "col"), scatter_dimension=0, tiled=True)
-    g_ffn = lax.psum(g_ffn.reshape(feat, -1), "dp").astype(F32)
-
     dq = dq.reshape(own, heads, 2, HW)[:, :, 0].reshape(own, hid)
     dkv = dkv.reshape(own, heads, 2, HW)
     dqkv = jnp.concatenate(
@@ -414,13 +592,9 @@
     g_qkv = mm(x_own, dqkv).astype(BF)
     g_qkv = lax.psum_scatter(g_qkv, "row", scatter_dimension=0, tiled=True)
     g_qkv = lax.psum(g_qkv, "dp").astype(F32)
-    dqkv = lax.all_to_all(dqkv, "col", 0, 1, tiled=True)
-    grad_in = mm_nt(dqkv, w_back) + grad1
-    grad_in = lax.all_to_all(grad_in.T, "row", 0, 1, tiled=True)
-
-    sums = lax.psum(jnp.stack([g_gain1, g_bias1, g_gain2, g_bias2]), ("dp", "row", "col"))
-    sums = lax.dynamic_slice_in_dim(sums, row * feat, feat, axis=1)
-    ff = w_up.shape[1]
+    grad_in = scatter_col(mm_nt(dqkv, w_own).astype(BF)) + grad1
+    grad_in = lax.all_to_all(grad_in.T.astype(BF), "row", 0, 1, tiled=True).astype(F32)
+
     return (
         output,
         grad_in,
@@ -430,10 +604,10 @@
         g_ffn[:, 2 * ff :].T.reshape(1, 1, -1),
         g_ffn[:, :ff],
         g_ffn[:, ff : 2 * ff],
-        sums[0],
-        sums[1],
-        sums[2],
-        sums[3],
+        g_sums[0],
+        g_sums[1],
+        g_sums[2],
+        g_sums[3],
     )
 
 

time: 690 us -> 527 us (0.76)
  Pallas kernels: 71.5 us -> 170 us
  local copies, waits for them, and re-layouts: 145 us -> 51 us
  blocking collectives: 108 us -> 39.9 us
  waiting for transfers between devices: 240 us -> 172 us
  matrix products: 39.5 us -> 22.9 us
  starting transfers between devices: 22.7 us -> 11.8 us
    pallas_call x0 -> x8, Pallas kernels: none -> 98.2 us  [the longest x4 51.9 us: scatter_col(): pl.pallas_call(scatter_kernel, name='scatter_col', out_shape=jax.ShapeDty...]
    reduce_scatter x1 -> x0, waiting for transfers between devices: 93.3 us -> none  [on_device(): lax.psum_scatter(g_ffn, ('row', 'col'), scatter_dimension=0, tiled=True)]
    reshape x9 -> x2, local copies, waits for them, and re-layouts: 56.8 us -> 0.61 us  [the longest x1 0.3 us: on_device(): jnp.pad(w_heads[:, 0], ((0, 0), (0, 0), (0, HW)))]
    unnamed x8 -> x7, waiting for transfers between devices: 2.14 us -> 54.7 us
    all_gather x4 -> x2, waiting for transfers between devices: 70.2 us -> 27.7 us  [the longest x1 27.7 us: on_device(): x_parts = lax.all_gather(inputs, ('row', 'col'), axis=0)]
    psum x1, blocking collectives: 40.7 us -> 5.14 us  [on_device(): g_sums = lax.psum(g_sums, ('dp',)).astype(F32).T]
    psum x1, waiting for transfers between devices: 0.01 us -> 26 us  [on_device(): g_qkv = lax.psum(g_qkv, 'dp').astype(F32)]
    transpose x8 -> x1, local copies, waits for them, and re-layouts: 22.7 us -> 0.11 us  [on_device(): w_rest = jnp.concatenate([w_up, w_down, blk_o.T], axis=1)]
  transfers between devices with their start and end apart: 13 -> 9, of which waited for: 5 -> 6; matrix products, arithmetic and copies ran while one was open for 27% -> 13% of each run, Pallas kernels for 5% -> 10%
where the time goes in v2:
time: 527 us; the launch traced here: 519 us
  waiting for transfers between devices  172 us (33%)
  Pallas kernels  170 us (32%)
  local copies, waits for them, and re-layouts  51 us (10%)
  blocking collectives  39.9 us (8%)
  other arithmetic  36.3 us (7%)
  matrix products  22.9 us (4%)
  between operations  15.4 us (3%)
  starting transfers between devices  11.8 us (2%)
    unnamed x7, waiting for transfers between devices  54.7 us
    pallas_call x4, Pallas kernels, scatter_col(): pl.pallas_call(scatter_kernel, name='scatter_col', out_shape=jax.ShapeDty...  51.9 us
    reduce_scatter x1, waiting for transfers between devices, on_device(): dkv = lax.psum_scatter(dkv, 'row', scatter_dimension=0, tiled=True)  48.2 us
    pallas_call x1, Pallas kernels, attention_backward(): pl.pallas_call(functools.partial(backward_kernel, *dims), name='attn_bwd'...  40.4 us
    pallas_call x3, Pallas kernels, gather_col(): pl.pallas_call(gather_kernel, name='gather_col', out_shape=jax.ShapeDtype...  37.5 us
    all_gather x1, blocking collectives, on_device(): w_own = lax.all_gather(w_qkv, 'row', axis=0, tiled=True)  34.8 us
    pallas_call x1, Pallas kernels, attention_forward(): pl.pallas_call(functools.partial(forward_kernel, *dims), name='attn_fwd',...  30.9 us
    all_gather x1, waiting for transfers between devices, on_device(): x_parts = lax.all_gather(inputs, ('row', 'col'), axis=0)  27.7 us
  transfers between devices with their start and end apart: 9, of which 6 were waited for; matrix products, arithmetic and copies ran while one was open for 13% of the time, Pallas kernels for 10%

profile of v2, /device:TPU:0, one launch (start us, length us, event | category | flops | bytes accessed | tf_op | source)
XLA Modules:
  0.0 519.3 jit_solution(11508204014117396972)
XLA Ops:
  16.7 34.8 %all_gather.14 = bf16[768,588]{1,0:T(8,128)(2,1)S(1)} all-gather(bf16[192,588]{1,0:T(8,128)(2,1)S(1)} %concatenate.35), channel_id=1, replica_groups=mesh['dp'=2,'row'=4,'col'=4] {'row'}, dimensions={0}, use_global_device_ids=true | all-gather | bytes 1128960 | tf_op jit(solution)/shard_map/all_gather | solution.py:502
  56.4 2.7 fusion.12
  59.1 27.7 %all-gather.6.cloned.1.call-done = bf16[3072,1024]{1,0:T(8,128)(2,1)} async-done(((bf16[192,1024]{1,0:T(8,128)(2,1)}), bf16[3072,1024]{1,0:T(8,128)(2,1)}) %all-gather.6.cloned.1.call-update) | async-done | bytes 6291472 | tf_op jit(solution)/shard_map/all_gather | solution.py:503
  90.1 13.0 %fusion.9.km_ref = bf16[8256,128]{1,0:T(8,128)(2,1)S(1)} fusion(bf16[4096,64]{1,0:T(8,128)(2,1)S(1)} %fusion.11, bf16[4096,64]{1,0:T(8,128)(2,1)} %fusion.12, bf16[8256]{0:T(1024)(128)(2,1)S(1)} %pad.33.clone), kind=kLoop, calls=%fused_computation.14 | loop fusion | flops 10567680 | bytes 3178624 | tf_op jit(solution)/shard_map/concatenate | solution.py:528
  104.0 4.1 all-to-all-start.1
  108.3 3.0 slice_reduce_fusion.1
  111.3 8.8 %project.1 = (bf16[1024,384]{1,0:T(8,128)(2,1)S(1)}, bf16[4096,384]{1,0:T(8,128)(2,1)}, bf16[768,1024]{1,0:T(8,128)(2,1)S(1)}) custom-call(s32[1]{0:T(128)} %bitcast.row_ref, bf16[4,4,192,1024]{3,2,1,0:T(8,128)(2,1)} %bitcast.146, bf16[768,384]{1,0:T(8,128)(2,1)S(1)} %copy.101.wq_ref, bf16[768,384]{1,0:T(8,128)(2,1)S(1)} %copy.102.wkv_ref), custom_call_target="tpu_custom_call" | custom-call | flops 3623878656 | bytes 16777216 | tf_op jit(solution)/shard_map/project/pallas_call | solution.py:298
  122.2 2.6 copy.103
  125.9 30.9 %attn_fwd.1 = (bf16[1024,384]{1,0:T(8,128)(2,1)S(1)}, f32[1024,384]{1,0:T(8,128)S(1)}) custom-call(s32[1]{0:T(128)} %bitcast.row_ref, s32[576]{0:T(1024)S(1)} %copy-done.13, bf16[1024,384]{1,0:T(8,128)(2,1)S(1)} %copy-done.11, bf16[1024,128]{1,0:T(8,128)(2,1)S(1)} %bitcast.106, bf16[4096,384]{1,0:T(8,128)(2,1)} %get-tuple-element.25.kv_ref, ...), custom_call_target="tpu_custom_call" | custom-call | flops 1207959552 | bytes 12582912 | tf_op jit(solution)/shard_map/attn_fwd/pallas_call | solution.py:243
  162.8 13.0 %scatter_col.4 = f32[256,768]{1,0:T(8,128)S(1)} custom-call(bf16[4,256,768]{2,1,0:T(8,128)(2,1)S(1)} %bitcast.98), custom_call_target="tpu_custom_call" | custom-call | tf_op jit(solution)/shard_map/scatter_col/pallas_call | solution.py:440
  177.4 12.2 %gather_col.3 = bf16[4,256,768]{2,1,0:T(8,128)(2,1)S(1)} custom-call(bf16[256,768]{1,0:T(8,128)(2,1)S(1)} %fusion.23.x_ref), custom_call_target="tpu_custom_call" | custom-call | tf_op jit(solution)/shard_map/gather_col/pallas_call | solution.py:426
  193.1 13.0 %scatter_col.5 = f32[256,768]{1,0:T(8,128)S(1)} custom-call(bf16[4,256,768]{2,1,0:T(8,128)(2,1)S(1)} %bitcast.100), custom_call_target="tpu_custom_call" | custom-call | tf_op jit(solution)/shard_map/scatter_col/pallas_call | solution.py:440
  208.0 12.0 %gather_col.4 = bf16[4,256,768]{2,1,0:T(8,128)(2,1)S(1)} custom-call(bf16[256,768]{1,0:T(8,128)(2,1)S(1)} %get-tuple-element.112.x_ref), custom_call_target="tpu_custom_call" | custom-call | tf_op jit(solution)/shard_map/gather_col/pallas_call | solution.py:426
  221.2 3.7 fusion.7
  226.4 13.0 %scatter_col.6 = f32[256,768]{1,0:T(8,128)S(1)} custom-call(bf16[4,256,768]{2,1,0:T(8,128)(2,1)S(1)} %bitcast.101), custom_call_target="tpu_custom_call" | custom-call | tf_op jit(solution)/shard_map/scatter_col/pallas_call | solution.py:440
  241.1 13.2 %gather_col.5 = bf16[4,288,768]{2,1,0:T(8,128)(2,1)S(1)} custom-call(bf16[288,768]{1,0:T(8,128)(2,1)S(1)} %pad_maximum_fusion.6.x_ref), custom_call_target="tpu_custom_call" | custom-call | tf_op jit(solution)/shard_map/gather_col/pallas_call | solution.py:426
  255.5 2.1 convolution_convert_fusion.7
  258.6 2.3 copy.113.do_ref
  265.5 40.4 %attn_bwd.1 = (bf16[1024,384]{1,0:T(8,128)(2,1)S(1)}, bf16[4096,384]{1,0:T(8,128)(2,1)}) custom-call(s32[1]{0:T(128)} %bitcast.row_ref, s32[576]{0:T(1024)S(1)} %copy-done.13, bf16[1024,384]{1,0:T(8,128)(2,1)S(1)} %copy-done.12, bf16[1024,128]{1,0:T(8,128)(2,1)S(1)} %bitcast.107, bf16[4096,384]{1,0:T(8,128)(2,1)} %get-tuple-element.25.kv_ref, ...), custom_call_target="tpu_custom_call" | custom-call | flops 2415919104 | bytes 20971520 | tf_op jit(solution)/shard_map/attn_bwd/pallas_call | solution.py:262
  309.0 3.0 convolution_convert_fusion.5
  314.1 4.3 copy.120
  319.9 48.2 %reduce-scatter.6.cloned.1.call-done = bf16[1024,384]{1,0:T(8,128)(2,1)} async-done(((bf16[4096,384]{1,0:T(8,128)(2,1)}), bf16[1024,384]{1,0:T(8,128)(2,1)}) %reduce-scatter.6.cloned.1.call-update) | async-done | bytes 786448 | tf_op jit(solution)/shard_map/reduce_scatter | solution.py:586
  369.5 2.4 convolution_convert_fusion.6
  372.9 3.6 all-to-all-start
  376.7 53.9 %reduce-scatter.10.cloned.1.call-done = bf16[192,1732]{1,0:T(8,128)(2,1)} async-done(((bf16[768,1732]{1,0:T(8,128)(2,1)}), bf16[192,1732]{1,0:T(8,128)(2,1)}) %reduce-scatter.10.cloned.1.call-update) | async-done | bytes 665104
  430.7 2.3 copy.123
  434.4 13.0 %scatter_col.7 = f32[256,768]{1,0:T(8,128)S(1)} custom-call(bf16[4,256,768]{2,1,0:T(8,128)(2,1)S(1)} %bitcast.99), custom_call_target="tpu_custom_call" | custom-call | tf_op jit(solution)/shard_map/scatter_col/pallas_call | solution.py:440
  447.4 12.1 %reduce-scatter.8.cloned.1.call-done = bf16[192,576]{1,0:T(8,128)(2,1)} async-done(((bf16[768,576]{1,0:T(8,128)(2,1)}), bf16[192,576]{1,0:T(8,128)(2,1)}) %reduce-scatter.8.cloned.1.call-update) | async-done | bytes 221200 | tf_op jit(solution)/shard_map/reduce_scatter | solution.py:593
  460.6 3.5 all-to-all-start.2
  465.8 5.1 psum.23
  471.5 3.8 all-to-all-done.2
  476.3 26.0 %all-reduce.7.cloned.1.call-done = (bf16[192,576]{1,0:T(8,128)(2,1)}, bf16[192,1728]{0,1:T(8,128)(2,1)}) async-done(((bf16[192,576]{1,0:T(8,128)(2,1)}, bf16[192,1728]{0,1:T(8,128)(2,1)}), (bf16[192,576]{1,0:T(8,128)(2,1)}, bf16[192,1728]{0,1:T(8,128)(2,1)})) %all-reduce.7.cloned.1.call-update) | async-done | bytes 884752 | tf_op jit(solution)/shard_map/psum | solution.py:594
  (186 shorter events, 70.3 us)
Async XLA Ops:
  7.2 79.6 %all-gather.6.cloned.1.call-start = ((), (), s32[]{:S(2)}) async-start(), calls=%async_computation.9 | async-start | bytes 6684672 | tf_op jit(solution)/shard_map/all_gather | solution.py:503
  7.9 153.2 %all-gather.4.cloned.1.call-start = ((), (), s32[]{:S(2)}) async-start(), calls=%async_computation.6 | async-start | bytes 3440640 | tf_op jit(solution)/shard_map/all_gather | solution.py:507
  52.1 1.9 copy-start.24
  52.1 1.9 copy-start.25
  55.0 32.1 %copy-start.34 = (s32[1,3,64,3]{2,0,3,1:T(1,128)S(1)}, s32[1,3,64,3]{2,0,3,1:T(1,128)}, u32[]{:S(2)}) copy-start(s32[1,3,64,3]{2,0,3,1:T(1,128)} %param.28) | copy-start | bytes 6916
  86.8 1.9 copy-start.28
  86.8 1.9 copy-start.32
  87.0 37.7 %copy-start.5 = (bf16[4,1,256,128]{3,2,0,1:T(8,128)(2,1)}, bf16[4,1,256,128]{3,2,0,1:T(8,128)(2,1)S(1)}, u32[]{:S(2)}) copy-start(bf16[4,1,256,128]{3,2,0,1:T(8,128)(2,1)S(1)} %fusion.26) | copy-start | bytes 786436
  90.1 13.1 %copy-start.23 = (bf16[192,1024]{1,0:T(8,128)(2,1)S(1)}, bf16[192,1024]{1,0:T(8,128)(2,1)}, u32[]{:S(2)}) copy-start(bf16[192,1024]{1,0:T(8,128)(2,1)} %param.29) | copy-start | bytes 1179652
  103.1 21.6 %copy-start = (bf16[8256,128]{1,0:T(8,128)(2,1)}, bf16[8256,128]{1,0:T(8,128)(2,1)S(1)}, u32[]{:S(2)}) copy-start(bf16[8256,128]{1,0:T(8,128)(2,1)S(1)} %fusion.9.km_ref) | copy-start | bytes 6340612
  104.0 54.3 %all-to-all-start.1 = ((bf16[192,4,256]{2,0,1:T(8,128)(2,1)}), bf16[192,4,256]{2,0,1:T(8,128)(2,1)}, u32[]{:S(2)}, u32[]{:S(2)}) async-start(bf16[192,4,256]{2,0,1:T(8,128)(2,1)} %bitcast.119), calls=%async_computation.1 | async-start | bytes 786432 | tf_op jit(solution)/shard_map/all_to_all | solution.py:514
  108.1 259.9 %reduce-scatter.6.cloned.1.call-start = ((), (), s32[]{:S(2)}) async-start(), calls=%async_computation.7 | async-start | bytes 3932160 | tf_op jit(solution)/shard_map/reduce_scatter | solution.py:586
  122.2 2.6 copy-start.13
  158.3 4.5 copy-start.19
  162.8 14.4 %copy-start.27 = (f32[768]{0:T(1024)S(1)}, f32[768]{0:T(1024)}, u32[]{:S(2)}) copy-start(f32[768]{0:T(1024)} %get-tuple-element.106) | copy-start | bytes 9220
  162.8 14.4 %copy-start.30 = (f32[768]{0:T(1024)S(1)}, f32[768]{0:T(1024)}, u32[]{:S(2)}) copy-start(f32[768]{0:T(1024)} %get-tuple-element.105) | copy-start | bytes 9220
  175.8 13.9 %copy-start.26 = (bf16[768,1728]{1,0:T(8,128)(2,1)S(1)}, bf16[768,1728]{1,0:T(8,128)(2,1)}, u32[]{:S(2)}) copy-start(bf16[768,1728]{1,0:T(8,128)(2,1)} %all-gather.4.cloned.1.call-done) | copy-start | bytes 7962628
  191.1 29.0 %copy-start.35 = (f32[1024,768]{1,0:T(8,128)}, f32[1024,768]{1,0:T(8,128)S(1)}, u32[]{:S(2)}) copy-start(f32[1024,768]{1,0:T(8,128)S(1)} %fusion.19) | copy-start | bytes 9437188
  193.1 13.4 %copy-start.29 = (f32[768]{0:T(1024)S(1)}, f32[768]{0:T(1024)}, u32[]{:S(2)}) copy-start(f32[768]{0:T(1024)} %get-tuple-element.103) | copy-start | bytes 9220
  224.9 1.5 copy-start.37
  306.8 123.8 %reduce-scatter.10.cloned.1.call-start = ((), (), s32[]{:S(2)}) async-start(), calls=%async_computation.10 | async-start | bytes 3440640
  308.9 3.0 copy-start.4
  308.9 3.0 copy-start.36
  318.4 141.1 %reduce-scatter.8.cloned.1.call-start = ((), (), s32[]{:S(2)}) async-start(), calls=%async_computation.8 | async-start | bytes 1228800 | tf_op jit(solution)/shard_map/reduce_scatter | solution.py:593
  319.8 49.7 %copy-start.2 = (bf16[768,1024]{1,0:T(8,128)(2,1)S(1)}, bf16[768,1024]{1,0:T(8,128)(2,1)}, u32[]{:S(2)}) copy-start(bf16[768,1024]{1,0:T(8,128)(2,1)} %copy-done.1) | copy-start | bytes 4718596
  369.5 2.4 copy-start.21
  371.9 61.1 %copy-start.18 = (bf16[768,588]{1,0:T(8,128)(2,1)S(1)}, bf16[768,588]{1,0:T(8,128)(2,1)}, u32[]{:S(2)}) copy-start(bf16[768,588]{1,0:T(8,128)(2,1)} %copy-done.17) | copy-start | bytes 2709508
  372.9 87.7 %all-to-all-start = ((bf16[4,192,256]{2,1,0:T(8,128)(2,1)}), bf16[4,192,256]{2,1,0:T(8,128)(2,1)S(1)}, u32[]{:S(2)}, u32[]{:S(2)}) async-start(bf16[4,192,256]{2,1,0:T(8,128)(2,1)} %bitcast.23), calls=%async_computation | async-start | bytes 786432 | tf_op jit(solution)/shard_map/all_to_all | solution.py:554
  376.5 125.8 %all-reduce.7.cloned.1.call-start = ((), (), s32[]{:S(2)}) async-start(), calls=%async_computation.11 | async-start | bytes 2260992 | tf_op jit(solution)/shard_map/psum | solution.py:594
  434.4 25.1 %copy-start.20 = (f32[256,768]{1,0:T(8,128)S(1)}, f32[256,768]{1,0:T(8,128)}, u32[]{:S(2)}) copy-start(f32[256,768]{1,0:T(8,128)} %get-tuple-element.110) | copy-start | bytes 2359300
  460.6 14.7 %all-to-all-start.2 = ((bf16[4,192,256]{2,1,0:T(8,128)(2,1)}), bf16[4,192,256]{2,1,0:T(8,128)(2,1)S(1)}, u32[]{:S(2)}, u32[]{:S(2)}) async-start(bf16[4,192,256]{2,1,0:T(8,128)(2,1)} %bitcast.40), calls=%async_computation.3 | async-start | bytes 786432 | tf_op jit(solution)/shard_map/all_to_all | solution.py:596
  502.3 1.5 copy-start.22
  (15 other events, 16.5 us)
Sparse Core Ops, SparseCore 0:
  10.3 76.4 all-gather.5
  88.3 63.9 all-gather.3
  307.0 61.0 reduce-scatter.5
  370.2 60.4 reduce-scatter.9
  432.8 26.6 reduce-scatter.7
  461.7 40.5 all-reduce.6

commit v3 on v2

--- a/solution.py
+++ b/solution.py
@@ -6,6 +6,7 @@
 from jax.experimental import pallas as pl
 from jax.experimental.pallas import tpu as pltpu
 from jax.sharding import PartitionSpec as P
+
 
 BLOCK = 64
 HW = 64
@@ -38,32 +39,32 @@
 
 
 def sparse_lists(rand_ref, head, pos, nb):
-    picks = [rand_ref[(head * nb + pos) * 3 + i] for i in range(3)]
     before = jnp.maximum(pos - 1, 0)
     after = jnp.minimum(pos + 1, nb - 1)
-    blocks = [0, nb - 1, before, pos, after] + picks
-    masks = [
-        0,
-        nb - 1,
-        jnp.where(pos >= 2, before, 2 * nb),
-        nb + pos,
-        jnp.where(pos <= nb - 3, after, 2 * nb),
-    ] + picks
-    return blocks, masks
-
-
-def dense_lists(group, pos, nb):
-    blocks = [group * 8 + i for i in range(8)]
-    masks = [jnp.where(b == pos, nb + b, b) for b in blocks]
-    return blocks, masks
+    picks = [rand_ref[(head * nb + pos) * 3 + i] for i in range(3)]
+    return [0, nb - 1, before, pos, after] + picks
+
+
+def dense_list(group):
+    return [group * 8 + i for i in range(8)]
+
+
+def sparse_bar(pos, nb):
+    entry = lax.broadcasted_iota(jnp.int32, (1, 8 * BLOCK), 1) // BLOCK
+    no_before = jnp.where(pos < 2, 8.0, 0.0)
+    no_after = jnp.where(pos > nb - 3, 8.0, 0.0)
+    return 0.5 + jnp.where(entry == 2, no_before, 0.0) + jnp.where(entry == 4, no_after, 0.0)
 
 
 def gather(ref, blocks, head):
     return jnp.concatenate([rows_at(ref, b, head) for b in blocks], axis=0)
 
 
-def scores_of(query, query_mask, keys, key_mask):
-    return jnp.where(mm_nt(query_mask, key_mask) > 0.5, mm_nt(query, keys), NEG)
+def scores_of(query, query_mask, keys, key_mask, own, bar):
+    shape = (query.shape[0], keys.shape[0])
+    apart = lax.broadcasted_iota(jnp.int32, shape, 1) - lax.broadcasted_iota(jnp.int32, shape, 0)
+    allowed = (mm_nt(query_mask, key_mask) > bar) | (apart == own * BLOCK)
+    return jnp.where(allowed, mm_nt(query, keys), NEG)
 
 
 def forward_kernel(heads, nb, per, rows, row_ref, rand_ref, q_ref, qm_ref, kv_ref, km_ref, o_ref, lse_ref):
@@ -82,9 +83,11 @@
         def _():
             for head in range(heads):
                 at = place(j, head)
-                blocks, masks = sparse_lists(rand_ref, head, pos, nb)
+                blocks = sparse_lists(rand_ref, head, pos, nb)
                 keys = gather(kv_ref, blocks, head)
-                score = scores_of(q_ref[at], query_mask, keys, gather(km_ref, masks, 0))
+                score = scores_of(
+                    q_ref[at], query_mask, keys, gather(km_ref, blocks, 0), 3, sparse_bar(pos, nb)
+                )
                 top = jnp.max(score, axis=1, keepdims=True)
                 weight = jnp.exp(score - top)
                 total = jnp.sum(weight, axis=1, keepdims=True)
@@ -95,10 +98,11 @@
         @pl.when(is_global)
         def _():
             def score_at(group, head):
-                blocks, masks = dense_lists(group, pos, nb)
+                blocks = dense_list(group)
                 keys = gather(kv_ref, blocks, head)
                 score = scores_of(
-                    q_ref[place(j, head)], query_mask, keys, gather(km_ref, masks, 0)
+                    q_ref[place(j, head)], query_mask, keys, gather(km_ref, blocks, 0),
+                    pos - group * 8, 0.5,
                 )
                 return score, keys
 
@@ -152,10 +156,10 @@
         start = pl.multiple_of(j * BLOCK, BLOCK)
         return pl.ds(start, BLOCK), slice(head * LANES, (head + 1) * LANES)
 
-    def parts(j, head, query_mask, blocks, masks):
+    def parts(j, head, query_mask, blocks, mine, bar):
         at = place(j, head)
         keys = gather(kv_ref, blocks, head)
-        score = scores_of(q_ref[at], query_mask, keys, gather(km_ref, masks, 0))
+        score = scores_of(q_ref[at], query_mask, keys, gather(km_ref, blocks, 0), mine, bar)
         lse = lse_ref[at][:, :1]
         probs = jnp.exp(score - lse)
         return keys, probs, mm_nt(do_ref[at], keys)
@@ -179,8 +183,10 @@
         @pl.when(jnp.logical_not(is_global))
         def _():
             for head in range(heads):
-                blocks, masks = sparse_lists(rand_ref, head, pos, nb)
-                keys, probs, grad_probs = parts(j, head, query_mask, blocks, masks)
+                blocks = sparse_lists(rand_ref, head, pos, nb)
+                keys, probs, grad_probs = parts(
+                    j, head, query_mask, blocks, 3, sparse_bar(pos, nb)
+                )
                 dot_row = jnp.sum(probs * grad_probs, axis=1, keepdims=True)
                 grad_q = finish(j, head, blocks, keys, probs, grad_probs, dot_row)
                 dq_ref[place(j, head)] = (grad_q * 0.125).astype(BF)
@@ -188,10 +194,11 @@
         @pl.when(is_global)
         def _():
             def dots(group, kept):
-                blocks, masks = dense_lists(group, pos, nb)
+                blocks = dense_list(group)
+                mine = pos - group * 8
                 new = []
                 for head in range(heads):
-                    _, probs, grad_probs = parts(j, head, query_mask, blocks, masks)
+                    _, probs, grad_probs = parts(j, head, query_mask, blocks, mine, 0.5)
                     new.append(kept[head] + jnp.sum(probs * grad_probs, axis=1, keepdims=True))
                 return tuple(new)
 
@@ -200,10 +207,11 @@
             )
 
             def grads(group, kept):
-                blocks, masks = dense_lists(group, pos, nb)
+                blocks = dense_list(group)
+                mine = pos - group * 8
                 new = []
                 for head in range(heads):
-                    keys, probs, grad_probs = parts(j, head, query_mask, blocks, masks)
+                    keys, probs, grad_probs = parts(j, head, query_mask, blocks, mine, 0.5)
                     new.append(
                         kept[head]
                         + finish(j, head, blocks, keys, probs, grad_probs, dot_rows[head])
@@ -276,7 +284,17 @@
     )(row, rand, q, q_mask, kv, k_mask, d_o, lse)
 
 
-def project_kernel(rows, span, row_ref, x_ref, wq_ref, wkv_ref, q_ref, kv_ref, own_ref):
+def one_hot_rows(hot):
+    kinds = hot.shape[0]
+    shape = (kinds, LANES)
+    eye = lax.broadcasted_iota(jnp.int32, shape, 0) == lax.broadcasted_iota(jnp.int32, shape, 1)
+    return mm_tn(jnp.where(hot, 1.0, 0.0).astype(BF), jnp.where(eye, 1.0, 0.0).astype(BF)).astype(BF)
+
+
+def project_kernel(
+    rows, span, row_ref, x_ref, wq_ref, wkv_ref, seg_ref, pad_ref,
+    q_ref, kv_ref, own_ref, qm_ref, km_ref,
+):
     feat = x_ref.shape[2]
     start = pl.multiple_of(row_ref[0] * span, span)
     kv = q = None
@@ -290,9 +308,15 @@
         q = q_part if q is None else q + q_part
     kv_ref[...] = kv.astype(BF)
     q_ref[...] = (q.astype(BF) * 0.125).astype(BF)
-
-
-def project(row, x_parts, w_q, w_kv, span):
+    segs = seg_ref[...]
+    kinds = lax.broadcasted_iota(jnp.int32, (BLOCK, segs.shape[1]), 0)
+    km_ref[...] = one_hot_rows((kinds == segs) & (pad_ref[...] == 1))
+    mine = seg_ref[:, pl.ds(start, span)]
+    kinds = lax.broadcasted_iota(jnp.int32, (BLOCK, span), 0)
+    qm_ref[...] = one_hot_rows(kinds == mine)
+
+
+def project(row, x_parts, w_q, w_kv, span, segs, pads):
     rows, cols, feat, local = x_parts.shape
     model, wide = w_q.shape
     return pl.pallas_call(
@@ -303,23 +327,29 @@
             jax.ShapeDtypeStruct((cols * span, wide), BF),
             jax.ShapeDtypeStruct((cols * local, wide), BF),
             jax.ShapeDtypeStruct((model, cols * span), BF),
+            jax.ShapeDtypeStruct((cols * span, LANES), BF),
+            jax.ShapeDtypeStruct((cols * local, LANES), BF),
         ),
         in_specs=[
             pl.BlockSpec(memory_space=pltpu.SMEM),
             pl.BlockSpec((rows, 1, feat, local), lambda c: (0, c, 0, 0)),
             pl.BlockSpec((model, wide), lambda c: (0, 0)),
             pl.BlockSpec((model, wide), lambda c: (0, 0)),
+            pl.BlockSpec((1, local), lambda c: (0, c)),
+            pl.BlockSpec((1, local), lambda c: (0, c)),
         ],
         out_specs=(
             pl.BlockSpec((span, wide), lambda c: (c, 0)),
             pl.BlockSpec((local, wide), lambda c: (c, 0)),
             pl.BlockSpec((model, span), lambda c: (0, c)),
+            pl.BlockSpec((span, LANES), lambda c: (c, 0)),
+            pl.BlockSpec((local, LANES), lambda c: (c, 0)),
         ),
         cost_estimate=pl.CostEstimate(
             flops=cols * local * model * wide * 3, bytes_accessed=16 << 20, transcendentals=0
         ),
         compiler_params=pltpu.CompilerParams(vmem_limit_bytes=48 << 20),
-    )(row, x_parts, w_q, w_kv)
+    )(row, x_parts, w_q, w_kv, segs.reshape(1, -1), pads.reshape(1, -1))
 
 
 PIECES = 2
@@ -410,6 +440,119 @@
         over[i].wait_send()
 
 
+def scatter_row_kernel(
+    rows, swap, x_ref, out_ref, from_left, from_right, to_right, to_left, own_buf, peer_buf,
+    send_sem, recv_sem, swap_sem,
+):
+    me = lax.axis_index("row")
+    right, left = lax.rem(me + 1, rows), lax.rem(me + rows - 1, rows)
+    has_left, has_right = me > 0, me < rows - 1
+    mesh_id = pl.DeviceIdType.MESH
+    barrier = pltpu.get_barrier_semaphore()
+
+    @pl.when(has_left)
+    def _():
+        pl.semaphore_signal(barrier, inc=1, device_id={"row": left}, device_id_type=mesh_id)
+
+    @pl.when(has_right)
+    def _():
+        pl.semaphore_signal(barrier, inc=1, device_id={"row": right}, device_id_type=mesh_id)
+
+    if swap:
+        peer = 1 - lax.axis_index("dp")
+        pl.semaphore_signal(barrier, inc=1, device_id={"dp": peer}, device_id_type=mesh_id)
+
+    peers = jnp.where(has_left, 1, 0) + jnp.where(has_right, 1, 0) + (1 if swap else 0)
+    pl.semaphore_wait(barrier, peers)
+
+    size = x_ref.shape[1] // PIECES
+    cuts = [pl.ds(i * size, size) for i in range(PIECES)]
+
+    def hop(way, dest, i):
+        stage, target, to = ((to_right, from_left, right), (to_left, from_right, left))[way]
+        return pltpu.make_async_remote_copy(
+            src_ref=stage.at[dest, cuts[i]],
+            dst_ref=target.at[dest, cuts[i]],
+            send_sem=send_sem.at[way, dest, i],
+            recv_sem=recv_sem.at[way, dest, i],
+            device_id={"row": to},
+            device_id_type=mesh_id,
+        )
+
+    flows = []
+    for step in range(rows - 1):
+        flows.append((0, rows - 1 - step, me < rows - 1 - step, has_left))
+        flows.append((1, step, me > step, has_right))
+    for way, dest, active, relays in flows:
+        stage, came = ((to_right, from_left), (to_left, from_right))[way]
+        for i, cut in enumerate(cuts):
+
+            @pl.when(active & relays)
+            def _():
+                hop(way, dest, i).wait_recv()
+                stage[dest, cut, :] = (
+                    x_ref[dest, cut, :].astype(F32) + came[dest, cut, :].astype(F32)
+                ).astype(BF)
+
+            @pl.when(active & jnp.logical_not(relays))
+            def _():
+                stage[dest, cut, :] = x_ref[dest, cut, :]
+
+            @pl.when(active)
+            def _():
+                hop(way, dest, i).start()
+
+    out_ref[...] = x_ref[me].astype(F32)
+    for way, came, has in ((0, from_left, has_left), (1, from_right, has_right)):
+
+        @pl.when(has)
+        def _():
+            for i, cut in enumerate(cuts):
+                hop(way, me, i).wait_recv()
+                out_ref[cut, :] += came[me, cut, :].astype(F32)
+
+    for way, dest, active, _ in flows:
+
+        @pl.when(active)
+        def _():
+            for i in range(PIECES):
+                hop(way, dest, i).wait_send()
+
+    if swap:
+        own_buf[...] = out_ref[...].astype(BF)
+        copy = pltpu.make_async_remote_copy(
+            src_ref=own_buf,
+            dst_ref=peer_buf,
+            send_sem=swap_sem.at[0],
+            recv_sem=swap_sem.at[1],
+            device_id={"dp": peer},
+            device_id_type=mesh_id,
+        )
+        copy.start()
+        copy.wait()
+        out_ref[...] = own_buf[...].astype(F32) + peer_buf[...].astype(F32)
+
+
+def scatter_row(value, rows, swap):
+    count, wide = value.shape[0] // rows, value.shape[1]
+    vmem = pl.BlockSpec(memory_space=pltpu.VMEM)
+    return pl.pallas_call(
+        functools.partial(scatter_row_kernel, rows, swap),
+        name="scatter_row",
+        out_shape=jax.ShapeDtypeStruct((count, wide), F32),
+        in_specs=[vmem],
+        out_specs=vmem,
+        scratch_shapes=[pltpu.VMEM((rows, count, wide), BF)] * 4
+        + [pltpu.VMEM((count, wide), BF)] * 2
+        + [
+            pltpu.SemaphoreType.DMA((2, rows, PIECES)),
+            pltpu.SemaphoreType.DMA((2, rows, PIECES)),
+            pltpu.SemaphoreType.DMA((2,)),
+        ],
+        compiler_params=comm_params(4),
+    )(value.reshape(rows, count, wide))
+
+
 def comm_params(ident):
     return pltpu.CompilerParams(
         collective_id=ident, has_side_effects=True, vmem_limit_bytes=32 << 20
@@ -517,28 +660,12 @@
     w_kv = jnp.concatenate([w_heads[:, 1], w_heads[:, 2]], axis=2).reshape(model, heads * LANES)
     w_q = jnp.pad(w_heads[:, 0], ((0, 0), (0, 0), (0, HW))).reshape(model, heads * LANES)
     row_arr = jnp.reshape(row, (1,)).astype(jnp.int32)
-    q, kv, x_own = project(row_arr, x_parts, w_q, w_kv, span)
+    q, kv, x_own, q_mask, k_mask = project(
+        row_arr, x_parts, w_q, w_kv, span, segment_ids, pad_mask
+    )
     x_res = lax.dynamic_slice_in_dim(x_own, col * span, span, axis=1).T.astype(F32)
 
-    kinds = jnp.arange(BLOCK, dtype=jnp.int32)
-    seg_hot = segment_ids[:, None] == kinds[None, :]
-    key_hot = (seg_hot & (pad_mask[:, None] == 1)).astype(BF)
-    place_hot = ((jnp.arange(length, dtype=jnp.int32) % BLOCK)[:, None] == kinds[None, :]).astype(BF)
-    zeros = jnp.zeros_like(key_hot)
-    k_mask = jnp.concatenate(
-        [
-            jnp.concatenate([key_hot, zeros], axis=1),
-            jnp.concatenate([key_hot, place_hot], axis=1),
-            jnp.zeros((BLOCK, LANES), BF),
-        ],
-        axis=0,
-    )
-    q_mask = jnp.concatenate([seg_hot.astype(BF), place_hot], axis=1)
-    q_mask = lax.dynamic_index_in_dim(
-        q_mask.reshape(cols, rows, span, LANES), row, axis=1, keepdims=False
-    ).reshape(own, LANES)
     rand = rand_blocks.reshape(-1)
-
     o_wide, lse = attention_forward(dims, row_arr, rand, q, q_mask, kv, k_mask)
     o = o_wide.reshape(own, heads, 2, HW)[:, :, 1].reshape(own, hid)
     attn = scatter_col(mm_nt(o, w_o).astype(BF))
@@ -558,7 +685,13 @@
     g_down = mm_tn(df, act).astype(BF)
     du = gelu_back(mm(df, down))[0].astype(BF)
     g_up = mm_tn(hidden_all, du).astype(BF)
-    dh = scatter_col(mm_nt(du, up).astype(BF)) + grad2
+    g_ffn = jnp.concatenate(
+        [g_up.reshape(rows, feat, ff), g_down.reshape(rows, feat, ff)], axis=1
+    ).reshape(2 * model, ff)
+    du, g_ffn = lax.optimization_barrier((du, g_ffn))
+    g_ffn = lax.psum_scatter(g_ffn, "row", scatter_dimension=0, tiled=True)
+    dh = scatter_col(mm_nt(du, up).astype(BF))
+    dh = dh + grad2
     grad1 = norm_grad(dh, normed1, rstd1, gain1)
     sums = jnp.stack(
         [
@@ -576,22 +709,25 @@
     d_o = mm(dattn, w_o).astype(BF)
     d_o = jnp.pad(d_o.reshape(own, heads, HW), ((0, 0), (0, 0), (HW, 0))).reshape(own, -1)
 
-    g_ffn = jnp.concatenate([g_up, g_down, g_out, sums.T.astype(BF)], axis=1)
-    g_ffn = lax.psum_scatter(g_ffn, "row", scatter_dimension=0, tiled=True)
-    g_sums = g_ffn[:, 2 * ff + hid :]
-    g_ffn = lax.psum(g_ffn[:, : 2 * ff + hid], "dp").astype(F32)
-    g_sums = lax.psum(g_sums, ("dp",)).astype(F32).T
+    g_rest = jnp.concatenate([g_out, sums.T.astype(BF)], axis=1)
 
     dq, dkv = attention_backward(dims, row_arr, rand, q, q_mask, kv, k_mask, d_o, lse)
     dkv = lax.psum_scatter(dkv, "row", scatter_dimension=0, tiled=True)
+    dkv, g_ffn, g_rest = lax.optimization_barrier((dkv, g_ffn, g_rest))
+    g_rest = lax.psum_scatter(g_rest, "row", scatter_dimension=0, tiled=True)
+    g_ffn, g_rest = lax.psum((g_ffn, g_rest), "dp")
+    g_ffn, g_rest = g_ffn.astype(F32), g_rest.astype(F32)
+    g_sums = g_rest[:, hid:].T
     dq = dq.reshape(own, heads, 2, HW)[:, :, 0].reshape(own, hid)
     dkv = dkv.reshape(own, heads, 2, HW)
     dqkv = jnp.concatenate(
         [dq, dkv[:, :, 0].reshape(own, hid), dkv[:, :, 1].reshape(own, hid)], axis=1
     )
     g_qkv = mm(x_own, dqkv).astype(BF)
-    g_qkv = lax.psum_scatter(g_qkv, "row", scatter_dimension=0, tiled=True)
-    g_qkv = lax.psum(g_qkv, "dp").astype(F32)
+    swap = lax.axis_size("dp") == 2
+    g_qkv = scatter_row(g_qkv, rows, swap)
+    if not swap:
+        g_qkv = lax.psum(g_qkv.astype(BF), "dp").astype(F32)
     grad_in = scatter_col(mm_nt(dqkv, w_own).astype(BF)) + grad1
     grad_in = lax.all_to_all(grad_in.T.astype(BF), "row", 0, 1, tiled=True).astype(F32)
 
@@ -601,9 +737,9 @@
         g_qkv[:, :hid].reshape(1, 1, -1),
         g_qkv[:, hid : 2 * hid].reshape(1, 1, -1),
         g_qkv[:, 2 * hid :].reshape(1, 1, -1),
-        g_ffn[:, 2 * ff :].T.reshape(1, 1, -1),
-        g_ffn[:, :ff],
-        g_ffn[:, ff : 2 * ff],
+        g_rest[:, :hid].T.reshape(1, 1, -1),
+        g_ffn[:feat],
+        g_ffn[feat:],
         g_sums[0],
         g_sums[1],
         g_sums[2],

time: 527 us -> 479 us (0.909); the launches traced: 519 us -> 477 us
  waiting for transfers between devices: 172 us -> 117 us
  Pallas kernels: 170 us -> 204 us
  other arithmetic: 36.3 us -> 17.1 us
  blocking collectives: 39.9 us -> 32.5 us
    unnamed x7, waiting for transfers between devices: 54.7 us -> 0.76 us
    pallas_call x0 -> x1, Pallas kernels: none -> 35.9 us  [scatter_row(): pl.pallas_call(functools.partial(scatter_row_kernel, rows, swap), name='s...]
    all_gather x1, waiting for transfers between devices: 27.7 us -> 63 us  [on_device(): x_parts = lax.all_gather(inputs, ('row', 'col'), axis=0)]
    psum x1, waiting for transfers between devices: 26 us -> 0.01 us  [on_device(): g_ffn, g_rest = lax.psum((g_ffn, g_rest), 'dp')]
    reduce_scatter x1, waiting for transfers between devices: 12.1 us -> 0.01 us  [on_device(): g_ffn = lax.psum_scatter(g_ffn, 'row', scatter_dimension=0, tiled=True)]
    concatenate x3 -> x2, other arithmetic: 13.6 us -> 2.34 us  [the longest x1 1.6 us: on_device(): jnp.concatenate([g_up.reshape(rows, feat, ff), g_down.reshape(rows, feat,...]
    reduce_scatter x1, waiting for transfers between devices: 48.2 us -> 53.5 us  [on_device(): dkv = lax.psum_scatter(dkv, 'row', scatter_dimension=0, tiled=True)]
    unnamed x82 -> x67, local copies, waits for them, and re-layouts: 21.1 us -> 17.1 us
  transfers between devices with their start and end apart: 9 -> 9, of which waited for: 6 -> 2; matrix products, arithmetic and copies ran while one was open for 13% -> 12% of each run, Pallas kernels for 10% -> 32%
where the time goes in v3:
time: 479 us; the launch traced here: 477 us
  Pallas kernels  204 us (43%)
  waiting for transfers between devices  117 us (24%)
  local copies, waits for them, and re-layouts  52.6 us (11%)
  blocking collectives  32.5 us (7%)
  matrix products  24 us (5%)
  other arithmetic  17.1 us (4%)
  starting transfers between devices  15.2 us (3%)
  between operations  14.8 us (3%)
    all_gather x1, waiting for transfers between devices, on_device(): x_parts = lax.all_gather(inputs, ('row', 'col'), axis=0)  63 us
    reduce_scatter x1, waiting for transfers between devices, on_device(): dkv = lax.psum_scatter(dkv, 'row', scatter_dimension=0, tiled=True)  53.5 us
    pallas_call x4, Pallas kernels, scatter_col(): pl.pallas_call(scatter_kernel, name='scatter_col', out_shape=jax.ShapeDty...  50.4 us
    pallas_call x1, Pallas kernels, attention_backward(): pl.pallas_call(functools.partial(backward_kernel, *dims), name='attn_bwd'...  39.5 us
    pallas_call x3, Pallas kernels, gather_col(): pl.pallas_call(gather_kernel, name='gather_col', out_shape=jax.ShapeDtype...  38.1 us
    pallas_call x1, Pallas kernels, scatter_row(): pl.pallas_call(functools.partial(scatter_row_kernel, rows, swap), name='s...  35.9 us
    all_gather x1, blocking collectives, on_device(): w_own = lax.all_gather(w_qkv, 'row', axis=0, tiled=True)  32.5 us
    pallas_call x1, Pallas kernels, attention_forward(): pl.pallas_call(functools.partial(forward_kernel, *dims), name='attn_fwd',...  30.7 us
  transfers between devices with their start and end apart: 9, of which 2 were waited for; matrix products, arithmetic and copies ran while one was open for 12% of the time, Pallas kernels for 32%

profile of v3, /device:TPU:0, one launch (start us, length us, event | category | flops | bytes accessed | tf_op | source)
XLA Modules:
  0.0 477.2 jit_solution(14738712617079644981)
XLA Ops:
  9.6 2.0 pad_maximum_fusion.2
  11.6 63.0 %all-gather.6.cloned.1.call-done = bf16[3072,1024]{1,0:T(8,128)(2,1)} async-done(((bf16[192,1024]{1,0:T(8,128)(2,1)}), bf16[3072,1024]{1,0:T(8,128)(2,1)}) %all-gather.6.cloned.1.call-update) | async-done | bytes 6291472 | tf_op jit(solution)/shard_map/all_gather | solution.py:646
  77.2 32.5 %all_gather.14 = bf16[768,588]{1,0:T(8,128)(2,1)S(1)} all-gather(bf16[192,588]{1,0:T(8,128)(2,1)S(1)} %concatenate.22), channel_id=1, replica_groups=mesh['dp'=2,'row'=4,'col'=4] {'row'}, dimensions={0}, use_global_device_ids=true | all-gather | bytes 1128960 | tf_op jit(solution)/shard_map/all_gather | solution.py:645
  115.4 5.6 %all-to-all-start.1 = ((bf16[192,4,256]{2,0,1:T(8,128)(2,1)}), bf16[192,4,256]{2,0,1:T(8,128)(2,1)}, u32[]{:S(2)}, u32[]{:S(2)}) async-start(bf16[192,4,256]{2,0,1:T(8,128)(2,1)} %bitcast.101), calls=%async_computation.1 | async-start | bytes 786432 | tf_op jit(solution)/shard_map/all_to_all | solution.py:657
  122.8 9.2 %project.1 = (bf16[1024,384]{1,0:T(8,128)(2,1)S(1)}, bf16[4096,384]{1,0:T(8,128)(2,1)}, bf16[768,1024]{1,0:T(8,128)(2,1)S(1)}, bf16[1024,128]{1,0:T(8,128)(2,1)S(1)}, bf16[4096,128]{1,0:T(8,128)(2,1)S(1)}) custom-call(s32[1]{0:T(128)} %bitcast.row_ref, bf16[4,4,192,1024]{3,2,1,0:T(8,128)(2,1)} %bitcast.152, bf16[768,384]{1,0:T(8,128)(2,1)S(1)} %copy-done.7, ...), custom_call_target="tpu_custom_call" | custom-call | flops 3623878656 | bytes 16777216 | tf_op jit(solution)/shard_map/project/pallas_call | solution.py:322
  137.3 30.7 %attn_fwd.1 = (bf16[1024,384]{1,0:T(8,128)(2,1)S(1)}, f32[1024,384]{1,0:T(8,128)S(1)}) custom-call(s32[1]{0:T(128)} %bitcast.row_ref, s32[576]{0:T(1024)S(1)} %reshape.206.rand_ref, bf16[1024,384]{1,0:T(8,128)(2,1)S(1)} %copy-done.3, bf16[1024,128]{1,0:T(8,128)(2,1)S(1)} %copy-done.9, bf16[4096,384]{1,0:T(8,128)(2,1)} %get-tuple-element.33.kv_ref, ...), custom_call_target="tpu_custom_call" | custom-call | flops 1207959552 | bytes 12582912 | tf_op jit(solution)/shard_map/attn_fwd/pallas_call | solution.py:251
  171.5 2.1 bitcast_convert_fusion
  176.6 11.5 %scatter_col.4 = f32[256,768]{1,0:T(8,128)S(1)} custom-call(bf16[4,256,768]{2,1,0:T(8,128)(2,1)S(1)} %bitcast.103), custom_call_target="tpu_custom_call" | custom-call | tf_op jit(solution)/shard_map/scatter_col/pallas_call | solution.py:583
  189.7 12.8 %gather_col.3 = bf16[4,256,768]{2,1,0:T(8,128)(2,1)S(1)} custom-call(bf16[256,768]{1,0:T(8,128)(2,1)S(1)} %fusion.17.x_ref), custom_call_target="tpu_custom_call" | custom-call | tf_op jit(solution)/shard_map/gather_col/pallas_call | solution.py:569
  203.9 2.0 convolution_convert_fusion.2
  205.9 13.0 %scatter_col.5 = f32[256,768]{1,0:T(8,128)S(1)} custom-call(bf16[4,256,768]{2,1,0:T(8,128)(2,1)S(1)} %bitcast.107), custom_call_target="tpu_custom_call" | custom-call | tf_op jit(solution)/shard_map/scatter_col/pallas_call | solution.py:583
  221.0 12.0 %gather_col.4 = bf16[4,256,768]{2,1,0:T(8,128)(2,1)S(1)} custom-call(bf16[256,768]{1,0:T(8,128)(2,1)S(1)} %get-tuple-element.66.x_ref), custom_call_target="tpu_custom_call" | custom-call | tf_op jit(solution)/shard_map/gather_col/pallas_call | solution.py:569
  234.7 3.7 fusion.6
  242.8 3.2 convolution_convert_fusion.1
  246.0 13.0 %scatter_col.6 = f32[256,768]{1,0:T(8,128)S(1)} custom-call(bf16[4,256,768]{2,1,0:T(8,128)(2,1)S(1)} %bitcast.105), custom_call_target="tpu_custom_call" | custom-call | tf_op jit(solution)/shard_map/scatter_col/pallas_call | solution.py:583
  260.8 13.3 %gather_col.5 = bf16[4,288,768]{2,1,0:T(8,128)(2,1)S(1)} custom-call(bf16[288,768]{1,0:T(8,128)(2,1)S(1)} %pad_maximum_fusion.6.x_ref), custom_call_target="tpu_custom_call" | custom-call | tf_op jit(solution)/shard_map/gather_col/pallas_call | solution.py:569
  275.4 2.1 convolution_convert_fusion.7
  278.5 2.3 copy.105.do_ref
  286.7 39.5 %attn_bwd.1 = (bf16[1024,384]{1,0:T(8,128)(2,1)S(1)}, bf16[4096,384]{1,0:T(8,128)(2,1)}) custom-call(s32[1]{0:T(128)} %bitcast.row_ref, s32[576]{0:T(1024)S(1)} %reshape.206.rand_ref, bf16[1024,384]{1,0:T(8,128)(2,1)S(1)} %copy-done.4, bf16[1024,128]{1,0:T(8,128)(2,1)S(1)} %copy-done.10, bf16[4096,384]{1,0:T(8,128)(2,1)} %get-tuple-element.33.kv_ref, ...), custom_call_target="tpu_custom_call" | custom-call | flops 2415919104 | bytes 20971520 | tf_op jit(solution)/shard_map/attn_bwd/pallas_call | solution.py:270
  327.2 1.9 copy.99
  329.1 5.1 %all-to-all-start = ((bf16[4,192,256]{2,1,0:T(8,128)(2,1)}), bf16[4,192,256]{2,1,0:T(8,128)(2,1)}, u32[]{:S(2)}, u32[]{:S(2)}) async-start(bf16[4,192,256]{2,1,0:T(8,128)(2,1)} %bitcast.125), calls=%async_computation | async-start | bytes 786432 | tf_op jit(solution)/shard_map/all_to_all | solution.py:681
  334.2 2.3 copy.106
  336.5 1.8 slice.148
  338.4 2.0 convolution_convert_fusion.8
  341.2 53.5 %reduce-scatter.6.cloned.1.call-done = bf16[1024,384]{1,0:T(8,128)(2,1)} async-done(((bf16[4096,384]{1,0:T(8,128)(2,1)}), bf16[1024,384]{1,0:T(8,128)(2,1)}) %reduce-scatter.6.cloned.1.call-update) | async-done | bytes 786448 | tf_op jit(solution)/shard_map/reduce_scatter | solution.py:715
  397.0 1.9 copy.111
  398.9 2.7 convolution_convert_fusion
  401.6 13.0 %scatter_col.7 = f32[256,768]{1,0:T(8,128)S(1)} custom-call(bf16[4,256,768]{2,1,0:T(8,128)(2,1)S(1)} %bitcast.106), custom_call_target="tpu_custom_call" | custom-call | tf_op jit(solution)/shard_map/scatter_col/pallas_call | solution.py:583
  415.6 4.3 all-to-all-start.2
  423.4 2.2 convolution_convert_fusion.6
  426.3 35.9 %scatter_row.1 = f32[192,576]{1,0:T(8,128)S(1)} custom-call(bf16[4,192,576]{2,1,0:T(8,128)(2,1)S(1)} %bitcast.104), custom_call_target="tpu_custom_call" | custom-call | tf_op jit(solution)/shard_map/scatter_row/pallas_call | solution.py:539
  468.3 2.1 fusion.42
  (160 shorter events, 60.2 us)
Async XLA Ops:
  7.2 67.4 %copy-start.27 = (f32[192]{0:T(256)S(1)}, f32[192]{0:T(256)}, u32[]{:S(2)}) copy-start(f32[192]{0:T(256)} %param.25) | copy-start | bytes 2308
  7.2 67.4 %copy-start.28 = (f32[192]{0:T(256)S(1)}, f32[192]{0:T(256)}, u32[]{:S(2)}) copy-start(f32[192]{0:T(256)} %param.24) | copy-start | bytes 2308
  7.2 67.4 %copy-start.29 = (f32[192]{0:T(256)S(1)}, f32[192]{0:T(256)}, u32[]{:S(2)}) copy-start(f32[192]{0:T(256)} %param.23) | copy-start | bytes 2308
  7.2 67.4 %copy-start.30 = (f32[192]{0:T(256)S(1)}, f32[192]{0:T(256)}, u32[]{:S(2)}) copy-start(f32[192]{0:T(256)} %param.22) | copy-start | bytes 2308
  7.2 67.9 %copy-start.23 = (bf16[1,1,36864]{2,1,0:T(2,128)(2,1)S(1)}, bf16[1,1,36864]{2,1,0:T(2,128)(2,1)}, u32[]{:S(2)}) copy-start(bf16[1,1,36864]{2,1,0:T(2,128)(2,1)} %param.16) | copy-start | bytes 221188
  7.2 68.4 %copy-start.24 = (bf16[1,1,36864]{2,1,0:T(2,128)(2,1)S(1)}, bf16[1,1,36864]{2,1,0:T(2,128)(2,1)}, u32[]{:S(2)}) copy-start(bf16[1,1,36864]{2,1,0:T(2,128)(2,1)} %param.17) | copy-start | bytes 221188
  7.2 68.9 %copy-start.25 = (bf16[1,1,36864]{2,1,0:T(2,128)(2,1)S(1)}, bf16[1,1,36864]{2,1,0:T(2,128)(2,1)}, u32[]{:S(2)}) copy-start(bf16[1,1,36864]{2,1,0:T(2,128)(2,1)} %param.18) | copy-start | bytes 221188
  7.3 69.5 %copy-start.26 = (s32[1,3,64,3]{2,0,3,1:T(1,128)S(1)}, s32[1,3,64,3]{2,0,3,1:T(1,128)}, u32[]{:S(2)}) copy-start(s32[1,3,64,3]{2,0,3,1:T(1,128)} %param.28) | copy-start | bytes 6916
  7.3 67.2 %all-gather.6.cloned.1.call-start = ((), (), s32[]{:S(2)}) async-start(), calls=%async_computation.9 | async-start | bytes 6684672 | tf_op jit(solution)/shard_map/all_gather | solution.py:646
  8.0 167.0 %all-gather.4.cloned.1.call-start = ((), (), s32[]{:S(2)}) async-start(), calls=%async_computation.6 | async-start | bytes 3440640 | tf_op jit(solution)/shard_map/all_gather | solution.py:650
  109.7 3.4 copy-start.15
  113.3 8.4 %copy-start.13 = (s32[4096]{0:T(1024)S(1)}, s32[4096]{0:T(1024)}, u32[]{:S(2)}) copy-start(s32[4096]{0:T(1024)} %param.26) | copy-start | bytes 49156
  113.3 8.4 %copy-start.14 = (s32[4096]{0:T(1024)S(1)}, s32[4096]{0:T(1024)}, u32[]{:S(2)}) copy-start(s32[4096]{0:T(1024)} %param.27) | copy-start | bytes 49156
  115.4 56.1 %all-to-all-start.1 = ((bf16[192,4,256]{2,0,1:T(8,128)(2,1)}), bf16[192,4,256]{2,0,1:T(8,128)(2,1)}, u32[]{:S(2)}, u32[]{:S(2)}) async-start(bf16[192,4,256]{2,0,1:T(8,128)(2,1)} %bitcast.101), calls=%async_computation.1 | async-start | bytes 786432 | tf_op jit(solution)/shard_map/all_to_all | solution.py:657
  120.9 220.2 %reduce-scatter.8.cloned.1.call-start = ((), (), s32[]{:S(2)}) async-start(), calls=%async_computation.8 | async-start | bytes 2949120 | tf_op jit(solution)/shard_map/reduce_scatter | solution.py:692
  133.7 34.4 %copy-start = (bf16[4096,128]{1,0:T(8,128)(2,1)}, bf16[4096,128]{1,0:T(8,128)(2,1)S(1)}, u32[]{:S(2)}) copy-start(bf16[4096,128]{1,0:T(8,128)(2,1)S(1)} %get-tuple-element.34.km_ref) | copy-start | bytes 3145732
  168.1 1.2 copy-start.11
  171.4 5.2 %copy-start.17 = (bf16[1024,3,1,64]{0,3,2,1:T(8,128)(2,1)}, bf16[1024,3,1,64]{0,3,2,1:T(8,128)(2,1)S(1)}, u32[]{:S(2)}) copy-start(bf16[1024,3,1,64]{0,3,2,1:T(8,128)(2,1)S(1)} %slice.136) | copy-start | bytes 1179652
  188.1 14.4 %copy-start.22 = (bf16[768,1728]{1,0:T(8,128)(2,1)S(1)}, bf16[768,1728]{1,0:T(8,128)(2,1)}, u32[]{:S(2)}) copy-start(bf16[768,1728]{1,0:T(8,128)(2,1)} %all-gather.4.cloned.1.call-done) | copy-start | bytes 7962628
  238.4 1.5 copy-start.31
  241.5 153.1 %reduce-scatter.6.cloned.1.call-start = ((), (), s32[]{:S(2)}) async-start(), calls=%async_computation.7 | async-start | bytes 3932160 | tf_op jit(solution)/shard_map/reduce_scatter | solution.py:715
  246.0 13.0 %copy-start.19 = (f32[256,768]{1,0:T(8,128)S(1)}, f32[256,768]{1,0:T(8,128)}, u32[]{:S(2)}) copy-start(f32[256,768]{1,0:T(8,128)} %get-tuple-element.67) | copy-start | bytes 2359300
  280.8 1.2 copy-start.1
  283.2 1.2 copy-start.6
  285.3 1.4 copy-start.12
  329.1 86.5 %all-to-all-start = ((bf16[4,192,256]{2,1,0:T(8,128)(2,1)}), bf16[4,192,256]{2,1,0:T(8,128)(2,1)}, u32[]{:S(2)}, u32[]{:S(2)}) async-start(bf16[4,192,256]{2,1,0:T(8,128)(2,1)} %bitcast.125), calls=%async_computation | async-start | bytes 786432 | tf_op jit(solution)/shard_map/all_to_all | solution.py:681
  334.2 87.5 %reduce-scatter.10.cloned.1.call-start = ((), (), s32[]{:S(2)}) async-start(), calls=%async_computation.10 | async-start | bytes 491520
  340.4 58.5 %copy-start.16 = (bf16[768,588]{1,0:T(8,128)(2,1)S(1)}, bf16[768,588]{1,0:T(8,128)(2,1)}, u32[]{:S(2)}) copy-start(bf16[768,588]{1,0:T(8,128)(2,1)} %copy-done.15) | copy-start | bytes 2709508
  401.6 13.0 %copy-start.18 = (f32[256,768]{1,0:T(8,128)S(1)}, f32[256,768]{1,0:T(8,128)}, u32[]{:S(2)}) copy-start(f32[256,768]{1,0:T(8,128)} %get-tuple-element.64) | copy-start | bytes 2359300
  414.6 8.8 %copy-start.21 = (bf16[1024,3,1,64]{0,3,2,1:T(8,128)(2,1)S(1)}, bf16[1024,3,1,64]{0,3,2,1:T(8,128)(2,1)}, u32[]{:S(2)}) copy-start(bf16[1024,3,1,64]{0,3,2,1:T(8,128)(2,1)} %slice.148) | copy-start | bytes 1179652
  415.6 49.2 %all-to-all-start.2 = ((bf16[4,192,256]{2,1,0:T(8,128)(2,1)}), bf16[4,192,256]{2,1,0:T(8,128)(2,1)S(1)}, u32[]{:S(2)}, u32[]{:S(2)}) async-start(bf16[4,192,256]{2,1,0:T(8,128)(2,1)} %bitcast.45), calls=%async_computation.4 | async-start | bytes 786432 | tf_op jit(solution)/shard_map/all_to_all | solution.py:732
  420.0 45.9 %all-reduce.6.cloned.1.call-start = ((), (), s32[]{:S(2)}) async-start(), calls=%async_computation.11 | async-start | bytes 1384448 | tf_op jit(solution)/shard_map/psum | solution.py:718
  (9 other events, 8.7 us)
Sparse Core Ops, SparseCore 0:
  10.4 64.1 all-gather.5
  76.1 74.6 all-gather.3
  241.6 48.3 reduce-scatter.7
  327.3 67.3 reduce-scatter.5
  399.0 21.4 reduce-scatter.9
  423.5 37.5 all-reduce.5

commit v4 on v3

--- a/solution.py
+++ b/solution.py
@@ -553,6 +553,151 @@
     )(value.reshape(rows, count, wide))
 
 
+def gather_in_kernel(rows, x_ref, w_ref, xs_ref, ws_ref, send_x, recv_x, send_w, recv_w):
+    me, col = lax.axis_index("row"), lax.axis_index("col")
+    right, left = lax.rem(me + 1, rows), lax.rem(me + rows - 1, rows)
+    has_left, has_right = me > 0, me < rows - 1
+    partner = col + 1 - 2 * lax.rem(col, 2)
+    cross = lax.rem(col + 2, 4)
+    diag = lax.rem(partner + 2, 4)
+    mesh_id = pl.DeviceIdType.MESH
+    barrier = pltpu.get_barrier_semaphore()
+
+    @pl.when(has_left)
+    def _():
+        pl.semaphore_signal(barrier, inc=1, device_id={"row": left}, device_id_type=mesh_id)
+
+    @pl.when(has_right)
+    def _():
+        pl.semaphore_signal(barrier, inc=1, device_id={"row": right}, device_id_type=mesh_id)
+
+    for peer in (partner, cross):
+        pl.semaphore_signal(barrier, inc=1, device_id={"col": peer}, device_id_type=mesh_id)
+    pl.semaphore_wait(barrier, jnp.where(has_left, 1, 0) + jnp.where(has_right, 1, 0) + 2)
+
+    def copy_x(source, kind, shard, slot, where):
+        return pltpu.make_async_remote_copy(
+            src_ref=source,
+            dst_ref=xs_ref.at[shard, slot],
+            send_sem=send_x.at[kind, shard],
+            recv_sem=recv_x.at[kind, shard],
+            device_id=where,
+            device_id_type=mesh_id,
+        )
+
+    def copy_w(source, kind, shard, where):
+        return pltpu.make_async_remote_copy(
+            src_ref=source,
+            dst_ref=ws_ref.at[shard],
+            send_sem=send_w.at[kind, shard],
+            recv_sem=recv_w.at[kind, shard],
+            device_id=where,
+            device_id_type=mesh_id,
+        )
+
+    to_right, to_left = {"row": right}, {"row": left}
+    ways = ((0, has_right, to_right), (1, has_left, to_left))
+
+    for kind, onward, where in ways:
+
+        @pl.when(onward)
+        def _():
+            copy_x(x_ref, kind, me, col, where).start()
+
+    copy_x(x_ref, 2, me, col, {"col": cross}).start()
+    copy_x(x_ref, 3, me, col, {"col": partner}).start()
+    for kind, onward, where in ways:
+
+        @pl.when(onward)
+        def _():
+            copy_w(w_ref, kind, me, where).start()
+
+    xs_ref[me, col] = x_ref[...]
+    ws_ref[me] = w_ref[...]
+
+    def relay(shard):
+        copy_x(x_ref, 2, shard, cross, {"col": cross}).wait_recv()
+        source = xs_ref.at[shard, cross]
+        copy_x(source, 4, shard, cross, {"col": partner}).start()
+
+    def shards_at(step):
+        return (
+            (0, me - step, me >= step, has_right, to_right),
+            (1, me + step, me + step <= rows - 1, has_left, to_left),
+        )
+
+    for step in range(1, rows):
+        for kind, shard, exists, onward, where in shards_at(step):
+
+            @pl.when(exists)
+            def _():
+                copy_x(x_ref, kind, shard, col, where).wait_recv()
+
+                @pl.when(onward)
+                def _():
+                    copy_x(xs_ref.at[shard, col], kind, shard, col, where).start()
+
+                copy_x(xs_ref.at[shard, col], 2, shard, col, {"col": cross}).start()
+                copy_x(xs_ref.at[shard, col], 3, shard, col, {"col": partner}).start()
+
+        for kind, shard, exists, onward, where in shards_at(step):
+
+            @pl.when(exists)
+            def _():
+                copy_w(w_ref, kind, shard, where).wait_recv()
+
+                @pl.when(onward)
+                def _():
+                    copy_w(ws_ref.at[shard], kind, shard, where).start()
+
+        if step == 1:
+            relay(me)
+        else:
+            for _, shard, exists, _, _ in shards_at(step - 1):
+
+                @pl.when(exists)
+                def _():
+                    relay(shard)
+
+    for _, shard, exists, _, _ in shards_at(rows - 1):
+
+        @pl.when(exists)
+        def _():
+            relay(shard)
+
+    for shard in range(rows):
+        copy_x(x_ref, 3, shard, partner, {"col": partner}).wait_recv()
+        copy_x(x_ref, 4, shard, diag, {"col": partner}).wait_recv()
+        for kind in (2, 3, 4):
+            copy_x(x_ref, kind, shard, col, {"col": partner}).wait_send()
+        for kind, sent, where in (
+            (0, has_right & (me >= shard), to_right),
+            (1, has_left & (me <= shard), to_left),
+        ):
+
+            @pl.when(sent)
+            def _():
+                copy_x(x_ref, kind, shard, col, where).wait_send()
+                copy_w(w_ref, kind, shard, where).wait_send()
+
+
+def gather_in(x, w, rows):
+    vmem = pl.BlockSpec(memory_space=pltpu.VMEM)
+    sems = pltpu.SemaphoreType.DMA
+    return pl.pallas_call(
+        functools.partial(gather_in_kernel, rows),
+        name="gather_in",
+        out_shape=(
+            jax.ShapeDtypeStruct((rows, 4) + x.shape, BF),
+            jax.ShapeDtypeStruct((rows,) + w.shape, BF),
+        ),
+        in_specs=[vmem, vmem],
+        out_specs=(vmem, vmem),
+        scratch_shapes=[sems((5, rows)), sems((5, rows)), sems((2, rows)), sems((2, rows))],
+        compiler_params=comm_params(5),
+    )(x, w)
+
+
 def comm_params(ident):
     return pltpu.CompilerParams(
         collective_id=ident, has_side_effects=True, vmem_limit_bytes=32 << 20
@@ -636,24 +781,26 @@
     blk_k = w_key.reshape(feat, hid)
     blk_v = w_value.reshape(feat, hid)
     blk_o = w_out.reshape(hid, feat)
-    params = jnp.stack([ln1_gain, ln1_bias, ln2_gain, ln2_bias], axis=1)
+    params = jnp.stack([ln1_gain, ln1_bias, ln2_gain, ln2_bias])
     high = params.astype(BF)
     rest = params - high.astype(F32)
     middle = rest.astype(BF)
     low = (rest - middle.astype(F32)).astype(BF)
-    w_qkv = jnp.concatenate([blk_q, blk_k, blk_v, high, middle, low], axis=1)
-    w_own = lax.all_gather(w_qkv, "row", axis=0, tiled=True)
-    x_parts = lax.all_gather(inputs, ("row", "col"), axis=0)
-    w_rest = jnp.concatenate([w_up, w_down, blk_o.T], axis=1)
+    params = jnp.concatenate([high, middle, low], axis=0)
+    params = jnp.pad(params, ((0, 4), (0, 4 * hid - feat)))
+    w_small = jnp.concatenate([blk_q, blk_k, blk_v, blk_o.T], axis=1)
+    w_small = jnp.concatenate([w_small, params], axis=0)
+    x_parts, w_small = gather_in(inputs, w_small, rows)
+    w_rest = jnp.concatenate([w_up, w_down], axis=1)
     x_parts, w_rest, grad_out = lax.optimization_barrier((x_parts, w_rest, grad_out))
-    x_parts = x_parts.reshape(rows, cols, feat, local)
     w_rest = lax.all_gather(w_rest, "row", axis=0, tiled=True)
     ff = w_up.shape[1]
-    up, down, w_o = w_rest[:, :ff], w_rest[:, ff : 2 * ff], w_rest[:, 2 * ff :]
-    gains = w_own[:, 3 * hid :].astype(F32)
-    gains = (gains[:, :4] + gains[:, 4:8]) + gains[:, 8:12]
-    gains = gains.T.reshape(4, 1, model)
-    w_own = w_own[:, : 3 * hid]
+    up, down = w_rest[:, :ff], w_rest[:, ff:]
+    gains = w_small[:, feat : feat + 12, :feat].astype(F32).reshape(rows, 3, 4, feat)
+    gains = (gains[:, 0] + gains[:, 1]) + gains[:, 2]
+    gains = gains.transpose(1, 0, 2).reshape(4, 1, model)
+    w_small = w_small[:, :feat].reshape(model, 4 * hid)
+    w_own, w_o = w_small[:, : 3 * hid], w_small[:, 3 * hid :]
     grad_rows = lax.all_to_all(grad_out, "row", 1, 0, tiled=True).T.astype(F32)
 
     w_heads = w_own.reshape(model, 3, heads, HW)
@@ -709,15 +856,17 @@
     d_o = mm(dattn, w_o).astype(BF)
     d_o = jnp.pad(d_o.reshape(own, heads, HW), ((0, 0), (0, 0), (HW, 0))).reshape(own, -1)
 
-    g_rest = jnp.concatenate([g_out, sums.T.astype(BF)], axis=1)
-
+    sums = sums.reshape(4, rows, feat).transpose(1, 0, 2).astype(BF)
+    sums = jnp.pad(sums, ((0, 0), (0, 12), (0, hid - feat)))
+    g_rest = jnp.concatenate([g_out.reshape(rows, feat, hid), sums], axis=1).reshape(-1, hid)
+    d_o, g_rest = lax.optimization_barrier((d_o, g_rest))
+    g_rest = lax.psum_scatter(g_rest, "row", scatter_dimension=0, tiled=True)
     dq, dkv = attention_backward(dims, row_arr, rand, q, q_mask, kv, k_mask, d_o, lse)
     dkv = lax.psum_scatter(dkv, "row", scatter_dimension=0, tiled=True)
     dkv, g_ffn, g_rest = lax.optimization_barrier((dkv, g_ffn, g_rest))
-    g_rest = lax.psum_scatter(g_rest, "row", scatter_dimension=0, tiled=True)
     g_ffn, g_rest = lax.psum((g_ffn, g_rest), "dp")
     g_ffn, g_rest = g_ffn.astype(F32), g_rest.astype(F32)
-    g_sums = g_rest[:, hid:].T
+    g_sums = g_rest[feat : feat + 4, :feat]
     dq = dq.reshape(own, heads, 2, HW)[:, :, 0].reshape(own, hid)
     dkv = dkv.reshape(own, heads, 2, HW)
     dqkv = jnp.concatenate(
@@ -737,7 +886,7 @@
         g_qkv[:, :hid].reshape(1, 1, -1),
         g_qkv[:, hid : 2 * hid].reshape(1, 1, -1),
         g_qkv[:, 2 * hid :].reshape(1, 1, -1),
-        g_rest[:, :hid].T.reshape(1, 1, -1),
+        g_rest[:feat].T.reshape(1, 1, -1),
         g_ffn[:feat],
         g_ffn[feat:],
         g_sums[0],

time: 479 us -> 467 us (0.975)
  Pallas kernels: 204 us -> 261 us
  blocking collectives: 32.5 us -> 0 us
  waiting for transfers between devices: 117 us -> 85.6 us
  local copies, waits for them, and re-layouts: 52.6 us -> 46.6 us
    all_gather x1 -> x0, waiting for transfers between devices: 63 us -> none  [on_device(): x_parts = lax.all_gather(inputs, ('row', 'col'), axis=0)]
    pallas_call x0 -> x1, Pallas kernels: none -> 55.7 us  [gather_in(): pl.pallas_call(functools.partial(gather_in_kernel, rows), name='gather_in...]
    all_gather x1 -> x0, blocking collectives: 32.5 us -> none  [on_device(): w_own = lax.all_gather(w_qkv, 'row', axis=0, tiled=True)]
    reduce_scatter x1, waiting for transfers between devices: 0.01 us -> 21.8 us  [on_device(): g_ffn = lax.psum_scatter(g_ffn, 'row', scatter_dimension=0, tiled=True)]
    reduce_scatter x1, waiting for transfers between devices: 53.5 us -> 63.1 us  [on_device(): dkv = lax.psum_scatter(dkv, 'row', scatter_dimension=0, tiled=True)]
    unnamed x67 -> x80, local copies, waits for them, and re-layouts: 17.1 us -> 17.1 us
  transfers between devices with their start and end apart: 9 -> 8, of which waited for: 2 -> 2; matrix products, arithmetic and copies ran while one was open for 12% -> 7% of each run, Pallas kernels for 32% -> 33%
where the time goes in v4:
time: 467 us; the launch traced here: 465 us
  Pallas kernels  261 us (56%)
  waiting for transfers between devices  85.6 us (18%)
  local copies, waits for them, and re-layouts  46.6 us (10%)
  matrix products  23.5 us (5%)
  other arithmetic  20.4 us (4%)
  between operations  14.6 us (3%)
  starting transfers between devices  13.3 us (3%)
    reduce_scatter x1, waiting for transfers between devices, on_device(): dkv = lax.psum_scatter(dkv, 'row', scatter_dimension=0, tiled=True)  63.1 us
    pallas_call x1, Pallas kernels, gather_in(): pl.pallas_call(functools.partial(gather_in_kernel, rows), name='gather_in...  55.7 us
    pallas_call x4, Pallas kernels, scatter_col(): pl.pallas_call(scatter_kernel, name='scatter_col', out_shape=jax.ShapeDty...  52 us
    pallas_call x1, Pallas kernels, attention_backward(): pl.pallas_call(functools.partial(backward_kernel, *dims), name='attn_bwd'...  39.5 us
    pallas_call x3, Pallas kernels, gather_col(): pl.pallas_call(gather_kernel, name='gather_col', out_shape=jax.ShapeDtype...  37.3 us
    pallas_call x1, Pallas kernels, scatter_row(): pl.pallas_call(functools.partial(scatter_row_kernel, rows, swap), name='s...  36.5 us
    pallas_call x1, Pallas kernels, attention_forward(): pl.pallas_call(functools.partial(forward_kernel, *dims), name='attn_fwd',...  30.9 us
    reduce_scatter x1, waiting for transfers between devices, on_device(): g_ffn = lax.psum_scatter(g_ffn, 'row', scatter_dimension=0, tiled=True)  21.8 us
  transfers between devices with their start and end apart: 8, of which 2 were waited for; matrix products, arithmetic and copies ran while one was open for 7% of the time, Pallas kernels for 33%

profile of v4, /device:TPU:0, one launch (start us, length us, event | category | flops | bytes accessed | tf_op | source)
XLA Modules:
  0.0 465.2 jit_solution(809650046249953837)
XLA Ops:
  14.7 1.9 pad_maximum_fusion.2
  16.7 55.7 %gather_in.1 = (bf16[4,4,192,1024]{3,2,1,0:T(8,128)(2,1)S(1)}, bf16[4,208,768]{2,1,0:T(8,128)(2,1)S(1)}) custom-call(bf16[192,1024]{1,0:T(8,128)(2,1)S(1)} %copy-done.10, bf16[208,768]{1,0:T(8,128)(2,1)S(1)} %pad_maximum_fusion.7.w_ref), custom_call_target="tpu_custom_call" | custom-call | tf_op jit(solution)/shard_map/gather_in/pallas_call | solution.py:687
  72.4 2.6 copy-done.14
  75.9 4.1 all-to-all-start.1
  86.7 9.2 %project.1 = (bf16[1024,384]{1,0:T(8,128)(2,1)S(1)}, bf16[4096,384]{1,0:T(8,128)(2,1)}, bf16[768,1024]{1,0:T(8,128)(2,1)S(1)}, bf16[1024,128]{1,0:T(8,128)(2,1)S(1)}, bf16[4096,128]{1,0:T(8,128)(2,1)S(1)}) custom-call(s32[1]{0:T(128)} %bitcast.row_ref, bf16[4,4,192,1024]{3,2,1,0:T(8,128)(2,1)} %copy-done.14, bf16[768,384]{1,0:T(8,128)(2,1)S(1)} %copy-done.9, ...), custom_call_target="tpu_custom_call" | custom-call | flops 3623878656 | bytes 16777216 | tf_op jit(solution)/shard_map/project/pallas_call | solution.py:322
  99.3 30.9 %attn_fwd.1 = (bf16[1024,384]{1,0:T(8,128)(2,1)S(1)}, f32[1024,384]{1,0:T(8,128)S(1)}) custom-call(s32[1]{0:T(128)} %bitcast.row_ref, s32[576]{0:T(1024)S(1)} %reshape.226.rand_ref, bf16[1024,384]{1,0:T(8,128)(2,1)S(1)} %get-tuple-element.37.q_ref, bf16[1024,128]{1,0:T(8,128)(2,1)S(1)} %copy-done.12, bf16[4096,384]{1,0:T(8,128)(2,1)} %get-tuple-element.39.kv_ref, ...), custom_call_target="tpu_custom_call" | custom-call | flops 1207959552 | bytes 12582912 | tf_op jit(solution)/shard_map/attn_fwd/pallas_call | solution.py:251
  133.8 1.9 convolution_convert_fusion.3
  135.7 13.0 %scatter_col.4 = f32[256,768]{1,0:T(8,128)S(1)} custom-call(bf16[4,256,768]{2,1,0:T(8,128)(2,1)S(1)} %bitcast.104), custom_call_target="tpu_custom_call" | custom-call | tf_op jit(solution)/shard_map/scatter_col/pallas_call | solution.py:728
  151.1 12.1 %gather_col.3 = bf16[4,256,768]{2,1,0:T(8,128)(2,1)S(1)} custom-call(bf16[256,768]{1,0:T(8,128)(2,1)S(1)} %fusion.18.x_ref), custom_call_target="tpu_custom_call" | custom-call | tf_op jit(solution)/shard_map/gather_col/pallas_call | solution.py:714
  164.5 1.9 bitcast_convert_fusion
  166.4 2.3 copy.83
  168.7 2.8 fusion.13
  171.5 2.0 convolution_convert_fusion.2
  173.6 13.0 %scatter_col.5 = f32[256,768]{1,0:T(8,128)S(1)} custom-call(bf16[4,256,768]{2,1,0:T(8,128)(2,1)S(1)} %bitcast.108), custom_call_target="tpu_custom_call" | custom-call | tf_op jit(solution)/shard_map/scatter_col/pallas_call | solution.py:728
  188.8 12.0 %gather_col.4 = bf16[4,256,768]{2,1,0:T(8,128)(2,1)S(1)} custom-call(bf16[256,768]{1,0:T(8,128)(2,1)S(1)} %get-tuple-element.70.x_ref), custom_call_target="tpu_custom_call" | custom-call | tf_op jit(solution)/shard_map/gather_col/pallas_call | solution.py:714
  202.4 3.7 fusion.6
  209.8 2.7 convolution_convert_fusion.1
  212.5 13.0 %scatter_col.6 = f32[256,768]{1,0:T(8,128)S(1)} custom-call(bf16[4,256,768]{2,1,0:T(8,128)(2,1)S(1)} %bitcast.106), custom_call_target="tpu_custom_call" | custom-call | tf_op jit(solution)/shard_map/scatter_col/pallas_call | solution.py:728
  227.3 13.2 %gather_col.5 = bf16[4,288,768]{2,1,0:T(8,128)(2,1)S(1)} custom-call(bf16[288,768]{1,0:T(8,128)(2,1)S(1)} %pad_maximum_fusion.6.x_ref), custom_call_target="tpu_custom_call" | custom-call | tf_op jit(solution)/shard_map/gather_col/pallas_call | solution.py:714
  241.1 1.8 convolution_convert_fusion.7
  246.8 2.3 copy.88.do_ref
  252.6 39.5 %attn_bwd.1 = (bf16[1024,384]{1,0:T(8,128)(2,1)S(1)}, bf16[4096,384]{1,0:T(8,128)(2,1)}) custom-call(s32[1]{0:T(128)} %bitcast.row_ref, s32[576]{0:T(1024)S(1)} %reshape.226.rand_ref, bf16[1024,384]{1,0:T(8,128)(2,1)S(1)} %copy-done.3, bf16[1024,128]{1,0:T(8,128)(2,1)S(1)} %copy-done.13, bf16[4096,384]{1,0:T(8,128)(2,1)} %get-tuple-element.39.kv_ref, ...), custom_call_target="tpu_custom_call" | custom-call | flops 2415919104 | bytes 20971520 | tf_op jit(solution)/shard_map/attn_bwd/pallas_call | solution.py:270
  295.0 5.3 %all-to-all-start = ((bf16[4,192,256]{2,1,0:T(8,128)(2,1)}), bf16[4,192,256]{2,1,0:T(8,128)(2,1)}, u32[]{:S(2)}, u32[]{:S(2)}) async-start(bf16[4,192,256]{2,1,0:T(8,128)(2,1)} %bitcast.26), calls=%async_computation | async-start | bytes 786432 | tf_op jit(solution)/shard_map/all_to_all | solution.py:828
  301.3 21.8 %reduce-scatter.6.cloned.1.call-done = bf16[384,768]{1,0:T(8,128)(2,1)} async-done(((bf16[1536,768]{1,0:T(8,128)(2,1)}), bf16[384,768]{1,0:T(8,128)(2,1)}) %reduce-scatter.6.cloned.1.call-update) | async-done | bytes 589840 | tf_op jit(solution)/shard_map/reduce_scatter | solution.py:839
  323.1 63.1 %reduce-scatter.4.cloned.1.call-done = bf16[1024,384]{1,0:T(8,128)(2,1)} async-done(((bf16[4096,384]{1,0:T(8,128)(2,1)}), bf16[1024,384]{1,0:T(8,128)(2,1)}) %reduce-scatter.4.cloned.1.call-update) | async-done | bytes 786448 | tf_op jit(solution)/shard_map/reduce_scatter | solution.py:865
  387.6 2.7 convolution_convert_fusion
  390.4 13.0 %scatter_col.7 = f32[256,768]{1,0:T(8,128)S(1)} custom-call(bf16[4,256,768]{2,1,0:T(8,128)(2,1)S(1)} %bitcast.107), custom_call_target="tpu_custom_call" | custom-call | tf_op jit(solution)/shard_map/scatter_col/pallas_call | solution.py:728
  404.5 3.7 all-to-all-start.2
  408.2 1.8 copy.99
  410.1 2.2 convolution_convert_fusion.6
  413.0 36.5 %scatter_row.1 = f32[192,576]{1,0:T(8,128)S(1)} custom-call(bf16[4,192,576]{2,1,0:T(8,128)(2,1)S(1)} %bitcast.105), custom_call_target="tpu_custom_call" | custom-call | tf_op jit(solution)/shard_map/scatter_row/pallas_call | solution.py:539
  456.5 2.1 fusion.53
  (176 shorter events, 56.5 us)
Async XLA Ops:
  7.2 9.6 %copy-start.10 = (bf16[192,1024]{1,0:T(8,128)(2,1)S(1)}, bf16[192,1024]{1,0:T(8,128)(2,1)}, u32[]{:S(2)}) copy-start(bf16[192,1024]{1,0:T(8,128)(2,1)} %x_ref.1) | copy-start | bytes 1179652
  7.2 161.5 %all-gather.2.cloned.1.call-start = ((), (), s32[]{:S(2)}) async-start(), calls=%async_computation.6 | async-start | bytes 2949120 | tf_op jit(solution)/shard_map/all_gather | solution.py:796
  10.2 64.9 %copy-start.30 = (bf16[192,1024]{1,0:T(8,128)(2,1)S(1)}, bf16[192,1024]{1,0:T(8,128)(2,1)}, u32[]{:S(2)}) copy-start(bf16[192,1024]{1,0:T(8,128)(2,1)} %param.29) | copy-start | bytes 1179652
  14.7 65.4 %copy-start.34 = (s32[1,3,64,3]{2,0,3,1:T(1,128)S(1)}, s32[1,3,64,3]{2,0,3,1:T(1,128)}, u32[]{:S(2)}) copy-start(s32[1,3,64,3]{2,0,3,1:T(1,128)} %param.28) | copy-start | bytes 6916
  72.4 2.7 copy-start.14
  75.9 87.3 %all-to-all-start.1 = ((bf16[192,4,256]{2,0,1:T(8,128)(2,1)}), bf16[192,4,256]{2,0,1:T(8,128)(2,1)}, u32[]{:S(2)}, u32[]{:S(2)}) async-start(bf16[192,4,256]{2,0,1:T(8,128)(2,1)} %bitcast.103), calls=%async_computation.1 | async-start | bytes 786432 | tf_op jit(solution)/shard_map/all_to_all | solution.py:804
  80.0 221.3 %reduce-scatter.8.cloned.1.call-start = ((), (), s32[]{:S(2)}) async-start(), calls=%async_computation.9 | async-start | bytes 532480 | tf_op jit(solution)/shard_map/reduce_scatter | solution.py:863
  82.3 2.2 copy-start.17
  82.4 2.2 copy-start.18
  96.6 33.6 %copy-start = (bf16[4096,128]{1,0:T(8,128)(2,1)}, bf16[4096,128]{1,0:T(8,128)(2,1)S(1)}, u32[]{:S(2)}) copy-start(bf16[4096,128]{1,0:T(8,128)(2,1)S(1)} %get-tuple-element.40.km_ref) | copy-start | bytes 3145732
  96.6 33.6 %copy-start.2 = (bf16[1024,384]{1,0:T(8,128)(2,1)}, bf16[1024,384]{1,0:T(8,128)(2,1)S(1)}, u32[]{:S(2)}) copy-start(bf16[1024,384]{1,0:T(8,128)(2,1)S(1)} %get-tuple-element.37.q_ref) | copy-start | bytes 2359300
  133.8 2.0 copy-start.25
  168.7 2.8 copy-start.35
  173.6 13.0 %copy-start.20 = (f32[256,768]{1,0:T(8,128)S(1)}, f32[256,768]{1,0:T(8,128)}, u32[]{:S(2)}) copy-start(f32[256,768]{1,0:T(8,128)} %copy-done.19) | copy-start | bytes 2359300
  173.6 13.4 %copy-start.24 = (f32[768,256]{0,1:T(8,128)S(1)}, f32[768,256]{0,1:T(8,128)}, u32[]{:S(2)}) copy-start(f32[768,256]{0,1:T(8,128)} %copy.83) | copy-start | bytes 2359300
  207.7 2.1 copy-start.37
  212.5 13.0 %copy-start.21 = (f32[256,768]{1,0:T(8,128)S(1)}, f32[256,768]{1,0:T(8,128)}, u32[]{:S(2)}) copy-start(f32[256,768]{1,0:T(8,128)} %copy-done.19) | copy-start | bytes 2359300
  212.5 13.0 %copy-start.28 = (f32[256,768]{1,0:T(8,128)S(1)}, f32[256,768]{1,0:T(8,128)}, u32[]{:S(2)}) copy-start(f32[256,768]{1,0:T(8,128)} %get-tuple-element.71) | copy-start | bytes 2359300
  227.3 13.3 %copy-start.26 = (bf16[1024,3,1,64]{0,3,2,1:T(8,128)(2,1)S(1)}, bf16[1024,3,1,64]{0,3,2,1:T(8,128)(2,1)}, u32[]{:S(2)}) copy-start(bf16[1024,3,1,64]{0,3,2,1:T(8,128)(2,1)} %copy-done.25) | copy-start | bytes 1179652
  246.0 3.1 copy-start.1
  246.0 3.1 copy-start.3
  246.0 77.0 %reduce-scatter.6.cloned.1.call-start = ((), (), s32[]{:S(2)}) async-start(), calls=%async_computation.8 | async-start | bytes 2949120 | tf_op jit(solution)/shard_map/reduce_scatter | solution.py:839
  246.8 139.4 %reduce-scatter.4.cloned.1.call-start = ((), (), s32[]{:S(2)}) async-start(), calls=%async_computation.7 | async-start | bytes 3932160 | tf_op jit(solution)/shard_map/reduce_scatter | solution.py:865
  293.0 7.2 %copy-start.5 = (bf16[1024,384]{1,0:T(8,128)(2,1)S(1)}, bf16[1024,384]{1,0:T(8,128)(2,1)}, u32[]{:S(2)}) copy-start(bf16[1024,384]{1,0:T(8,128)(2,1)} %copy-done.4) | copy-start | bytes 2359300
  295.0 109.5 %all-to-all-start = ((bf16[4,192,256]{2,1,0:T(8,128)(2,1)}), bf16[4,192,256]{2,1,0:T(8,128)(2,1)}, u32[]{:S(2)}, u32[]{:S(2)}) async-start(bf16[4,192,256]{2,1,0:T(8,128)(2,1)} %bitcast.26), calls=%async_computation | async-start | bytes 786432 | tf_op jit(solution)/shard_map/all_to_all | solution.py:828
  300.5 87.1 %copy-start.23 = (bf16[4,192,768]{2,1,0:T(8,128)(2,1)S(1)}, bf16[4,192,768]{2,1,0:T(8,128)(2,1)}, u32[]{:S(2)}) copy-start(bf16[4,192,768]{2,1,0:T(8,128)(2,1)} %copy-done.22) | copy-start | bytes 3538948
  387.6 2.8 copy-start.32
  387.6 2.8 copy-start.33
  390.4 13.0 %copy-start.27 = (f32[256,768]{1,0:T(8,128)S(1)}, f32[256,768]{1,0:T(8,128)}, u32[]{:S(2)}) copy-start(f32[256,768]{1,0:T(8,128)} %get-tuple-element.68) | copy-start | bytes 2359300
  403.4 6.6 %copy-start.31 = (bf16[1024,3,1,64]{0,3,2,1:T(8,128)(2,1)S(1)}, bf16[1024,3,1,64]{0,3,2,1:T(8,128)(2,1)}, u32[]{:S(2)}) copy-start(bf16[1024,3,1,64]{0,3,2,1:T(8,128)(2,1)} %slice.152) | copy-start | bytes 1179652
  404.5 47.7 %all-to-all-start.2 = ((bf16[4,192,256]{2,1,0:T(8,128)(2,1)}), bf16[4,192,256]{2,1,0:T(8,128)(2,1)S(1)}, u32[]{:S(2)}, u32[]{:S(2)}) async-start(bf16[4,192,256]{2,1,0:T(8,128)(2,1)} %bitcast.48), calls=%async_computation.5 | async-start | bytes 786432 | tf_op jit(solution)/shard_map/all_to_all | solution.py:881
  408.2 45.0 %all-reduce.8.cloned.1.call-start = ((), (), s32[]{:S(2)}) async-start(), calls=%async_computation.10 | async-start | bytes 1392640 | tf_op jit(solution)/shard_map/psum | solution.py:867
  (14 other events, 14.7 us)
Sparse Core Ops, SparseCore 0:
  75.2 55.7 all-gather.1
  246.2 22.1 reduce-scatter.7
  270.6 52.3 reduce-scatter.5
  325.2 60.8 reduce-scatter.3
  411.0 37.7 all-reduce.7

commit v5 on v4

--- a/solution.py
+++ b/solution.py
@@ -38,7 +38,7 @@
     return ref[pl.ds(start, BLOCK), head * LANES : (head + 1) * LANES]
 
 
-def sparse_lists(rand_ref, head, pos, nb):
+def sparse_list(rand_ref, head, pos, nb):
     before = jnp.maximum(pos - 1, 0)
     after = jnp.minimum(pos + 1, nb - 1)
     picks = [rand_ref[(head * nb + pos) * 3 + i] for i in range(3)]
@@ -49,96 +49,84 @@
     return [group * 8 + i for i in range(8)]
 
 
-def sparse_bar(pos, nb):
-    entry = lax.broadcasted_iota(jnp.int32, (1, 8 * BLOCK), 1) // BLOCK
-    no_before = jnp.where(pos < 2, 8.0, 0.0)
-    no_after = jnp.where(pos > nb - 3, 8.0, 0.0)
-    return 0.5 + jnp.where(entry == 2, no_before, 0.0) + jnp.where(entry == 4, no_after, 0.0)
-
-
 def gather(ref, blocks, head):
     return jnp.concatenate([rows_at(ref, b, head) for b in blocks], axis=0)
 
 
-def scores_of(query, query_mask, keys, key_mask, own, bar):
-    shape = (query.shape[0], keys.shape[0])
+def allowed_of(query_segs, sk_ref, blocks, own, drop):
+    def segs_of(i):
+        segs = sk_ref[pl.ds(blocks[i], 1), :]
+        if i in drop:
+            keep = jnp.where(drop[i], 0, 1)
+            segs = segs * keep - 2 * (1 - keep)
+        return segs
+
+    low = lax.broadcasted_iota(jnp.int32, (1, LANES), 1) < BLOCK
+    segs = jnp.concatenate(
+        [jnp.where(low, segs_of(i), segs_of(i + 1)) for i in range(0, len(blocks), 2)], axis=1
+    )
+    shape = (query_segs.shape[0], segs.shape[1])
     apart = lax.broadcasted_iota(jnp.int32, shape, 1) - lax.broadcasted_iota(jnp.int32, shape, 0)
-    allowed = (mm_nt(query_mask, key_mask) > bar) | (apart == own * BLOCK)
-    return jnp.where(allowed, mm_nt(query, keys), NEG)
-
-
-def forward_kernel(heads, nb, per, rows, row_ref, rand_ref, q_ref, qm_ref, kv_ref, km_ref, o_ref, lse_ref):
+    query = jnp.concatenate([query_segs] * (len(blocks) // 2), axis=1)
+    return (query == segs) | (apart == own * BLOCK)
+
+
+def forward_kernel(
+    heads, nb, per, rows, row_ref, rand_ref, q_ref, qs_ref, kv_ref, sk_ref, o_ref, lse_ref
+):
     row = row_ref[0]
 
     def place(j, head):
         start = pl.multiple_of(j * BLOCK, BLOCK)
         return pl.ds(start, BLOCK), slice(head * LANES, (head + 1) * LANES)
 
+    def store(at, top, total, summed):
+        o_ref[at] = (summed * (1.0 / total)).astype(BF)
+        lse_ref[at] = jnp.broadcast_to(top + jnp.log(total), (BLOCK, LANES))
+
     def step(j, carry):
         pos = block_of(j, row, per, rows)
         is_global = (pos == 0) | (pos == nb - 1)
-        query_mask = qm_ref[pl.ds(pl.multiple_of(j * BLOCK, BLOCK), BLOCK), :]
+        query_segs = qs_ref[pl.ds(pl.multiple_of(j * BLOCK, BLOCK), BLOCK), :]
 
         @pl.when(jnp.logical_not(is_global))
         def _():
             for head in range(heads):
                 at = place(j, head)
-                blocks = sparse_lists(rand_ref, head, pos, nb)
+                blocks = sparse_list(rand_ref, head, pos, nb)
+                allowed = allowed_of(query_segs, sk_ref, blocks, 3, {2: pos < 2, 4: pos > nb - 3})
                 keys = gather(kv_ref, blocks, head)
-                score = scores_of(
-                    q_ref[at], query_mask, keys, gather(km_ref, blocks, 0), 3, sparse_bar(pos, nb)
-                )
+                score = jnp.where(allowed, mm_nt(q_ref[at], keys), NEG)
                 top = jnp.max(score, axis=1, keepdims=True)
                 weight = jnp.exp(score - top)
                 total = jnp.sum(weight, axis=1, keepdims=True)
-                probs = (weight * (1.0 / total)).astype(BF)
-                o_ref[at] = mm(probs, keys).astype(BF)
-                lse_ref[at] = jnp.broadcast_to(top + jnp.log(total), (BLOCK, LANES))
+                store(at, top, total, mm(weight.astype(BF), keys))
 
         @pl.when(is_global)
         def _():
-            def score_at(group, head):
+            def online(group, kept):
                 blocks = dense_list(group)
-                keys = gather(kv_ref, blocks, head)
-                score = scores_of(
-                    q_ref[place(j, head)], query_mask, keys, gather(km_ref, blocks, 0),
-                    pos - group * 8, 0.5,
-                )
-                return score, keys
-
-            def stats(group, kept):
+                allowed = allowed_of(query_segs, sk_ref, blocks, pos - group * 8, {})
                 new = []
                 for head in range(heads):
-                    top, total = kept[head]
-                    score, _ = score_at(group, head)
+                    top, total, summed = kept[head]
+                    keys = gather(kv_ref, blocks, head)
+                    score = jnp.where(allowed, mm_nt(q_ref[place(j, head)], keys), NEG)
                     above = jnp.maximum(top, jnp.max(score, axis=1, keepdims=True))
-                    total = total * jnp.exp(top - above) + jnp.sum(
-                        jnp.exp(score - above), axis=1, keepdims=True
-                    )
-                    new.append((above, total))
+                    fade = jnp.exp(top - above)
+                    weight = jnp.exp(score - above)
+                    total = total * fade + jnp.sum(weight, axis=1, keepdims=True)
+                    new.append((above, total, summed * fade + mm(weight.astype(BF), keys)))
                 return tuple(new)
 
-            first = tuple(
-                (jnp.full((BLOCK, 1), 2 * NEG, F32), jnp.zeros((BLOCK, 1), F32))
-                for _ in range(heads)
+            first = (
+                jnp.full((BLOCK, 1), 2 * NEG, F32),
+                jnp.zeros((BLOCK, 1), F32),
+                jnp.zeros((BLOCK, LANES), F32),
             )
-            found = lax.fori_loop(0, nb // 8, stats, first)
-            lses = [top + jnp.log(total) for top, total in found]
-
-            def outs(group, kept):
-                new = []
-                for head in range(heads):
-                    score, keys = score_at(group, head)
-                    new.append(kept[head] + mm(jnp.exp(score - lses[head]).astype(BF), keys))
-                return tuple(new)
-
-            done = lax.fori_loop(
-                0, nb // 8, outs, tuple(jnp.zeros((BLOCK, LANES), F32) for _ in range(heads))
-            )
+            found = lax.fori_loop(0, nb // 8, online, (first,) * heads)
             for head in range(heads):
-                at = place(j, head)
-                o_ref[at] = done[head].astype(BF)
-                lse_ref[at] = jnp.broadcast_to(lses[head], (BLOCK, LANES))
+                store(place(j, head), *found[head])
 
         return carry
 
@@ -146,7 +134,7 @@
 
 
 def backward_kernel(
-    heads, nb, per, rows, row_ref, rand_ref, q_ref, qm_ref, kv_ref, km_ref, do_ref, lse_ref,
+    heads, nb, per, rows, row_ref, rand_ref, q_ref, qs_ref, kv_ref, sk_ref, do_ref, lse_ref, o_ref,
     dq_ref, dkv_ref, acc_ref,
 ):
     row = row_ref[0]
@@ -156,20 +144,16 @@
         start = pl.multiple_of(j * BLOCK, BLOCK)
         return pl.ds(start, BLOCK), slice(head * LANES, (head + 1) * LANES)
 
-    def parts(j, head, query_mask, blocks, mine, bar):
+    def work(j, head, blocks, allowed):
         at = place(j, head)
         keys = gather(kv_ref, blocks, head)
-        score = scores_of(q_ref[at], query_mask, keys, gather(km_ref, blocks, 0), mine, bar)
-        lse = lse_ref[at][:, :1]
-        probs = jnp.exp(score - lse)
-        return keys, probs, mm_nt(do_ref[at], keys)
-
-    def finish(j, head, blocks, keys, probs, grad_probs, dot_row):
-        at = place(j, head)
-        low = (probs * (grad_probs - dot_row)).astype(BF)
-        both = jnp.concatenate([low, probs.astype(BF)], axis=0)
-        sides = jnp.concatenate([q_ref[at], do_ref[at]], axis=0)
-        grad = mm_tn(both, sides)
+        grad_o = do_ref[at]
+        sides = jnp.concatenate([q_ref[at], grad_o], axis=0)
+        both = mm_nt(sides, keys)
+        dot_row = jnp.sum(grad_o.astype(F32) * o_ref[at].astype(F32), axis=1, keepdims=True)
+        probs = jnp.exp(jnp.where(allowed, both[:BLOCK], NEG) - lse_ref[at][:, :1])
+        low = (probs * (both[BLOCK:] - dot_row)).astype(BF)
+        grad = mm_tn(jnp.concatenate([low, probs.astype(BF)], axis=0), sides)
         for i, block in enumerate(blocks):
             start = pl.multiple_of(block * BLOCK, BLOCK)
             acc_ref[pl.ds(start, BLOCK), at[1]] += grad[i * BLOCK : (i + 1) * BLOCK, :]
@@ -178,45 +162,24 @@
     def step(j, carry):
         pos = block_of(j, row, per, rows)
         is_global = (pos == 0) | (pos == nb - 1)
-        query_mask = qm_ref[pl.ds(pl.multiple_of(j * BLOCK, BLOCK), BLOCK), :]
+        query_segs = qs_ref[pl.ds(pl.multiple_of(j * BLOCK, BLOCK), BLOCK), :]
 
         @pl.when(jnp.logical_not(is_global))
         def _():
             for head in range(heads):
-                blocks = sparse_lists(rand_ref, head, pos, nb)
-                keys, probs, grad_probs = parts(
-                    j, head, query_mask, blocks, 3, sparse_bar(pos, nb)
-                )
-                dot_row = jnp.sum(probs * grad_probs, axis=1, keepdims=True)
-                grad_q = finish(j, head, blocks, keys, probs, grad_probs, dot_row)
+                blocks = sparse_list(rand_ref, head, pos, nb)
+                allowed = allowed_of(query_segs, sk_ref, blocks, 3, {2: pos < 2, 4: pos > nb - 3})
+                grad_q = work(j, head, blocks, allowed)
                 dq_ref[place(j, head)] = (grad_q * 0.125).astype(BF)
 
         @pl.when(is_global)
         def _():
-            def dots(group, kept):
-                blocks = dense_list(group)
-                mine = pos - group * 8
-                new = []
-                for head in range(heads):
-                    _, probs, grad_probs = parts(j, head, query_mask, blocks, mine, 0.5)
-                    new.append(kept[head] + jnp.sum(probs * grad_probs, axis=1, keepdims=True))
-                return tuple(new)
-
-            dot_rows = lax.fori_loop(
-                0, nb // 8, dots, tuple(jnp.zeros((BLOCK, 1), F32) for _ in range(heads))
-            )
-
             def grads(group, kept):
                 blocks = dense_list(group)
-                mine = pos - group * 8
-                new = []
-                for head in range(heads):
-                    keys, probs, grad_probs = parts(j, head, query_mask, blocks, mine, 0.5)
-                    new.append(
-                        kept[head]
-                        + finish(j, head, blocks, keys, probs, grad_probs, dot_rows[head])
-                    )
-                return tuple(new)
+                allowed = allowed_of(query_segs, sk_ref, blocks, pos - group * 8, {})
+                return tuple(
+                    kept[head] + work(j, head, blocks, allowed) for head in range(heads)
+                )
 
             done = lax.fori_loop(
                 0, nb // 8, grads, tuple(jnp.zeros((BLOCK, LANES), F32) for _ in range(heads))
@@ -245,7 +208,7 @@
     ] * count
 
 
-def attention_forward(dims, row, rand, q, q_mask, kv, k_mask):
+def attention_forward(dims, row, rand, q, q_segs, kv, k_segs):
     own, wide = q.shape
     vmem = pl.BlockSpec(memory_space=pltpu.VMEM)
     return pl.pallas_call(
@@ -261,10 +224,10 @@
             flops=own * 512 * wide * 6, bytes_accessed=12 << 20, transcendentals=own * 512 * 3
         ),
         compiler_params=pltpu.CompilerParams(vmem_limit_bytes=48 << 20),
-    )(row, rand, q, q_mask, kv, k_mask)
-
-
-def attention_backward(dims, row, rand, q, q_mask, kv, k_mask, d_o, lse):
+    )(row, rand, q, q_segs, kv, k_segs)
+
+
+def attention_backward(dims, row, rand, q, q_segs, kv, k_segs, d_o, lse, o):
     own, wide = q.shape
     vmem = pl.BlockSpec(memory_space=pltpu.VMEM)
     return pl.pallas_call(
@@ -274,26 +237,18 @@
             jax.ShapeDtypeStruct((own, wide), BF),
             jax.ShapeDtypeStruct(kv.shape, BF),
         ),
-        in_specs=specs(6),
+        in_specs=specs(7),
         out_specs=(vmem, vmem),
         scratch_shapes=[pltpu.VMEM(kv.shape, F32)],
         cost_estimate=pl.CostEstimate(
             flops=own * 512 * wide * 12, bytes_accessed=20 << 20, transcendentals=own * 512 * 3
         ),
         compiler_params=pltpu.CompilerParams(vmem_limit_bytes=48 << 20),
-    )(row, rand, q, q_mask, kv, k_mask, d_o, lse)
-
-
-def one_hot_rows(hot):
-    kinds = hot.shape[0]
-    shape = (kinds, LANES)
-    eye = lax.broadcasted_iota(jnp.int32, shape, 0) == lax.broadcasted_iota(jnp.int32, shape, 1)
-    return mm_tn(jnp.where(hot, 1.0, 0.0).astype(BF), jnp.where(eye, 1.0, 0.0).astype(BF)).astype(BF)
+    )(row, rand, q, q_segs, kv, k_segs, d_o, lse, o)
 
 
 def project_kernel(
-    rows, span, row_ref, x_ref, wq_ref, wkv_ref, seg_ref, pad_ref,
-    q_ref, kv_ref, own_ref, qm_ref, km_ref,
+    rows, span, row_ref, x_ref, wq_ref, wkv_ref, q_ref, kv_ref, own_ref
 ):
     feat = x_ref.shape[2]
     start = pl.multiple_of(row_ref[0] * span, span)
@@ -308,15 +263,9 @@
         q = q_part if q is None else q + q_part
     kv_ref[...] = kv.astype(BF)
     q_ref[...] = (q.astype(BF) * 0.125).astype(BF)
-    segs = seg_ref[...]
-    kinds = lax.broadcasted_iota(jnp.int32, (BLOCK, segs.shape[1]), 0)
-    km_ref[...] = one_hot_rows((kinds == segs) & (pad_ref[...] == 1))
-    mine = seg_ref[:, pl.ds(start, span)]
-    kinds = lax.broadcasted_iota(jnp.int32, (BLOCK, span), 0)
-    qm_ref[...] = one_hot_rows(kinds == mine)
-
-
-def project(row, x_parts, w_q, w_kv, span, segs, pads):
+
+
+def project(row, x_parts, w_q, w_kv, span):
     rows, cols, feat, local = x_parts.shape
     model, wide = w_q.shape
     return pl.pallas_call(
@@ -327,29 +276,23 @@
             jax.ShapeDtypeStruct((cols * span, wide), BF),
             jax.ShapeDtypeStruct((cols * local, wide), BF),
             jax.ShapeDtypeStruct((model, cols * span), BF),
-            jax.ShapeDtypeStruct((cols * span, LANES), BF),
-            jax.ShapeDtypeStruct((cols * local, LANES), BF),
         ),
         in_specs=[
             pl.BlockSpec(memory_space=pltpu.SMEM),
             pl.BlockSpec((rows, 1, feat, local), lambda c: (0, c, 0, 0)),
             pl.BlockSpec((model, wide), lambda c: (0, 0)),
             pl.BlockSpec((model, wide), lambda c: (0, 0)),
-            pl.BlockSpec((1, local), lambda c: (0, c)),
-            pl.BlockSpec((1, local), lambda c: (0, c)),
         ],
         out_specs=(
             pl.BlockSpec((span, wide), lambda c: (c, 0)),
             pl.BlockSpec((local, wide), lambda c: (c, 0)),
             pl.BlockSpec((model, span), lambda c: (0, c)),
-            pl.BlockSpec((span, LANES), lambda c: (c, 0)),
-            pl.BlockSpec((local, LANES), lambda c: (c, 0)),
         ),
         cost_estimate=pl.CostEstimate(
             flops=cols * local * model * wide * 3, bytes_accessed=16 << 20, transcendentals=0
         ),
         compiler_params=pltpu.CompilerParams(vmem_limit_bytes=48 << 20),
-    )(row, x_parts, w_q, w_kv, segs.reshape(1, -1), pads.reshape(1, -1))
+    )(row, x_parts, w_q, w_kv)
 
 
 PIECES = 2
@@ -807,13 +750,17 @@
     w_kv = jnp.concatenate([w_heads[:, 1], w_heads[:, 2]], axis=2).reshape(model, heads * LANES)
     w_q = jnp.pad(w_heads[:, 0], ((0, 0), (0, 0), (0, HW))).reshape(model, heads * LANES)
     row_arr = jnp.reshape(row, (1,)).astype(jnp.int32)
-    q, kv, x_own, q_mask, k_mask = project(
-        row_arr, x_parts, w_q, w_kv, span, segment_ids, pad_mask
+    q, kv, x_own = project(row_arr, x_parts, w_q, w_kv, span)
+    x_res = lax.dynamic_slice_in_dim(x_own, col * span, span, axis=1).T.astype(F32)
+
+    rand = rand_blocks.reshape(-1)
+    k_segs = jnp.where(pad_mask == 1, segment_ids, -1).reshape(nb, BLOCK)
+    k_segs = jnp.concatenate([k_segs, k_segs], axis=1)
+    q_segs = lax.dynamic_index_in_dim(
+        segment_ids.reshape(cols, rows, span), row, axis=1, keepdims=False
     )
-    x_res = lax.dynamic_slice_in_dim(x_own, col * span, span, axis=1).T.astype(F32)
-
-    rand = rand_blocks.reshape(-1)
-    o_wide, lse = attention_forward(dims, row_arr, rand, q, q_mask, kv, k_mask)
+    q_segs = jnp.broadcast_to(q_segs.reshape(own, 1), (own, LANES))
+    o_wide, lse = attention_forward(dims, row_arr, rand, q, q_segs, kv, k_segs)
     o = o_wide.reshape(own, heads, 2, HW)[:, :, 1].reshape(own, hid)
     attn = scatter_col(mm_nt(o, w_o).astype(BF))
 
@@ -861,7 +808,7 @@
     g_rest = jnp.concatenate([g_out.reshape(rows, feat, hid), sums], axis=1).reshape(-1, hid)
     d_o, g_rest = lax.optimization_barrier((d_o, g_rest))
     g_rest = lax.psum_scatter(g_rest, "row", scatter_dimension=0, tiled=True)
-    dq, dkv = attention_backward(dims, row_arr, rand, q, q_mask, kv, k_mask, d_o, lse)
+    dq, dkv = attention_backward(dims, row_arr, rand, q, q_segs, kv, k_segs, d_o, lse, o_wide)
     dkv = lax.psum_scatter(dkv, "row", scatter_dimension=0, tiled=True)
     dkv, g_ffn, g_rest = lax.optimization_barrier((dkv, g_ffn, g_rest))
     g_ffn, g_rest = lax.psum((g_ffn, g_rest), "dp")
@@ -877,7 +824,8 @@
     g_qkv = scatter_row(g_qkv, rows, swap)
     if not swap:
         g_qkv = lax.psum(g_qkv.astype(BF), "dp").astype(F32)
-    grad_in = scatter_col(mm_nt(dqkv, w_own).astype(BF)) + grad1
+    grad_in = scatter_col(mm_nt(dqkv, w_own).astype(BF))
+    grad_in = grad_in + grad1
     grad_in = lax.all_to_all(grad_in.T.astype(BF), "row", 0, 1, tiled=True).astype(F32)
 
     return (

time: 467 us -> 454 us (0.972)
  Pallas kernels: 261 us -> 241 us
  waiting for transfers between devices: 85.6 us -> 98.5 us
    reduce_scatter x1, waiting for transfers between devices: 21.8 us -> 34.6 us  [on_device(): g_ffn = lax.psum_scatter(g_ffn, 'row', scatter_dimension=0, tiled=True)]
    pallas_call x1, Pallas kernels: 39.5 us -> 27.4 us  [attention_backward(): pl.pallas_call(functools.partial(backward_kernel, *dims), name='attn_bwd'...]
    pallas_call x1, Pallas kernels: 30.9 us -> 22.8 us  [attention_forward(): pl.pallas_call(functools.partial(forward_kernel, *dims), name='attn_fwd',...]
    unnamed x80 -> x66, local copies, waits for them, and re-layouts: 17.1 us -> 13.8 us
  transfers between devices with their start and end apart: 8 -> 8, of which waited for: 2 -> 2; matrix products, arithmetic and copies ran while one was open for 7% -> 7% of each run, Pallas kernels for 33% -> 30%
where the time goes in v5:
time: 454 us; the launch traced here: 453 us
  Pallas kernels  241 us (53%)
  waiting for transfers between devices  98.5 us (22%)
  local copies, waits for them, and re-layouts  42.3 us (9%)
  matrix products  24.3 us (5%)
  other arithmetic  20.5 us (5%)
  between operations  14.6 us (3%)
  starting transfers between devices  12.2 us (3%)
    reduce_scatter x1, waiting for transfers between devices, on_device(): dkv = lax.psum_scatter(dkv, 'row', scatter_dimension=0, tiled=True)  63.1 us
    pallas_call x1, Pallas kernels, gather_in(): pl.pallas_call(functools.partial(gather_in_kernel, rows), name='gather_in...  55.7 us
    pallas_call x4, Pallas kernels, scatter_col(): pl.pallas_call(scatter_kernel, name='scatter_col', out_shape=jax.ShapeDty...  52 us
    pallas_call x3, Pallas kernels, gather_col(): pl.pallas_call(gather_kernel, name='gather_col', out_shape=jax.ShapeDtype...  37.5 us
    pallas_call x1, Pallas kernels, scatter_row(): pl.pallas_call(functools.partial(scatter_row_kernel, rows, swap), name='s...  36.5 us
    reduce_scatter x1, waiting for transfers between devices, on_device(): g_ffn = lax.psum_scatter(g_ffn, 'row', scatter_dimension=0, tiled=True)  34.6 us
    pallas_call x1, Pallas kernels, attention_backward(): pl.pallas_call(functools.partial(backward_kernel, *dims), name='attn_bwd'...  27.4 us
    pallas_call x1, Pallas kernels, attention_forward(): pl.pallas_call(functools.partial(forward_kernel, *dims), name='attn_fwd',...  22.8 us
  transfers between devices with their start and end apart: 8, of which 2 were waited for; matrix products, arithmetic and copies ran while one was open for 7% of the time, Pallas kernels for 30%

profile of v5, /device:TPU:0, one launch (start us, length us, event | category | flops | bytes accessed | tf_op | source)
XLA Modules:
  0.0 453.2 jit_solution(2908640705087619937)
XLA Ops:
  14.7 1.9 pad_maximum_fusion.2
  16.8 55.7 %gather_in.1 = (bf16[4,4,192,1024]{3,2,1,0:T(8,128)(2,1)S(1)}, bf16[4,208,768]{2,1,0:T(8,128)(2,1)S(1)}) custom-call(bf16[192,1024]{1,0:T(8,128)(2,1)S(1)} %copy-done.10, bf16[208,768]{1,0:T(8,128)(2,1)S(1)} %pad_maximum_fusion.7.w_ref), custom_call_target="tpu_custom_call" | custom-call | tf_op jit(solution)/shard_map/gather_in/pallas_call | solution.py:630
  72.5 2.6 copy-done.11
  75.9 3.8 all-to-all-start.1
  83.0 9.0 %project.1 = (bf16[1024,384]{1,0:T(8,128)(2,1)S(1)}, bf16[4096,384]{1,0:T(8,128)(2,1)}, bf16[768,1024]{1,0:T(8,128)(2,1)S(1)}) custom-call(s32[1]{0:T(128)} %bitcast.row_ref, bf16[4,4,192,1024]{3,2,1,0:T(8,128)(2,1)} %copy-done.11, bf16[768,384]{1,0:T(8,128)(2,1)S(1)} %copy.74.wq_ref, bf16[768,384]{1,0:T(8,128)(2,1)S(1)} %copy.75.wkv_ref), custom_call_target="tpu_custom_call" | custom-call | flops 3623878656 | bytes 16777216 | tf_op jit(solution)/shard_map/project/pallas_call | solution.py:271
  95.8 22.8 %attn_fwd.1 = (bf16[1024,384]{1,0:T(8,128)(2,1)S(1)}, f32[1024,384]{1,0:T(8,128)S(1)}) custom-call(s32[1]{0:T(128)} %bitcast.row_ref, s32[576]{0:T(1024)S(1)} %reshape.227.rand_ref, bf16[1024,384]{1,0:T(8,128)(2,1)S(1)} %copy-done.8, s32[1024,128]{1,0:T(8,128)S(1)} %broadcast_in_dim.9.qs_ref, bf16[4096,384]{1,0:T(8,128)(2,1)} %get-tuple-element.36.kv_ref, ...), custom_call_target="tpu_custom_call" | custom-call | flops 1207959552 | bytes 12582912 | tf_op jit(solution)/shard_map/attn_fwd/pallas_call | solution.py:214
  122.0 1.9 convolution_convert_fusion.3
  123.9 13.0 %scatter_col.4 = f32[256,768]{1,0:T(8,128)S(1)} custom-call(bf16[4,256,768]{2,1,0:T(8,128)(2,1)S(1)} %bitcast.103), custom_call_target="tpu_custom_call" | custom-call | tf_op jit(solution)/shard_map/scatter_col/pallas_call | solution.py:671
  136.9 2.0 fusion.48
  140.6 12.3 %gather_col.3 = bf16[4,256,768]{2,1,0:T(8,128)(2,1)S(1)} custom-call(bf16[256,768]{1,0:T(8,128)(2,1)S(1)} %fusion.18.x_ref), custom_call_target="tpu_custom_call" | custom-call | tf_op jit(solution)/shard_map/gather_col/pallas_call | solution.py:657
  155.6 3.3 fusion.13
  158.9 2.0 convolution_convert_fusion.2
  160.9 13.0 %scatter_col.5 = f32[256,768]{1,0:T(8,128)S(1)} custom-call(bf16[4,256,768]{2,1,0:T(8,128)(2,1)S(1)} %bitcast.107), custom_call_target="tpu_custom_call" | custom-call | tf_op jit(solution)/shard_map/scatter_col/pallas_call | solution.py:671
  176.0 12.0 %gather_col.4 = bf16[4,256,768]{2,1,0:T(8,128)(2,1)S(1)} custom-call(bf16[256,768]{1,0:T(8,128)(2,1)S(1)} %get-tuple-element.66.x_ref), custom_call_target="tpu_custom_call" | custom-call | tf_op jit(solution)/shard_map/gather_col/pallas_call | solution.py:657
  189.6 3.7 fusion.6
  194.8 1.6 pad_maximum_fusion
  196.5 3.2 convolution_convert_fusion.1
  199.6 13.0 %scatter_col.6 = f32[256,768]{1,0:T(8,128)S(1)} custom-call(bf16[4,256,768]{2,1,0:T(8,128)(2,1)S(1)} %bitcast.105), custom_call_target="tpu_custom_call" | custom-call | tf_op jit(solution)/shard_map/scatter_col/pallas_call | solution.py:671
  214.4 13.2 %gather_col.5 = bf16[4,288,768]{2,1,0:T(8,128)(2,1)S(1)} custom-call(bf16[288,768]{1,0:T(8,128)(2,1)S(1)} %pad_maximum_fusion.6.x_ref), custom_call_target="tpu_custom_call" | custom-call | tf_op jit(solution)/shard_map/gather_col/pallas_call | solution.py:657
  228.2 1.8 convolution_convert_fusion.7
  235.6 2.3 copy.88.do_ref
  241.6 27.4 %attn_bwd.1 = (bf16[1024,384]{1,0:T(8,128)(2,1)S(1)}, bf16[4096,384]{1,0:T(8,128)(2,1)}) custom-call(s32[1]{0:T(128)} %bitcast.row_ref, s32[576]{0:T(1024)S(1)} %reshape.227.rand_ref, bf16[1024,384]{1,0:T(8,128)(2,1)S(1)} %copy-done.9, s32[1024,128]{1,0:T(8,128)S(1)} %broadcast_in_dim.9.qs_ref, bf16[4096,384]{1,0:T(8,128)(2,1)} %get-tuple-element.36.kv_ref, ...), custom_call_target="tpu_custom_call" | custom-call | flops 2415919104 | bytes 20971520 | tf_op jit(solution)/shard_map/attn_bwd/pallas_call | solution.py:233
  270.8 4.8 %all-to-all-start = ((bf16[4,192,256]{2,1,0:T(8,128)(2,1)}), bf16[4,192,256]{2,1,0:T(8,128)(2,1)}, u32[]{:S(2)}, u32[]{:S(2)}) async-start(bf16[4,192,256]{2,1,0:T(8,128)(2,1)} %bitcast.25), calls=%async_computation | async-start | bytes 786432 | tf_op jit(solution)/shard_map/all_to_all | solution.py:775
  276.7 34.6 %reduce-scatter.6.cloned.1.call-done = bf16[384,768]{1,0:T(8,128)(2,1)} async-done(((bf16[1536,768]{1,0:T(8,128)(2,1)}), bf16[384,768]{1,0:T(8,128)(2,1)}) %reduce-scatter.6.cloned.1.call-update) | async-done | bytes 589840 | tf_op jit(solution)/shard_map/reduce_scatter | solution.py:786
  311.3 63.1 %reduce-scatter.4.cloned.1.call-done = bf16[1024,384]{1,0:T(8,128)(2,1)} async-done(((bf16[4096,384]{1,0:T(8,128)(2,1)}), bf16[1024,384]{1,0:T(8,128)(2,1)}) %reduce-scatter.4.cloned.1.call-update) | async-done | bytes 786448 | tf_op jit(solution)/shard_map/reduce_scatter | solution.py:812
  375.9 2.7 convolution_convert_fusion
  378.7 13.0 %scatter_col.7 = f32[256,768]{1,0:T(8,128)S(1)} custom-call(bf16[4,256,768]{2,1,0:T(8,128)(2,1)S(1)} %bitcast.106), custom_call_target="tpu_custom_call" | custom-call | tf_op jit(solution)/shard_map/scatter_col/pallas_call | solution.py:671
  392.7 3.6 all-to-all-start.2
  396.3 1.8 copy.99
  398.1 2.2 convolution_convert_fusion.6
  401.0 36.5 %scatter_row.1 = f32[192,576]{1,0:T(8,128)S(1)} custom-call(bf16[4,192,576]{2,1,0:T(8,128)(2,1)S(1)} %bitcast.104), custom_call_target="tpu_custom_call" | custom-call | tf_op jit(solution)/shard_map/scatter_row/pallas_call | solution.py:482
  444.5 2.1 fusion.53
  (168 shorter events, 52.8 us)
Async XLA Ops:
  7.2 9.6 %copy-start.10 = (bf16[192,1024]{1,0:T(8,128)(2,1)S(1)}, bf16[192,1024]{1,0:T(8,128)(2,1)}, u32[]{:S(2)}) copy-start(bf16[192,1024]{1,0:T(8,128)(2,1)} %x_ref.1) | copy-start | bytes 1179652
  7.2 148.4 %all-gather.2.cloned.1.call-start = ((), (), s32[]{:S(2)}) async-start(), calls=%async_computation.6 | async-start | bytes 2949120 | tf_op jit(solution)/shard_map/all_gather | solution.py:739
  10.2 65.0 %copy-start.22 = (bf16[192,1024]{1,0:T(8,128)(2,1)S(1)}, bf16[192,1024]{1,0:T(8,128)(2,1)}, u32[]{:S(2)}) copy-start(bf16[192,1024]{1,0:T(8,128)(2,1)} %param.29) | copy-start | bytes 1179652
  14.7 65.0 %copy-start.26 = (s32[4096]{0:T(1024)S(1)}, s32[4096]{0:T(1024)}, u32[]{:S(2)}) copy-start(s32[4096]{0:T(1024)} %param.26) | copy-start | bytes 49156
  14.7 65.0 %copy-start.27 = (s32[4096]{0:T(1024)S(1)}, s32[4096]{0:T(1024)}, u32[]{:S(2)}) copy-start(s32[4096]{0:T(1024)} %param.27) | copy-start | bytes 49156
  14.7 65.1 %copy-start.28 = (s32[1,3,64,3]{2,0,3,1:T(1,128)S(1)}, s32[1,3,64,3]{2,0,3,1:T(1,128)}, u32[]{:S(2)}) copy-start(s32[1,3,64,3]{2,0,3,1:T(1,128)} %param.28) | copy-start | bytes 6916
  72.5 2.7 copy-start.11
  75.9 78.1 %all-to-all-start.1 = ((bf16[192,4,256]{2,0,1:T(8,128)(2,1)}), bf16[192,4,256]{2,0,1:T(8,128)(2,1)S(1)}, u32[]{:S(2)}, u32[]{:S(2)}) async-start(bf16[192,4,256]{2,0,1:T(8,128)(2,1)} %bitcast.102), calls=%async_computation.1 | async-start | bytes 786432 | tf_op jit(solution)/shard_map/all_to_all | solution.py:747
  79.7 197.0 %reduce-scatter.8.cloned.1.call-start = ((), (), s32[]{:S(2)}) async-start(), calls=%async_computation.9 | async-start | bytes 532480 | tf_op jit(solution)/shard_map/reduce_scatter | solution.py:810
  118.6 1.2 copy-start.12
  119.7 4.2 copy-start.2
  122.0 2.0 copy-start.18
  155.6 3.3 copy-start.29
  160.9 13.0 %copy-start.14 = (f32[256,768]{1,0:T(8,128)S(1)}, f32[256,768]{1,0:T(8,128)}, u32[]{:S(2)}) copy-start(f32[256,768]{1,0:T(8,128)} %get-tuple-element.69) | copy-start | bytes 2359300
  160.9 13.4 %copy-start.17 = (f32[768,256]{0,1:T(8,128)S(1)}, f32[768,256]{0,1:T(8,128)}, u32[]{:S(2)}) copy-start(f32[768,256]{0,1:T(8,128)} %copy.83) | copy-start | bytes 2359300
  189.6 3.7 copy-start.1
  193.3 1.5 copy-start.30
  199.6 13.0 %copy-start.21 = (f32[256,768]{1,0:T(8,128)S(1)}, f32[256,768]{1,0:T(8,128)}, u32[]{:S(2)}) copy-start(f32[256,768]{1,0:T(8,128)} %get-tuple-element.67) | copy-start | bytes 2359300
  214.4 13.3 %copy-start.19 = (bf16[1024,3,1,64]{0,3,2,1:T(8,128)(2,1)S(1)}, bf16[1024,3,1,64]{0,3,2,1:T(8,128)(2,1)}, u32[]{:S(2)}) copy-start(bf16[1024,3,1,64]{0,3,2,1:T(8,128)(2,1)} %copy-done.18) | copy-start | bytes 1179652
  234.8 3.1 copy-start.3
  234.8 76.5 %reduce-scatter.6.cloned.1.call-start = ((), (), s32[]{:S(2)}) async-start(), calls=%async_computation.8 | async-start | bytes 2949120 | tf_op jit(solution)/shard_map/reduce_scatter | solution.py:786
  235.6 138.9 %reduce-scatter.4.cloned.1.call-start = ((), (), s32[]{:S(2)}) async-start(), calls=%async_computation.7 | async-start | bytes 3932160 | tf_op jit(solution)/shard_map/reduce_scatter | solution.py:812
  240.2 1.4 copy-start.13
  269.9 5.7 %copy-start.5 = (bf16[1024,384]{1,0:T(8,128)(2,1)S(1)}, bf16[1024,384]{1,0:T(8,128)(2,1)}, u32[]{:S(2)}) copy-start(bf16[1024,384]{1,0:T(8,128)(2,1)} %copy-done.4) | copy-start | bytes 2359300
  270.8 121.9 %all-to-all-start = ((bf16[4,192,256]{2,1,0:T(8,128)(2,1)}), bf16[4,192,256]{2,1,0:T(8,128)(2,1)}, u32[]{:S(2)}, u32[]{:S(2)}) async-start(bf16[4,192,256]{2,1,0:T(8,128)(2,1)} %bitcast.25), calls=%async_computation | async-start | bytes 786432 | tf_op jit(solution)/shard_map/all_to_all | solution.py:775
  275.9 100.0 %copy-start.16 = (bf16[4,192,768]{2,1,0:T(8,128)(2,1)S(1)}, bf16[4,192,768]{2,1,0:T(8,128)(2,1)}, u32[]{:S(2)}) copy-start(bf16[4,192,768]{2,1,0:T(8,128)(2,1)} %copy-done.15) | copy-start | bytes 3538948
  375.9 2.8 copy-start.24
  375.9 2.8 copy-start.25
  378.7 13.0 %copy-start.20 = (f32[256,768]{1,0:T(8,128)S(1)}, f32[256,768]{1,0:T(8,128)}, u32[]{:S(2)}) copy-start(f32[256,768]{1,0:T(8,128)} %get-tuple-element.64) | copy-start | bytes 2359300
  391.7 6.4 %copy-start.23 = (bf16[1024,3,1,64]{0,3,2,1:T(8,128)(2,1)S(1)}, bf16[1024,3,1,64]{0,3,2,1:T(8,128)(2,1)}, u32[]{:S(2)}) copy-start(bf16[1024,3,1,64]{0,3,2,1:T(8,128)(2,1)} %slice.152) | copy-start | bytes 1179652
  392.7 47.5 %all-to-all-start.2 = ((bf16[4,192,256]{2,1,0:T(8,128)(2,1)}), bf16[4,192,256]{2,1,0:T(8,128)(2,1)S(1)}, u32[]{:S(2)}, u32[]{:S(2)}) async-start(bf16[4,192,256]{2,1,0:T(8,128)(2,1)} %bitcast.47), calls=%async_computation.5 | async-start | bytes 786432 | tf_op jit(solution)/shard_map/all_to_all | solution.py:829
  396.3 44.9 %all-reduce.8.cloned.1.call-start = ((), (), s32[]{:S(2)}) async-start(), calls=%async_computation.10 | async-start | bytes 1392640 | tf_op jit(solution)/shard_map/psum | solution.py:814
  (7 other events, 7.4 us)
Sparse Core Ops, SparseCore 0:
  75.3 55.2 all-gather.1
  234.9 21.6 reduce-scatter.7
  258.9 52.3 reduce-scatter.5
  313.5 60.8 reduce-scatter.3
  399.2 37.7 all-reduce.7

commit v6 on v5

--- a/solution.py
+++ b/solution.py
@@ -383,13 +383,17 @@
         over[i].wait_send()
 
 
-def scatter_row_kernel(
-    rows, swap, x_ref, out_ref, from_left, from_right, to_right, to_left, own_buf, peer_buf,
-    send_sem, recv_sem, swap_sem,
+def scatter_both_kernel(
+    rows, swap, x_ref, g_ref, out_ref, grad_ref, near_buf, sum_buf, over_buf,
+    from_left, from_right, to_right, to_left, own_buf, peer_buf,
+    col_send, col_recv, send_sem, recv_sem, swap_sem,
 ):
-    me = lax.axis_index("row")
+    me, col = lax.axis_index("row"), lax.axis_index("col")
     right, left = lax.rem(me + 1, rows), lax.rem(me + rows - 1, rows)
     has_left, has_right = me > 0, me < rows - 1
+    partner = col + 1 - 2 * lax.rem(col, 2)
+    cross = lax.rem(col + 2, 4)
+    diag = lax.rem(partner + 2, 4)
     mesh_id = pl.DeviceIdType.MESH
     barrier = pltpu.get_barrier_semaphore()
 
@@ -401,15 +405,19 @@
     def _():
         pl.semaphore_signal(barrier, inc=1, device_id={"row": right}, device_id_type=mesh_id)
 
+    for peer in (partner, cross):
+        pl.semaphore_signal(barrier, inc=1, device_id={"col": peer}, device_id_type=mesh_id)
     if swap:
-        peer = 1 - lax.axis_index("dp")
-        pl.semaphore_signal(barrier, inc=1, device_id={"dp": peer}, device_id_type=mesh_id)
-
-    peers = jnp.where(has_left, 1, 0) + jnp.where(has_right, 1, 0) + (1 if swap else 0)
+        other = 1 - lax.axis_index("dp")
+        pl.semaphore_signal(barrier, inc=1, device_id={"dp": other}, device_id_type=mesh_id)
+    peers = jnp.where(has_left, 1, 0) + jnp.where(has_right, 1, 0) + (3 if swap else 2)
     pl.semaphore_wait(barrier, peers)
 
-    size = x_ref.shape[1] // PIECES
+    size = g_ref.shape[1] // PIECES
     cuts = [pl.ds(i * size, size) for i in range(PIECES)]
+    deep = x_ref.shape[1] // PIECES
+    slabs = [pl.ds(i * deep, deep) for i in range(PIECES)]
+    sems = (col_send, col_recv)
 
     def hop(way, dest, i):
         stage, target, to = ((to_right, from_left, right), (to_left, from_right, left))[way]
@@ -426,77 +434,117 @@
     for step in range(rows - 1):
         flows.append((0, rows - 1 - step, me < rows - 1 - step, has_left))
         flows.append((1, step, me > step, has_right))
+
+    first = [
+        send_to(x_ref.at[diag, cut], near_buf.at[1, cut], sems, 0, i, partner)
+        for i, cut in enumerate(slabs)
+    ]
+    for way, dest, active, relays in flows:
+        stage = (to_right, to_left)[way]
+
+        @pl.when(active & jnp.logical_not(relays))
+        def _():
+            for i, cut in enumerate(cuts):
+                stage[dest, cut, :] = g_ref[dest, cut, :]
+                hop(way, dest, i).start()
+
+    second = [
+        send_to(x_ref.at[partner, cut], near_buf.at[0, cut], sems, 1, i, partner)
+        for i, cut in enumerate(slabs)
+    ]
+    over = []
+    for i, cut in enumerate(slabs):
+        first[i].wait_recv()
+        sum_buf[cut, :] = (
+            x_ref[cross, cut, :].astype(F32) + near_buf[1, cut, :].astype(F32)
+        ).astype(BF)
+        over.append(send_to(sum_buf.at[cut], over_buf.at[cut], sems, 2, i, cross))
     for way, dest, active, relays in flows:
         stage, came = ((to_right, from_left), (to_left, from_right))[way]
-        for i, cut in enumerate(cuts):
-
-            @pl.when(active & relays)
-            def _():
+
+        @pl.when(active & relays)
+        def _():
+            for i, cut in enumerate(cuts):
                 hop(way, dest, i).wait_recv()
                 stage[dest, cut, :] = (
-                    x_ref[dest, cut, :].astype(F32) + came[dest, cut, :].astype(F32)
+                    g_ref[dest, cut, :].astype(F32) + came[dest, cut, :].astype(F32)
                 ).astype(BF)
-
-            @pl.when(active & jnp.logical_not(relays))
-            def _():
-                stage[dest, cut, :] = x_ref[dest, cut, :]
-
-            @pl.when(active)
-            def _():
                 hop(way, dest, i).start()
 
-    out_ref[...] = x_ref[me].astype(F32)
+    for i, cut in enumerate(slabs):
+        second[i].wait_recv()
+        out_ref[cut, :] = x_ref[col, cut, :].astype(F32) + near_buf[0, cut, :].astype(F32)
+    for i, cut in enumerate(slabs):
+        over[i].wait_recv()
+        out_ref[cut, :] += over_buf[cut, :].astype(F32)
+
+    grad_ref[...] = g_ref[me].astype(F32)
     for way, came, has in ((0, from_left, has_left), (1, from_right, has_right)):
 
         @pl.when(has)
         def _():
             for i, cut in enumerate(cuts):
                 hop(way, me, i).wait_recv()
-                out_ref[cut, :] += came[me, cut, :].astype(F32)
-
-    for way, dest, active, _ in flows:
-
-        @pl.when(active)
-        def _():
-            for i in range(PIECES):
-                hop(way, dest, i).wait_send()
+                grad_ref[cut, :] += came[me, cut, :].astype(F32)
 
     if swap:
-        own_buf[...] = out_ref[...].astype(BF)
+        own_buf[...] = grad_ref[...].astype(BF)
         copy = pltpu.make_async_remote_copy(
             src_ref=own_buf,
             dst_ref=peer_buf,
             send_sem=swap_sem.at[0],
             recv_sem=swap_sem.at[1],
-            device_id={"dp": peer},
+            device_id={"dp": other},
             device_id_type=mesh_id,
         )
         copy.start()
         copy.wait()
-        out_ref[...] = own_buf[...].astype(F32) + peer_buf[...].astype(F32)
-
-
-def scatter_row(value, rows, swap):
-    count, wide = value.shape[0] // rows, value.shape[1]
+        grad_ref[...] = own_buf[...].astype(F32) + peer_buf[...].astype(F32)
+
+    for way, dest, active, _ in flows:
+
+        @pl.when(active)
+        def _():
+            for i in range(PIECES):
+                hop(way, dest, i).wait_send()
+
+    for i in range(PIECES):
+        first[i].wait_send()
+        second[i].wait_send()
+        over[i].wait_send()
+
+
+def scatter_both(value, grad, rows, swap):
+    count, wide = value.shape[0] // 4, value.shape[1]
+    deep, span = grad.shape[0] // rows, grad.shape[1]
     vmem = pl.BlockSpec(memory_space=pltpu.VMEM)
     return pl.pallas_call(
-        functools.partial(scatter_row_kernel, rows, swap),
-        name="scatter_row",
-        out_shape=jax.ShapeDtypeStruct((count, wide), F32),
-        in_specs=[vmem],
-        out_specs=vmem,
-        scratch_shapes=[pltpu.VMEM((rows, count, wide), BF)] * 4
-        + [pltpu.VMEM((count, wide), BF)] * 2
+        functools.partial(scatter_both_kernel, rows, swap),
+        name="scatter_both",
+        out_shape=(
+            jax.ShapeDtypeStruct((count, wide), F32),
+            jax.ShapeDtypeStruct((deep, span), F32),
+        ),
+        in_specs=[vmem, vmem],
+        out_specs=(vmem, vmem),
+        scratch_shapes=[
+            pltpu.VMEM((2, count, wide), BF),
+            pltpu.VMEM((count, wide), BF),
+            pltpu.VMEM((count, wide), BF),
+        ]
+        + [pltpu.VMEM((rows, deep, span), BF)] * 4
+        + [pltpu.VMEM((deep, span), BF)] * 2
+        + comm_sems(3)
         + [
             pltpu.SemaphoreType.DMA((2, rows, PIECES)),
             pltpu.SemaphoreType.DMA((2, rows, PIECES)),
             pltpu.SemaphoreType.DMA((2,)),
         ],
         compiler_params=comm_params(4),
-    )(value.reshape(rows, count, wide))
-
-
-def gather_in_kernel(rows, x_ref, w_ref, xs_ref, ws_ref, send_x, recv_x, send_w, recv_w):
+    )(value.reshape(4, count, wide), grad.reshape(rows, deep, span))
+
+
+def gather_in_kernel(rows, swap, x_ref, w_ref, xs_ref, ws_ref, send_x, recv_x, send_w, recv_w):
     me, col = lax.axis_index("row"), lax.axis_index("col")
     right, left = lax.rem(me + 1, rows), lax.rem(me + rows - 1, rows)
     has_left, has_right = me > 0, me < rows - 1
@@ -516,7 +564,15 @@
 
     for peer in (partner, cross):
         pl.semaphore_signal(barrier, inc=1, device_id={"col": peer}, device_id_type=mesh_id)
-    pl.semaphore_wait(barrier, jnp.where(has_left, 1, 0) + jnp.where(has_right, 1, 0) + 2)
+    half = w_ref.shape[0] // 2
+    cut = far = pl.ds(0, w_ref.shape[0])
+    if swap:
+        dp = lax.axis_index("dp")
+        pl.semaphore_signal(barrier, inc=1, device_id={"dp": 1 - dp}, device_id_type=mesh_id)
+        cut = pl.ds(pl.multiple_of(dp * half, half), half)
+        far = pl.ds(pl.multiple_of((1 - dp) * half, half), half)
+    peers = jnp.where(has_left, 1, 0) + jnp.where(has_right, 1, 0) + (3 if swap else 2)
+    pl.semaphore_wait(barrier, peers)
 
     def copy_x(source, kind, shard, slot, where):
         return pltpu.make_async_remote_copy(
@@ -528,10 +584,10 @@
             device_id_type=mesh_id,
         )
 
-    def copy_w(source, kind, shard, where):
+    def copy_w(source, kind, shard, where, cut=cut):
         return pltpu.make_async_remote_copy(
-            src_ref=source,
-            dst_ref=ws_ref.at[shard],
+            src_ref=source.at[cut],
+            dst_ref=ws_ref.at[shard, cut],
             send_sem=send_w.at[kind, shard],
             recv_sem=recv_w.at[kind, shard],
             device_id=where,
@@ -592,6 +648,9 @@
                 @pl.when(onward)
                 def _():
                     copy_w(ws_ref.at[shard], kind, shard, where).start()
+
+                if swap:
+                    copy_w(ws_ref.at[shard], 2, shard, {"dp": 1 - dp}).start()
 
         if step == 1:
             relay(me)
@@ -623,12 +682,19 @@
                 copy_x(x_ref, kind, shard, col, where).wait_send()
                 copy_w(w_ref, kind, shard, where).wait_send()
 
-
-def gather_in(x, w, rows):
+        if swap:
+
+            @pl.when(me != shard)
+            def _():
+                copy_w(w_ref, 2, shard, {"dp": 1 - dp}).wait_send()
+                copy_w(w_ref, 2, shard, {"dp": 1 - dp}, far).wait_recv()
+
+
+def gather_in(x, w, rows, swap):
     vmem = pl.BlockSpec(memory_space=pltpu.VMEM)
     sems = pltpu.SemaphoreType.DMA
     return pl.pallas_call(
-        functools.partial(gather_in_kernel, rows),
+        functools.partial(gather_in_kernel, rows, swap),
         name="gather_in",
         out_shape=(
             jax.ShapeDtypeStruct((rows, 4) + x.shape, BF),
@@ -636,7 +702,7 @@
         ),
         in_specs=[vmem, vmem],
         out_specs=(vmem, vmem),
-        scratch_shapes=[sems((5, rows)), sems((5, rows)), sems((2, rows)), sems((2, rows))],
+        scratch_shapes=[sems((5, rows)), sems((5, rows)), sems((3, rows)), sems((3, rows))],
         compiler_params=comm_params(5),
     )(x, w)
 
@@ -730,10 +796,11 @@
     middle = rest.astype(BF)
     low = (rest - middle.astype(F32)).astype(BF)
     params = jnp.concatenate([high, middle, low], axis=0)
-    params = jnp.pad(params, ((0, 4), (0, 4 * hid - feat)))
+    params = jnp.pad(params, ((0, 20), (0, 4 * hid - feat)))
     w_small = jnp.concatenate([blk_q, blk_k, blk_v, blk_o.T], axis=1)
     w_small = jnp.concatenate([w_small, params], axis=0)
-    x_parts, w_small = gather_in(inputs, w_small, rows)
+    swap = lax.axis_size("dp") == 2
+    x_parts, w_small = gather_in(inputs, w_small, rows, swap)
     w_rest = jnp.concatenate([w_up, w_down], axis=1)
     x_parts, w_rest, grad_out = lax.optimization_barrier((x_parts, w_rest, grad_out))
     w_rest = lax.all_gather(w_rest, "row", axis=0, tiled=True)
@@ -820,11 +887,9 @@
         [dq, dkv[:, :, 0].reshape(own, hid), dkv[:, :, 1].reshape(own, hid)], axis=1
     )
     g_qkv = mm(x_own, dqkv).astype(BF)
-    swap = lax.axis_size("dp") == 2
-    g_qkv = scatter_row(g_qkv, rows, swap)
+    grad_in, g_qkv = scatter_both(mm_nt(dqkv, w_own).astype(BF), g_qkv, rows, swap)
     if not swap:
         g_qkv = lax.psum(g_qkv.astype(BF), "dp").astype(F32)
-    grad_in = scatter_col(mm_nt(dqkv, w_own).astype(BF))
     grad_in = grad_in + grad1
     grad_in = lax.all_to_all(grad_in.T.astype(BF), "row", 0, 1, tiled=True).astype(F32)
 

time: 454 us -> 461 us (1.015)
  waiting for transfers between devices: 98.5 us -> 130 us
  Pallas kernels: 241 us -> 215 us
    psum x1, waiting for transfers between devices: 0.01 us -> 26.5 us  [on_device(): g_ffn, g_rest = lax.psum((g_ffn, g_rest), 'dp')]
    pallas_call x4 -> x3, Pallas kernels: 52 us -> 39 us  [scatter_col(): pl.pallas_call(scatter_kernel, name='scatter_col', out_shape=jax.ShapeDty...]
    pallas_call x2, Pallas kernels: 92.2 us -> 79.4 us  [the longest x1 49.4 us: gather_in(): pl.pallas_call(functools.partial(gather_in_kernel, rows, swap), name='gat...]
    all_to_all x1, waiting for transfers between devices: 0.01 us -> 4.86 us  [on_device(): lax.all_to_all(grad_in.T.astype(BF), 'row', 0, 1, tiled=True).astype(F32)]
  transfers between devices with their start and end apart: 8 -> 8, of which waited for: 2 -> 4; matrix products, arithmetic and copies ran while one was open for 7% -> 7% of each run, Pallas kernels for 30% -> 25%
where the time goes in v6:
time: 461 us; the launch traced here: 460 us
  Pallas kernels  215 us (47%)
  waiting for transfers between devices  130 us (28%)
  local copies, waits for them, and re-layouts  43.1 us (9%)
  matrix products  24 us (5%)
  other arithmetic  20.5 us (4%)
  between operations  14.5 us (3%)
  starting transfers between devices  12.7 us (3%)
    reduce_scatter x1, waiting for transfers between devices, on_device(): dkv = lax.psum_scatter(dkv, 'row', scatter_dimension=0, tiled=True)  63.1 us
    pallas_call x1, Pallas kernels, gather_in(): pl.pallas_call(functools.partial(gather_in_kernel, rows, swap), name='gat...  49.4 us
    pallas_call x3, Pallas kernels, scatter_col(): pl.pallas_call(scatter_kernel, name='scatter_col', out_shape=jax.ShapeDty...  39 us
    pallas_call x3, Pallas kernels, gather_col(): pl.pallas_call(gather_kernel, name='gather_col', out_shape=jax.ShapeDtype...  37.5 us
    reduce_scatter x1, waiting for transfers between devices, on_device(): g_ffn = lax.psum_scatter(g_ffn, 'row', scatter_dimension=0, tiled=True)  34.7 us
    pallas_call x1, Pallas kernels, scatter_both(): pl.pallas_call(functools.partial(scatter_both_kernel, rows, swap), name='...  30 us
    pallas_call x1, Pallas kernels, attention_backward(): pl.pallas_call(functools.partial(backward_kernel, *dims), name='attn_bwd'...  27.4 us
    psum x1, waiting for transfers between devices, on_device(): g_ffn, g_rest = lax.psum((g_ffn, g_rest), 'dp')  26.5 us
  transfers between devices with their start and end apart: 8, of which 4 were waited for; matrix products, arithmetic and copies ran while one was open for 7% of the time, Pallas kernels for 25%

profile of v6, /device:TPU:0, one launch (start us, length us, event | category | flops | bytes accessed | tf_op | source)
XLA Modules:
  0.0 460.3 jit_solution(2229105771464629888)
XLA Ops:
  14.7 1.9 pad_maximum_fusion.2
  16.8 49.4 %gather_in.1 = (bf16[4,4,192,1024]{3,2,1,0:T(8,128)(2,1)S(1)}, bf16[4,224,768]{2,1,0:T(8,128)(2,1)S(1)}) custom-call(bf16[192,1024]{1,0:T(8,128)(2,1)S(1)} %copy-done.10, bf16[224,768]{1,0:T(8,128)(2,1)S(1)} %pad_maximum_fusion.7.w_ref), custom_call_target="tpu_custom_call" | custom-call | tf_op jit(solution)/shard_map/gather_in/pallas_call | solution.py:696
  66.2 2.6 copy-done.11
  69.7 3.8 all-to-all-start.1
  76.7 9.0 %project.1 = (bf16[1024,384]{1,0:T(8,128)(2,1)S(1)}, bf16[4096,384]{1,0:T(8,128)(2,1)}, bf16[768,1024]{1,0:T(8,128)(2,1)S(1)}) custom-call(s32[1]{0:T(128)} %bitcast.row_ref, bf16[4,4,192,1024]{3,2,1,0:T(8,128)(2,1)} %copy-done.11, bf16[768,384]{1,0:T(8,128)(2,1)S(1)} %copy.74.wq_ref, bf16[768,384]{1,0:T(8,128)(2,1)S(1)} %copy.75.wkv_ref), custom_call_target="tpu_custom_call" | custom-call | flops 3623878656 | bytes 16777216 | tf_op jit(solution)/shard_map/project/pallas_call | solution.py:271
  89.5 22.8 %attn_fwd.1 = (bf16[1024,384]{1,0:T(8,128)(2,1)S(1)}, f32[1024,384]{1,0:T(8,128)S(1)}) custom-call(s32[1]{0:T(128)} %bitcast.row_ref, s32[576]{0:T(1024)S(1)} %reshape.227.rand_ref, bf16[1024,384]{1,0:T(8,128)(2,1)S(1)} %copy-done.8, s32[1024,128]{1,0:T(8,128)S(1)} %broadcast_in_dim.9.qs_ref, bf16[4096,384]{1,0:T(8,128)(2,1)} %get-tuple-element.38.kv_ref, ...), custom_call_target="tpu_custom_call" | custom-call | flops 1207959552 | bytes 12582912 | tf_op jit(solution)/shard_map/attn_fwd/pallas_call | solution.py:214
  115.7 1.9 convolution_convert_fusion.3
  117.7 13.0 %scatter_col.3 = f32[256,768]{1,0:T(8,128)S(1)} custom-call(bf16[4,256,768]{2,1,0:T(8,128)(2,1)S(1)} %bitcast.103), custom_call_target="tpu_custom_call" | custom-call | tf_op jit(solution)/shard_map/scatter_col/pallas_call | solution.py:737
  130.7 2.0 fusion.48
  134.4 12.3 %gather_col.3 = bf16[4,256,768]{2,1,0:T(8,128)(2,1)S(1)} custom-call(bf16[256,768]{1,0:T(8,128)(2,1)S(1)} %fusion.18.x_ref), custom_call_target="tpu_custom_call" | custom-call | tf_op jit(solution)/shard_map/gather_col/pallas_call | solution.py:723
  149.4 3.3 fusion.13
  152.7 2.0 convolution_convert_fusion.2
  154.7 13.0 %scatter_col.4 = f32[256,768]{1,0:T(8,128)S(1)} custom-call(bf16[4,256,768]{2,1,0:T(8,128)(2,1)S(1)} %bitcast.107), custom_call_target="tpu_custom_call" | custom-call | tf_op jit(solution)/shard_map/scatter_col/pallas_call | solution.py:737
  169.7 12.0 %gather_col.4 = bf16[4,256,768]{2,1,0:T(8,128)(2,1)S(1)} custom-call(bf16[256,768]{1,0:T(8,128)(2,1)S(1)} %get-tuple-element.70.x_ref), custom_call_target="tpu_custom_call" | custom-call | tf_op jit(solution)/shard_map/gather_col/pallas_call | solution.py:723
  183.4 3.7 fusion.6
  188.6 1.6 pad_maximum_fusion
  190.2 3.2 convolution_convert_fusion.1
  193.4 13.0 %scatter_col.5 = f32[256,768]{1,0:T(8,128)S(1)} custom-call(bf16[4,256,768]{2,1,0:T(8,128)(2,1)S(1)} %bitcast.106), custom_call_target="tpu_custom_call" | custom-call | tf_op jit(solution)/shard_map/scatter_col/pallas_call | solution.py:737
  208.2 13.2 %gather_col.5 = bf16[4,288,768]{2,1,0:T(8,128)(2,1)S(1)} custom-call(bf16[288,768]{1,0:T(8,128)(2,1)S(1)} %pad_maximum_fusion.6.x_ref), custom_call_target="tpu_custom_call" | custom-call | tf_op jit(solution)/shard_map/gather_col/pallas_call | solution.py:723
  222.0 1.8 convolution_convert_fusion.7
  229.4 2.3 copy.88.do_ref
  235.4 27.4 %attn_bwd.1 = (bf16[1024,384]{1,0:T(8,128)(2,1)S(1)}, bf16[4096,384]{1,0:T(8,128)(2,1)}) custom-call(s32[1]{0:T(128)} %bitcast.row_ref, s32[576]{0:T(1024)S(1)} %reshape.227.rand_ref, bf16[1024,384]{1,0:T(8,128)(2,1)S(1)} %copy-done.9, s32[1024,128]{1,0:T(8,128)S(1)} %broadcast_in_dim.9.qs_ref, bf16[4096,384]{1,0:T(8,128)(2,1)} %get-tuple-element.38.kv_ref, ...), custom_call_target="tpu_custom_call" | custom-call | flops 2415919104 | bytes 20971520 | tf_op jit(solution)/shard_map/attn_bwd/pallas_call | solution.py:233
  264.6 4.7 %all-to-all-start = ((bf16[4,192,256]{2,1,0:T(8,128)(2,1)}), bf16[4,192,256]{2,1,0:T(8,128)(2,1)S(1)}, u32[]{:S(2)}, u32[]{:S(2)}) async-start(bf16[4,192,256]{2,1,0:T(8,128)(2,1)} %bitcast.25), calls=%async_computation | async-start | bytes 786432 | tf_op jit(solution)/shard_map/all_to_all | solution.py:842
  270.4 34.7 %reduce-scatter.6.cloned.1.call-done = bf16[384,768]{1,0:T(8,128)(2,1)} async-done(((bf16[1536,768]{1,0:T(8,128)(2,1)}), bf16[384,768]{1,0:T(8,128)(2,1)}) %reduce-scatter.6.cloned.1.call-update) | async-done | bytes 589840 | tf_op jit(solution)/shard_map/reduce_scatter | solution.py:853
  305.2 63.1 %reduce-scatter.4.cloned.1.call-done = bf16[1024,384]{1,0:T(8,128)(2,1)} async-done(((bf16[4096,384]{1,0:T(8,128)(2,1)}), bf16[1024,384]{1,0:T(8,128)(2,1)}) %reduce-scatter.4.cloned.1.call-update) | async-done | bytes 786448 | tf_op jit(solution)/shard_map/reduce_scatter | solution.py:879
  370.6 2.1 convolution_convert_fusion.6
  374.2 2.6 convolution_convert_fusion
  376.8 30.0 %scatter_both.1 = (f32[256,768]{1,0:T(8,128)S(1)}, f32[192,576]{1,0:T(8,128)S(1)}) custom-call(bf16[4,256,768]{2,1,0:T(8,128)(2,1)S(1)} %bitcast.105, bf16[4,192,576]{2,1,0:T(8,128)(2,1)S(1)} %bitcast.104), custom_call_target="tpu_custom_call" | custom-call | tf_op jit(solution)/shard_map/scatter_both/pallas_call | solution.py:521
  407.8 4.1 all-to-all-start.2
  415.9 4.9 %all-to-all-done.2 = bf16[4,192,256]{2,1,0:T(8,128)(2,1)S(1)} async-done(((bf16[4,192,256]{2,1,0:T(8,128)(2,1)}), bf16[4,192,256]{2,1,0:T(8,128)(2,1)S(1)}, u32[]{:S(2)}, u32[]{:S(2)}) %all-to-all-start.2) | async-done | bytes 393248 | tf_op jit(solution)/shard_map/all_to_all | solution.py:894
  421.8 26.5 %all-reduce.8.cloned.1.call-done = (bf16[208,192]{1,0:T(8,128)(2,1)}, bf16[384,768]{1,0:T(8,128)(2,1)}) async-done(((bf16[208,192]{1,0:T(8,128)(2,1)}, bf16[384,768]{1,0:T(8,128)(2,1)}), (bf16[208,192]{1,0:T(8,128)(2,1)}, bf16[384,768]{1,0:T(8,128)(2,1)})) %all-reduce.8.cloned.1.call-update) | async-done | bytes 669712 | tf_op jit(solution)/shard_map/psum | solution.py:881
  451.7 2.1 fusion.53
  (167 shorter events, 56.0 us)
Async XLA Ops:
  7.2 9.6 %copy-start.10 = (bf16[192,1024]{1,0:T(8,128)(2,1)S(1)}, bf16[192,1024]{1,0:T(8,128)(2,1)}, u32[]{:S(2)}) copy-start(bf16[192,1024]{1,0:T(8,128)(2,1)} %x_ref.1) | copy-start | bytes 1179652
  7.2 142.2 %all-gather.2.cloned.1.call-start = ((), (), s32[]{:S(2)}) async-start(), calls=%async_computation.6 | async-start | bytes 2949120 | tf_op jit(solution)/shard_map/all_gather | solution.py:806
  10.2 58.7 %copy-start.22 = (bf16[192,1024]{1,0:T(8,128)(2,1)S(1)}, bf16[192,1024]{1,0:T(8,128)(2,1)}, u32[]{:S(2)}) copy-start(bf16[192,1024]{1,0:T(8,128)(2,1)} %param.29) | copy-start | bytes 1179652
  14.7 58.8 %copy-start.26 = (s32[4096]{0:T(1024)S(1)}, s32[4096]{0:T(1024)}, u32[]{:S(2)}) copy-start(s32[4096]{0:T(1024)} %param.26) | copy-start | bytes 49156
  14.7 58.8 %copy-start.27 = (s32[4096]{0:T(1024)S(1)}, s32[4096]{0:T(1024)}, u32[]{:S(2)}) copy-start(s32[4096]{0:T(1024)} %param.27) | copy-start | bytes 49156
  14.7 58.9 %copy-start.28 = (s32[1,3,64,3]{2,0,3,1:T(1,128)S(1)}, s32[1,3,64,3]{2,0,3,1:T(1,128)}, u32[]{:S(2)}) copy-start(s32[1,3,64,3]{2,0,3,1:T(1,128)} %param.28) | copy-start | bytes 6916
  66.2 2.7 copy-start.11
  69.7 78.1 %all-to-all-start.1 = ((bf16[192,4,256]{2,0,1:T(8,128)(2,1)}), bf16[192,4,256]{2,0,1:T(8,128)(2,1)S(1)}, u32[]{:S(2)}, u32[]{:S(2)}) async-start(bf16[192,4,256]{2,0,1:T(8,128)(2,1)} %bitcast.102), calls=%async_computation.1 | async-start | bytes 786432 | tf_op jit(solution)/shard_map/all_to_all | solution.py:814
  73.5 197.0 %reduce-scatter.8.cloned.1.call-start = ((), (), s32[]{:S(2)}) async-start(), calls=%async_computation.9 | async-start | bytes 532480 | tf_op jit(solution)/shard_map/reduce_scatter | solution.py:877
  88.4 1.1 copy-start.8
  112.3 1.2 copy-start.12
  113.5 4.2 copy-start.2
  115.7 2.0 copy-start.18
  146.6 1.2 copy-start
  149.4 3.3 copy-start.29
  154.6 13.0 %copy-start.14 = (f32[256,768]{1,0:T(8,128)S(1)}, f32[256,768]{1,0:T(8,128)}, u32[]{:S(2)}) copy-start(f32[256,768]{1,0:T(8,128)} %get-tuple-element.73) | copy-start | bytes 2359300
  154.6 13.4 %copy-start.17 = (f32[768,256]{0,1:T(8,128)S(1)}, f32[768,256]{0,1:T(8,128)}, u32[]{:S(2)}) copy-start(f32[768,256]{0,1:T(8,128)} %copy.83) | copy-start | bytes 2359300
  183.4 3.7 copy-start.1
  187.1 1.5 copy-start.30
  193.4 13.0 %copy-start.21 = (f32[256,768]{1,0:T(8,128)S(1)}, f32[256,768]{1,0:T(8,128)}, u32[]{:S(2)}) copy-start(f32[256,768]{1,0:T(8,128)} %get-tuple-element.71) | copy-start | bytes 2359300
  208.1 13.3 %copy-start.19 = (bf16[1024,3,1,64]{0,3,2,1:T(8,128)(2,1)S(1)}, bf16[1024,3,1,64]{0,3,2,1:T(8,128)(2,1)}, u32[]{:S(2)}) copy-start(bf16[1024,3,1,64]{0,3,2,1:T(8,128)(2,1)} %copy-done.18) | copy-start | bytes 1179652
  228.6 3.1 copy-start.3
  228.6 76.5 %reduce-scatter.6.cloned.1.call-start = ((), (), s32[]{:S(2)}) async-start(), calls=%async_computation.8 | async-start | bytes 2949120 | tf_op jit(solution)/shard_map/reduce_scatter | solution.py:853
  229.4 138.9 %reduce-scatter.4.cloned.1.call-start = ((), (), s32[]{:S(2)}) async-start(), calls=%async_computation.7 | async-start | bytes 3932160 | tf_op jit(solution)/shard_map/reduce_scatter | solution.py:879
  234.0 1.4 copy-start.13
  263.7 5.7 %copy-start.5 = (bf16[1024,384]{1,0:T(8,128)(2,1)S(1)}, bf16[1024,384]{1,0:T(8,128)(2,1)}, u32[]{:S(2)}) copy-start(bf16[1024,384]{1,0:T(8,128)(2,1)} %copy-done.4) | copy-start | bytes 2359300
  264.6 143.2 %all-to-all-start = ((bf16[4,192,256]{2,1,0:T(8,128)(2,1)}), bf16[4,192,256]{2,1,0:T(8,128)(2,1)S(1)}, u32[]{:S(2)}, u32[]{:S(2)}) async-start(bf16[4,192,256]{2,1,0:T(8,128)(2,1)} %bitcast.25), calls=%async_computation | async-start | bytes 786432 | tf_op jit(solution)/shard_map/all_to_all | solution.py:842
  270.4 100.2 %copy-start.23 = (bf16[1024,3,1,64]{0,3,2,1:T(8,128)(2,1)S(1)}, bf16[1024,3,1,64]{0,3,2,1:T(8,128)(2,1)}, u32[]{:S(2)}) copy-start(bf16[1024,3,1,64]{0,3,2,1:T(8,128)(2,1)} %slice.152) | copy-start | bytes 1179652
  370.6 3.6 copy-start.16
  376.8 30.0 %copy-start.20 = (f32[256,768]{1,0:T(8,128)S(1)}, f32[256,768]{1,0:T(8,128)}, u32[]{:S(2)}) copy-start(f32[256,768]{1,0:T(8,128)} %get-tuple-element.68) | copy-start | bytes 2359300
  407.8 13.0 %all-to-all-start.2 = ((bf16[4,192,256]{2,1,0:T(8,128)(2,1)}), bf16[4,192,256]{2,1,0:T(8,128)(2,1)S(1)}, u32[]{:S(2)}, u32[]{:S(2)}) async-start(bf16[4,192,256]{2,1,0:T(8,128)(2,1)} %bitcast.48), calls=%async_computation.5 | async-start | bytes 786432 | tf_op jit(solution)/shard_map/all_to_all | solution.py:894
  411.9 36.4 %all-reduce.8.cloned.1.call-start = ((), (), s32[]{:S(2)}) async-start(), calls=%async_computation.10 | async-start | bytes 1392640 | tf_op jit(solution)/shard_map/psum | solution.py:881
  (7 other events, 6.7 us)
Sparse Core Ops, SparseCore 0:
  69.0 55.2 all-gather.1
  228.7 21.6 reduce-scatter.7
  252.7 52.3 reduce-scatter.5
  307.3 60.8 reduce-scatter.3
  414.8 33.5 all-reduce.7
